TPU v7x, 8 devices: a whole 2x2x1 slice. The times are simulated.
8 devices in a mesh: rep: 4 (over z, y, x), fsdp: 2 (over core).
Axes of the slice: x: 2, y: 2, z: 1, core: 2. Of those that a mesh axis runs over, the one named last changes fastest.
Arguments:
- tokens: int32 [256, 32], P(('rep', 'fsdp'))
- resp_mask: int32 [256, 32], P(('rep', 'fsdp'))
- logp_old: float32 [256, 32], P(('rep', 'fsdp'))
- rewards: float32 [256], P(('rep', 'fsdp'))
- group_id: int32 [256], P(('rep', 'fsdp'))
- pol_wq: bfloat16 [2, 1600, 1600], P(None, 'fsdp')
- pol_wkv: bfloat16 [2, 1600, 640], P(None, 'fsdp')
- pol_wo: bfloat16 [2, 1600, 1600], P(None, 'fsdp')
- pol_wgu: bfloat16 [2, 1600, 8704], P(None, 'fsdp')
- pol_wdown: bfloat16 [2, 4352, 1600], P(None, 'fsdp')
- pol_norms: bfloat16 [5, 1600], P(None, 'fsdp')
- pol_embed: bfloat16 [32000, 1600], P('fsdp')
- pol_head: bfloat16 [32000, 1600], P('fsdp')
- ref_wq: bfloat16 [2, 1600, 1600], P(None, ('rep', 'fsdp'))
- ref_wkv: bfloat16 [2, 1600, 640], P(None, ('rep', 'fsdp'))
- ref_wo: bfloat16 [2, 1600, 1600], P(None, ('rep', 'fsdp'))
- ref_wgu: bfloat16 [2, 1600, 8704], P(None, ('rep', 'fsdp'))
- ref_wdown: bfloat16 [2, 4352, 1600], P(None, ('rep', 'fsdp'))
- ref_norms: bfloat16 [5, 1600], P(None, ('rep', 'fsdp'))
- ref_embed: bfloat16 [32000, 1600], P(('rep', 'fsdp'))
- ref_head: bfloat16 [32000, 1600], P(('rep', 'fsdp'))
Outputs:
- output 1: float32 [], replicated
- output 2: float32 [256, 32], P(('rep', 'fsdp'))
- output 3: float32 [256, 32], P(('rep', 'fsdp'))
All inputs are finite; a program needn't handle non-finite values.
Results may differ from a plain program's by a relative error of at most 0.00177.
Values are sent between devices in bfloat16 or wider.
A program may use at most 1 GiB of HBM per device.

v0:
```python
import jax
import jax.numpy as jnp
from jax import lax
from jax.sharding import PartitionSpec as P

HEAD_DIM = 64
EPS = 1e-6
ROPE_BASE = 10000.0
CLIP_EPS = 0.2
BETA = 0.04
ADV_EPS = 1e-4


def rms_norm(hidden, gain):
    hidden_f32 = hidden.astype(jnp.float32)
    inv_rms = lax.rsqrt(jnp.mean(hidden_f32 * hidden_f32, axis=-1, keepdims=True) + EPS)
    return (hidden_f32 * inv_rms * gain.astype(jnp.float32)).astype(jnp.bfloat16)


def rope_tables(seq_len):
    half = HEAD_DIM // 2
    inv_freq = ROPE_BASE ** (-jnp.arange(half, dtype=jnp.float32) / half)
    angles = jnp.arange(seq_len, dtype=jnp.float32)[:, None] * inv_freq[None, :]
    return jnp.cos(angles)[None, :, None, :], jnp.sin(angles)[None, :, None, :]


def apply_rope(vec_f32, cos_tab, sin_tab):
    half = HEAD_DIM // 2
    first = vec_f32[..., :half]
    second = vec_f32[..., half:]
    return jnp.concatenate([first * cos_tab - second * sin_tab, second * cos_tab + first * sin_tab], axis=-1)


def decoder_layer(hidden, weights, gain_attn, gain_mlp, cos_tab, sin_tab):
    w_q, w_kv, w_o, w_gu, w_down = weights
    rows, seq_len = hidden.shape[0], hidden.shape[1]
    heads = w_q.shape[1] // HEAD_DIM
    kv_heads = w_kv.shape[1] // (2 * HEAD_DIM)
    ff_width = w_down.shape[0]
    normed = rms_norm(hidden, gain_attn)
    query = jnp.einsum('bsd,de->bse', normed, w_q, preferred_element_type=jnp.float32).reshape(rows, seq_len, heads, HEAD_DIM)
    key_val = jnp.einsum('bsd,de->bse', normed, w_kv, preferred_element_type=jnp.float32).reshape(rows, seq_len, 2, kv_heads, HEAD_DIM)
    q_rot = apply_rope(query, cos_tab, sin_tab).astype(jnp.bfloat16).reshape(rows, seq_len, kv_heads, heads // kv_heads, HEAD_DIM)
    k_rot = apply_rope(key_val[:, :, 0], cos_tab, sin_tab).astype(jnp.bfloat16)
    v_val = key_val[:, :, 1].astype(jnp.bfloat16)
    scores = jnp.einsum('bqkrd,bskd->bkrqs', q_rot, k_rot, preferred_element_type=jnp.float32) * HEAD_DIM ** -0.5
    positions = jnp.arange(seq_len)
    scores = jnp.where(positions[:, None] >= positions[None, :], scores, -1e30)
    attn_prob = jax.nn.softmax(scores, axis=-1).astype(jnp.bfloat16)
    attn_out = jnp.einsum('bkrqs,bskd->bqkrd', attn_prob, v_val, preferred_element_type=jnp.float32).astype(jnp.bfloat16).reshape(rows, seq_len, heads * HEAD_DIM)
    attn_proj = jnp.einsum('bse,ed->bsd', attn_out, w_o, preferred_element_type=jnp.float32)
    hidden = (hidden.astype(jnp.float32) + attn_proj).astype(jnp.bfloat16)
    normed = rms_norm(hidden, gain_mlp)
    gate_up = jnp.einsum('bsd,df->bsf', normed, w_gu, preferred_element_type=jnp.float32)
    swiglu = (jax.nn.silu(gate_up[..., :ff_width]) * gate_up[..., ff_width:]).astype(jnp.bfloat16)
    down = jnp.einsum('bsf,fd->bsd', swiglu, w_down, preferred_element_type=jnp.float32)
    return (hidden.astype(jnp.float32) + down).astype(jnp.bfloat16)


def token_logprobs(hidden, gain_final, w_head, tokens):
    normed = rms_norm(hidden, gain_final)
    logits = jnp.einsum('bsd,vd->bsv', normed, w_head, preferred_element_type=jnp.float32)
    targets = jnp.roll(tokens, -1, axis=1)
    picked = jnp.take_along_axis(logits, targets[:, :, None], axis=-1)[:, :, 0]
    next_lp = picked - jax.nn.logsumexp(logits, axis=-1)
    col_index = jnp.arange(tokens.shape[1])[None, :]
    return jnp.where(col_index == 0, 0.0, jnp.roll(next_lp, 1, axis=1))


def advantages(all_rewards, all_groups, own_rewards, own_groups):
    slots = all_rewards.shape[0]
    counts = jnp.maximum(jax.ops.segment_sum(jnp.ones_like(all_rewards), all_groups, num_segments=slots), 1.0)
    means = jax.ops.segment_sum(all_rewards, all_groups, num_segments=slots) / counts
    centred = all_rewards - means[all_groups]
    spread = jnp.sqrt(jax.ops.segment_sum(centred * centred, all_groups, num_segments=slots) / counts)
    return (own_rewards - means[own_groups]) / (spread[own_groups] + ADV_EPS)


def row_losses(logp, logp_ref, logp_old, resp_mask, advantage):
    log_gap = logp_ref - logp
    kl_est = jnp.exp(log_gap) - log_gap - 1.0
    ratio = jnp.exp(logp - logp_old)
    adv_row = advantage[:, None]
    surrogate = jnp.minimum(ratio * adv_row, jnp.clip(ratio, 1.0 - CLIP_EPS, 1.0 + CLIP_EPS) * adv_row)
    per_token = -surrogate + BETA * kl_est
    weights = resp_mask.astype(jnp.float32)
    return jnp.sum(per_token * weights, axis=1) / jnp.sum(weights, axis=1)


def run_model(tokens, params, axes):
    w_q, w_kv, w_o, w_gu, w_down, norms, embed, head = params
    layers = w_q.shape[0]
    gains = lax.all_gather(norms, axes, axis=1, tiled=True)
    table = lax.all_gather(embed, axes, axis=0, tiled=True)
    hidden = jnp.take(table, tokens, axis=0)
    cos_tab, sin_tab = rope_tables(tokens.shape[1])
    for layer in range(layers):
        weights = [lax.all_gather(weight_arr[layer], axes, axis=0, tiled=True) for weight_arr in (w_q, w_kv, w_o, w_gu, w_down)]
        hidden = decoder_layer(hidden, weights, gains[2 * layer], gains[2 * layer + 1], cos_tab, sin_tab)
    w_head = lax.all_gather(head, axes, axis=0, tiled=True)
    return token_logprobs(hidden, gains[2 * layers], w_head, tokens)


def solution(mesh):
    both = ('rep', 'fsdp')
    row_spec = P(both, None)

    def weight_specs(axes):
        return [P(None, axes, None)] * 5 + [P(None, axes), P(axes, None), P(axes, None)]

    in_specs = tuple([row_spec, row_spec, row_spec, P(both), P(both)] + weight_specs('fsdp') + weight_specs(both))
    out_specs = (P(), row_spec, row_spec)

    def device_step(tokens, resp_mask, logp_old, rewards, group_id, *weights):
        logp = run_model(tokens, weights[:8], 'fsdp')
        logp_ref = run_model(tokens, weights[8:], both)
        all_rewards = lax.all_gather(rewards, both, tiled=True)
        all_groups = lax.all_gather(group_id, both, tiled=True)
        advantage = advantages(all_rewards, all_groups, rewards, group_id)
        row_part = row_losses(logp, logp_ref, logp_old, resp_mask, advantage)
        loss = lax.psum(jnp.sum(row_part), both) / all_rewards.shape[0]
        return loss, logp, logp_ref

    return jax.shard_map(device_step, mesh=mesh, in_specs=in_specs, out_specs=out_specs, check_vma=False)
```

profile of v0, /device:TPU:0, one launch (start us, length us, event | category | flops | bytes accessed | tf_op | source)
XLA Modules:
  0.0 2690.3 jit_solution(2511007018385644422)
XLA Ops:
  7.2 66.3 %copy.74 = bf16[16000,1600]{1,0:T(8,128)(2,1)} copy(bf16[16000,1600]{0,1:T(8,128)(2,1)} %param.36) | data formatting | bytes 102400000 | tf_op args[11]
  102.3 20.1 fusion.280
  159.6 22.2 all-reduce
  182.0 23.0 all-reduce.1
  217.2 17.3 gather_fusion.3
  234.6 443.7 %all-gather.93.cloned.1.call-done = bf16[8,4000,1600]{1,2,0:T(8,128)(2,1)} async-done(((bf16[1,4000,1600]{1,2,0:T(8,128)(2,1)}), bf16[8,4000,1600]{1,2,0:T(8,128)(2,1)}) %all-gather.93.cloned.1.call-update) | async-done | bytes 102400016 | tf_op jit(solution)/shard_map/all_gather | solution.py:94
  678.3 126.8 %copy.88 = bf16[8,4000,1600]{2,1,0:T(8,128)(2,1)} copy(bf16[8,4000,1600]{1,2,0:T(8,128)(2,1)} %all-gather.93.cloned.1.call-done) | data formatting | bytes 204800000 | tf_op jit(solution)/shard_map/all_gather | solution.py:94
  805.1 22.9 gather_fusion.5
  920.8 34.2 %subtract_convert_fusion.1 = (bf16[32,32,25,32]{3,2,1,0:T(8,128)(2,1)}, bf16[32,32,25,32]{3,2,1,0:T(8,128)(2,1)}, bf16[32,32,25,32]{3,2,1,0:T(8,128)(2,1)}, bf16[32,32,25,32]{3,2,1,0:T(8,128)(2,1)}) fusion(f32[32,32,25,64]{3,2,1,0:T(8,128)} %reshape.312, f32[32,32]{1,0:T(8,128)S(1)} %get-tuple-element.68, f32[32,32]{1,0:T(8,128)S(1)} %get-tuple-element.67, ...), kind=kLoop, calls=%fused_computation.37 | loop fusion | flops 13107200 | bytes 19668992 | tf_op jit(solution)/shard_map/convert.20
  976.9 17.7 fusion.293
  1036.9 40.6 %fusion.8 = f32[32,32,8704]{2,1,0:T(8,128)} fusion(bf16[1,1600,8704]{2,1,0:T(8,128)(2,1)} %all-gather.79.cloned.1.call-done, bf16[32,32,1600]{2,1,0:T(8,128)(2,1)} %get-tuple-element.76, f32[1600]{0:T(1024)S(1)} %copy-done.50, f32[32,32]{1,0:T(8,128)S(1)} %add_rsqrt_fusion.3), kind=kOutput, calls=%fused_computation.20 | convolution fusion | flops 28527820800 | bytes 66791680 | tf_op jit(solution)/shard_map/bsd,df->bsf/dot_general | solution.py:54
  1077.5 27.9 %fusion.64 = (f32[32,32]{1,0:T(8,128)S(1)}, bf16[32,32,1600]{2,1,0:T(8,128)(2,1)}) fusion(bf16[1,4352,1600]{2,1,0:T(8,128)(2,1)} %all-gather.81.cloned.1.call-done, f32[32,32,8704]{2,1,0:T(8,128)} %fusion.8, bf16[32,32,1600]{2,1,0:T(8,128)(2,1)} %get-tuple-element.76), kind=kOutput, calls=%fused_computation.128 | convolution fusion | flops 14297201664 | bytes 56135680 | tf_op jit(solution)/shard_map/bsf,fd->bsd/dot_general | solution.py:56
  1136.0 17.8 fusion.290
  1195.9 40.6 %fusion.12 = f32[32,32,8704]{2,1,0:T(8,128)} fusion(bf16[1,1600,8704]{2,1,0:T(8,128)(2,1)} %all-gather.59.cloned.1.call-done, bf16[32,32,1600]{2,1,0:T(8,128)(2,1)} %get-tuple-element.72, f32[1600]{0:T(1024)S(1)} %copy-done.49, f32[32,32]{1,0:T(8,128)S(1)} %add_rsqrt_fusion.8), kind=kOutput, calls=%fused_computation.24 | convolution fusion | flops 28527820800 | bytes 66791680 | tf_op jit(solution)/shard_map/bsd,df->bsf/dot_general | solution.py:54
  1236.6 30.2 %fusion.48 = (f32[32,32]{1,0:T(8,128)S(1)}, bf16[32,32,1600]{2,1,0:T(8,128)(2,1)}) fusion(bf16[1,4352,1600]{1,2,0:T(8,128)(2,1)} %all-gather.61.cloned.1.call-done, f32[32,32,8704]{2,1,0:T(8,128)} %fusion.12, bf16[32,32,1600]{2,1,0:T(8,128)(2,1)} %get-tuple-element.72), kind=kOutput, calls=%fused_computation.112 | convolution fusion | flops 14297201664 | bytes 56135680 | tf_op jit(solution)/shard_map/bsf,fd->bsd/dot_general | solution.py:56
  1335.4 34.5 %subtract_convert_fusion = (bf16[32,32,25,32]{3,2,1,0:T(8,128)(2,1)}, bf16[32,32,25,32]{3,2,1,0:T(8,128)(2,1)}, bf16[32,32,25,32]{3,2,1,0:T(8,128)(2,1)}, bf16[32,32,25,32]{3,2,1,0:T(8,128)(2,1)}) fusion(f32[32,32,25,64]{3,2,1,0:T(8,128)} %reshape.315, f32[32,32]{1,0:T(8,128)S(1)} %copy-done.27, f32[32,32]{1,0:T(8,128)S(1)} %copy-done.25, ...), kind=kLoop, calls=%fused_computation.35 | loop fusion | flops 13107200 | bytes 19668992 | tf_op jit(solution)/shard_map/convert.13
  1390.6 16.9 fusion.300
  1448.0 40.6 %fusion.6 = f32[32,32,8704]{2,1,0:T(8,128)} fusion(bf16[1,1600,8704]{2,1,0:T(8,128)(2,1)} %all-gather.89.cloned.1.call-done, bf16[32,32,1600]{2,1,0:T(8,128)(2,1)} %get-tuple-element.92, f32[1600]{0:T(1024)S(1)} %copy-done.45, f32[32,32]{1,0:T(8,128)S(1)} %add_rsqrt_fusion.1), kind=kOutput, calls=%fused_computation.18 | convolution fusion | flops 28527820800 | bytes 66791680 | tf_op jit(solution)/shard_map/bsd,df->bsf/dot_general | solution.py:54
  1488.6 27.7 %fusion.37 = (f32[32,32]{1,0:T(8,128)S(1)}, bf16[32,32,1600]{2,1,0:T(8,128)(2,1)}) fusion(bf16[1,4352,1600]{2,1,0:T(8,128)(2,1)} %all-gather.91.cloned.1.call-done, f32[32,32,8704]{2,1,0:T(8,128)} %fusion.6, bf16[32,32,1600]{2,1,0:T(8,128)(2,1)} %get-tuple-element.92), kind=kOutput, calls=%fused_computation.101 | convolution fusion | flops 14297201664 | bytes 56135680 | tf_op jit(solution)/shard_map/bsf,fd->bsd/dot_general | solution.py:56
  1516.3 375.2 %all-gather.95.cloned.1.call-done = bf16[8,4000,1600]{1,2,0:T(8,128)(2,1)} async-done(((bf16[1,4000,1600]{1,2,0:T(8,128)(2,1)}), bf16[8,4000,1600]{1,2,0:T(8,128)(2,1)}) %all-gather.95.cloned.1.call-update) | async-done | bytes 102400016 | tf_op jit(solution)/shard_map/all_gather | solution.py:100
  1891.6 86.1 %copy.104 = bf16[8,4000,1600]{1,0,2:T(8,128)(2,1)} copy(bf16[8,4000,1600]{1,2,0:T(8,128)(2,1)} %all-gather.95.cloned.1.call-done) | data formatting | bytes 204800000 | tf_op jit(solution)/shard_map/all_gather | solution.py:100
  1977.7 163.8 %reshape.501 = bf16[32000,1600,1]{0,1,2:T(8,128)(2,1)} reshape(bf16[8,4000,1600]{1,0,2:T(8,128)(2,1)} %copy.104) | data formatting | bytes 204800000
  2141.5 131.4 %fusion.303 = (f32[32,32]{1,0:T(8,128)S(1)}, f32[32,32,32000]{2,1,0:T(8,128)}) fusion(bf16[32000,1600,1]{0,1,2:T(8,128)(2,1)} %reshape.501, bf16[32,32,1600]{2,1,0:T(8,128)(2,1)} %get-tuple-element.94, f32[1600]{0:T(1024)S(1)} %copy-done.44, f32[32,32]{1,0:T(8,128)S(1)} %add_rsqrt_fusion), kind=kOutput, calls=%fused_computation.362 | convolution fusion | flops 104896921600 | bytes 236763392 | tf_op jit(solution)/shard_map/bsd,vd->bsv/dot_general | solution.py:62
  2272.8 14.3 gather_fusion.6
  2303.3 17.3 fusion.296
  2361.8 41.0 %fusion.10 = f32[32,32,8704]{2,1,0:T(8,128)} fusion(bf16[1,1600,8704]{2,1,0:T(8,128)(2,1)} %all-gather.69.cloned.1.call-done, bf16[32,32,1600]{2,1,0:T(8,128)(2,1)} %get-tuple-element.84, f32[1600]{0:T(1024)S(1)} %copy-done.43, f32[32,32]{1,0:T(8,128)S(1)} %add_rsqrt_fusion.6), kind=kOutput, calls=%fused_computation.22 | convolution fusion | flops 28527820800 | bytes 66791680 | tf_op jit(solution)/shard_map/bsd,df->bsf/dot_general | solution.py:54
  2402.8 28.4 %fusion.34 = (f32[32,32]{1,0:T(8,128)S(1)}, bf16[32,32,1600]{2,1,0:T(8,128)(2,1)S(1)}) fusion(bf16[1,4352,1600]{1,2,0:T(8,128)(2,1)} %all-gather.71.cloned.1.call-done, f32[32,32,8704]{2,1,0:T(8,128)} %fusion.10, bf16[32,32,1600]{2,1,0:T(8,128)(2,1)} %get-tuple-element.84), kind=kOutput, calls=%fused_computation.98 | convolution fusion | flops 14297201664 | bytes 56135680 | tf_op jit(solution)/shard_map/bsf,fd->bsd/dot_general | solution.py:56
  2431.2 40.6 %exponential_reduce_fusion = f32[32,32]{1,0:T(8,128)} fusion(f32[32,32,32000]{2,1,0:T(8,128)} %get-tuple-element.96, f32[32,32]{1,0:T(8,128)S(1)} %copy-done.31), kind=kLoop, calls=%fused_computation.14 | loop fusion | flops 65534976 | bytes 131080192 | tf_op jit(solution)/shard_map/reduce_sum | solution.py:65
  2471.8 131.1 %fusion.299 = (f32[32,32]{1,0:T(8,128)S(1)}, f32[32,32,32000]{2,1,0:T(8,128)}) fusion(bf16[32000,1600]{0,1:T(8,128)(2,1)} %all-gather.51.cloned.1.call-done, bf16[32,32,1600]{2,1,0:T(8,128)(2,1)S(1)} %get-tuple-element.86, f32[1600]{0:T(1024)S(1)} %copy-done.42, f32[32,32]{1,0:T(8,128)S(1)} %add_rsqrt_fusion.5), kind=kOutput, calls=%fused_computation.360 | convolution fusion | flops 104896921600 | bytes 236763392 | tf_op jit(solution)/shard_map/bsd,vd->bsv/dot_general | solution.py:62
  2603.0 14.1 gather_fusion.4
  2617.2 40.0 %exponential_reduce_fusion.1 = f32[32,32]{1,0:T(8,128)S(1)} fusion(f32[32,32,32000]{2,1,0:T(8,128)} %get-tuple-element.88, f32[32,32]{1,0:T(8,128)S(1)} %is-finite_select_fusion.1), kind=kLoop, calls=%fused_computation.15 | loop fusion | flops 65534976 | bytes 131080192 | tf_op jit(solution)/shard_map/reduce_sum | solution.py:65
  2659.0 22.4 psum.7
  (323 shorter events, 496.3 us)
Async XLA Ops:
  7.2 210.1 %all-gather.49.cloned.1.call-start = ((), (), s32[]{:S(2)}) async-start(), calls=%async_computation | async-start | bytes 159744000 | tf_op jit(solution)/shard_map/all_gather | solution.py:94
  73.6 604.7 %all-gather.93.cloned.1.call-start = ((), (), s32[]{:S(2)}) async-start(), calls=%async_computation.22 | async-start | bytes 117964800 | tf_op jit(solution)/shard_map/all_gather | solution.py:94
  74.3 757.3 %all-gather.53.cloned.1.call-start = ((), (), s32[]{:S(2)}) async-start(), calls=%async_computation.2 | async-start | bytes 3072000 | tf_op jit(solution)/shard_map/all_gather | solution.py:98
  76.7 772.8 %all-gather.73.cloned.1.call-start = ((), (), s32[]{:S(2)}) async-start(), calls=%async_computation.12 | async-start | bytes 2304000 | tf_op jit(solution)/shard_map/all_gather | solution.py:98
  77.7 794.1 %all-gather.55.cloned.1.call-start = ((), (), s32[]{:S(2)}) async-start(), calls=%async_computation.3 | async-start | bytes 7987200 | tf_op jit(solution)/shard_map/all_gather | solution.py:98
  83.1 813.3 %all-gather.75.cloned.1.call-start = ((), (), s32[]{:S(2)}) async-start(), calls=%async_computation.13 | async-start | bytes 5990400 | tf_op jit(solution)/shard_map/all_gather | solution.py:98
  84.4 941.0 %all-gather.77.cloned.1.call-start = ((), (), s32[]{:S(2)}) async-start(), calls=%async_computation.14 | async-start | bytes 5990400 | tf_op jit(solution)/shard_map/all_gather | solution.py:98
  85.6 951.2 %all-gather.79.cloned.1.call-start = ((), (), s32[]{:S(2)}) async-start(), calls=%async_computation.15 | async-start | bytes 31334400 | tf_op jit(solution)/shard_map/all_gather | solution.py:98
  92.1 985.4 %all-gather.81.cloned.1.call-start = ((), (), s32[]{:S(2)}) async-start(), calls=%async_computation.16 | async-start | bytes 16293888 | tf_op jit(solution)/shard_map/all_gather | solution.py:98
  96.3 1009.2 %all-gather.83.cloned.1.call-start = ((), (), s32[]{:S(2)}) async-start(), calls=%async_computation.17 | async-start | bytes 2304000 | tf_op jit(solution)/shard_map/all_gather | solution.py:98
  96.9 1087.5 %all-gather.57.cloned.1.call-start = ((), (), s32[]{:S(2)}) async-start(), calls=%async_computation.4 | async-start | bytes 7987200 | tf_op jit(solution)/shard_map/all_gather | solution.py:98
  102.2 1093.7 %all-gather.59.cloned.1.call-start = ((), (), s32[]{:S(2)}) async-start(), calls=%async_computation.5 | async-start | bytes 41779200 | tf_op jit(solution)/shard_map/all_gather | solution.py:98
  122.4 1114.1 %all-gather.61.cloned.1.call-start = ((), (), s32[]{:S(2)}) async-start(), calls=%async_computation.6 | async-start | bytes 20889600 | tf_op jit(solution)/shard_map/all_gather | solution.py:98
  132.7 1134.1 %all-gather.63.cloned.1.call-start = ((), (), s32[]{:S(2)}) async-start(), calls=%async_computation.7 | async-start | bytes 3072000 | tf_op jit(solution)/shard_map/all_gather | solution.py:98
  133.2 1152.3 %all-gather.65.cloned.1.call-start = ((), (), s32[]{:S(2)}) async-start(), calls=%async_computation.8 | async-start | bytes 7987200 | tf_op jit(solution)/shard_map/all_gather | solution.py:98
  133.8 1176.7 %all-gather.85.cloned.1.call-start = ((), (), s32[]{:S(2)}) async-start(), calls=%async_computation.18 | async-start | bytes 5990400 | tf_op jit(solution)/shard_map/all_gather | solution.py:98
  134.4 1302.1 %all-gather.87.cloned.1.call-start = ((), (), s32[]{:S(2)}) async-start(), calls=%async_computation.19 | async-start | bytes 5990400 | tf_op jit(solution)/shard_map/all_gather | solution.py:98
  135.0 1313.0 %all-gather.89.cloned.1.call-start = ((), (), s32[]{:S(2)}) async-start(), calls=%async_computation.20 | async-start | bytes 31334400 | tf_op jit(solution)/shard_map/all_gather | solution.py:98
  135.6 1353.1 %all-gather.91.cloned.1.call-start = ((), (), s32[]{:S(2)}) async-start(), calls=%async_computation.21 | async-start | bytes 16293888 | tf_op jit(solution)/shard_map/all_gather | solution.py:98
  136.3 1755.3 %all-gather.95.cloned.1.call-start = ((), (), s32[]{:S(2)}) async-start(), calls=%async_computation.23 | async-start | bytes 117964800 | tf_op jit(solution)/shard_map/all_gather | solution.py:100
  136.9 2213.6 %all-gather.67.cloned.1.call-start = ((), (), s32[]{:S(2)}) async-start(), calls=%async_computation.9 | async-start | bytes 7987200 | tf_op jit(solution)/shard_map/all_gather | solution.py:98
  137.6 2224.2 %all-gather.69.cloned.1.call-start = ((), (), s32[]{:S(2)}) async-start(), calls=%async_computation.10 | async-start | bytes 41779200 | tf_op jit(solution)/shard_map/all_gather | solution.py:98
  138.4 2264.5 %all-gather.71.cloned.1.call-start = ((), (), s32[]{:S(2)}) async-start(), calls=%async_computation.11 | async-start | bytes 20889600 | tf_op jit(solution)/shard_map/all_gather | solution.py:98
  139.2 2332.7 %all-gather.51.cloned.1.call-start = ((), (), s32[]{:S(2)}) async-start(), calls=%async_computation.1 | async-start | bytes 153600000 | tf_op jit(solution)/shard_map/all_gather | solution.py:100
  139.9 885.5 %copy-start.35 = (pred[32,32]{1,0:T(8,128)(4,1)}, pred[32,32]{1,0:T(8,128)(4,1)S(1)}, u32[]{:S(2)}) copy-start(pred[32,32]{1,0:T(8,128)(4,1)S(1)} %compare_and_fusion.1) | copy-start | bytes 3076
  158.6 815.2 %copy-start.24 = (f32[32,32]{1,0:T(8,128)}, f32[32,32]{1,0:T(8,128)S(1)}, u32[]{:S(2)}) copy-start(f32[32,32]{1,0:T(8,128)S(1)} %get-tuple-element.67) | copy-start | bytes 12292
  158.6 815.2 %copy-start.26 = (f32[32,32]{1,0:T(8,128)}, f32[32,32]{1,0:T(8,128)S(1)}, u32[]{:S(2)}) copy-start(f32[32,32]{1,0:T(8,128)S(1)} %get-tuple-element.68) | copy-start | bytes 12292
  234.6 637.2 %copy-start.8 = (bf16[1024,1600]{1,0:T(8,128)(2,1)}, bf16[1024,1600]{1,0:T(8,128)(2,1)S(1)}, u32[]{:S(2)}) copy-start(bf16[1024,1600]{1,0:T(8,128)(2,1)S(1)} %gather_fusion.3) | copy-start | bytes 9830404
  1977.7 163.8 %copy-start.44 = (f32[1600]{0:T(1024)S(1)}, f32[1600]{0:T(1024)}, u32[]{:S(2)}) copy-start(f32[1600]{0:T(1024)} %get-tuple-element.10) | copy-start | bytes 19204
  2141.5 131.4 %copy-start = (s32[1024]{0:T(1024)S(1)}, s32[1024]{0:T(1024)}, u32[]{:S(2)}) copy-start(s32[1024]{0:T(1024)} %reshape.458) | copy-start | bytes 12292
  2272.8 77.1 %copy-start.33 = (f32[32,32]{1,0:T(8,128)}, f32[32,32]{1,0:T(8,128)S(1)}, u32[]{:S(2)}) copy-start(f32[32,32]{1,0:T(8,128)S(1)} %get-tuple-element.95) | copy-start | bytes 12292
  2471.8 131.2 %copy-start.1 = (s32[1024]{0:T(1024)S(1)}, s32[1024]{0:T(1024)}, u32[]{:S(2)}) copy-start(s32[1024]{0:T(1024)} %reshape.458) | copy-start | bytes 12292
  (57 other events, 995.1 us)
Sparse Core Ops, SparseCore 0:
  73.7 143.5 all-gather.48
  219.1 459.1 all-gather.92
  679.8 7.7 all-gather.52
  689.2 22.8 all-gather.72
  713.5 13.0 all-gather.54
  728.3 36.6 all-gather.74
  766.8 35.4 all-gather.76
  804.1 131.0 all-gather.78
  937.0 74.3 all-gather.80
  1013.0 21.7 all-gather.82
  1036.3 13.0 all-gather.56
  1050.8 43.6 all-gather.58
  1096.0 25.4 all-gather.60
  1122.8 8.9 all-gather.62
  1133.1 14.2 all-gather.64
  1149.1 36.6 all-gather.84
  1187.4 35.4 all-gather.86
  1224.6 131.0 all-gather.88
  1357.5 74.3 all-gather.90
  1433.6 457.9 all-gather.94
  1893.1 13.0 all-gather.66
  1907.7 43.6 all-gather.68
  1952.9 25.4 all-gather.70
  1979.8 136.7 all-gather.50
where the time goes:
time: 2710 us; the launch traced here: 2690 us
  local copies, waits for them, and re-layouts  829 us (31%)
  waiting for transfers between devices  828 us (31%)
  matrix products  758 us (28%)
  other arithmetic  174 us (6%)
  blocking collectives  83.2 us (3%)
    all_gather x2, waiting for transfers between devices, run_model(): table = lax.all_gather(embed, axes, axis=0, tiled=True)  445 us
    all_gather x2, waiting for transfers between devices, run_model(): w_head = lax.all_gather(head, axes, axis=0, tiled=True)  375 us
    dot_general x2, matrix products, token_logprobs(): jnp.einsum('bsd,vd->bsv', normed, w_head, preferred_element_type=jnp.floa...  263 us
    unnamed x133, local copies, waits for them, and re-layouts  245 us
    dot_general x4, matrix products, decoder_layer(): jnp.einsum('bsd,df->bsf', normed, w_gu, preferred_element_type=jnp.float32)  163 us
    all_gather x1, local copies, waits for them, and re-layouts, run_model(): table = lax.all_gather(embed, axes, axis=0, tiled=True)  127 us
    dot_general x4, matrix products, decoder_layer(): jnp.einsum('bsf,fd->bsd', swiglu, w_down, preferred_element_type=jnp.floa...  114 us
    all_gather x1, local copies, waits for them, and re-layouts, run_model(): w_head = lax.all_gather(head, axes, axis=0, tiled=True)  86.1 us
  transfers between devices with their start and end apart: 24, of which 3 were waited for; matrix products, arithmetic and copies ran while one was open for 56% of the time, Pallas kernels for 0%

commit v1 on v0

v1 whole, which is shorter than its diff:
```python
import functools

import jax
import jax.numpy as jnp
from jax import lax
from jax.experimental import pallas as pl
from jax.experimental.pallas import tpu as pltpu
from jax.sharding import PartitionSpec as P

HEAD_DIM = 64
EPS = 1e-6
ROPE_BASE = 10000.0
CLIP_EPS = 0.2
BETA = 0.04
ADV_EPS = 1e-4

F32 = jnp.float32
BF16 = jnp.bfloat16
NEG = -3.0e38
VMEM_LIMIT = 62 * 1024 * 1024

D = 1600
QH = 25
KVH = 5
QKV = 2240
FF = 4352
SEQ = 32
TB = 256
SUB = 128
FT = 256
VT = 2048


def dot(lhs, rhs):
    return lax.dot_general(lhs, rhs, (((1,), (0,)), ((), ())), preferred_element_type=F32)


def dot_nt(lhs, rhs):
    return lax.dot_general(lhs, rhs, (((1,), (1,)), ((), ())), preferred_element_type=F32)


def rms(x, gain):
    x = x.astype(F32)
    inv = lax.rsqrt(jnp.sum(x * x, axis=-1, keepdims=True) * (1.0 / D) + EPS)
    return (x * inv * gain).astype(BF16)


def row_copies(parts, layer, half_of, dst, sems, base):
    out = []
    for p, part in enumerate(parts):
        src = part if layer is None else part.at[layer]
        rows = src.shape[0]
        at = pl.multiple_of(half_of(p) * rows, 8) if len(parts) > 1 else 0
        out.append(pltpu.make_async_copy(src, dst.at[pl.ds(at, rows)], sems.at[base + p]))
    return out


def attn_kernel(n, layer, core_ref, h_ref, gain_ref, cos_ref, sin_ref, *refs):
    qkv_parts, wo_parts = refs[:n], refs[n:2 * n]
    out_ref, wqkv, wo, qkv_s, qk_s, o_s, sc_s, p_s, sems = refs[2 * n:]
    core = core_ref[0]

    def half_of(p):
        return jnp.bitwise_xor(core, p)

    first = row_copies(qkv_parts, layer, half_of, wqkv, sems, 0)
    second = row_copies(wo_parts, layer, half_of, wo, sems, n)
    for copy in first + second:
        copy.start()
    for copy in first:
        copy.wait()

    lane = lax.broadcasted_iota(jnp.int32, (1, 128), 1)
    low_half = lane < 64
    rot_mask = (lane % 64) < 32
    q_idx = lax.broadcasted_iota(jnp.int32, (SUB, 2 * SUB), 0)
    k_idx = lax.broadcasted_iota(jnp.int32, (SUB, 2 * SUB), 1) % SUB
    keep = (q_idx // SEQ == k_idx // SEQ) & (k_idx <= q_idx)
    zero = jnp.zeros((), BF16)

    def project(b):
        rows = pl.ds(pl.multiple_of(b * TB, TB), TB)
        qkv_s[...] = dot(rms(h_ref[rows, :], gain_ref[...]), wqkv[...])
        cos, sin = cos_ref[...], sin_ref[...]
        for j in range(15):
            x = qkv_s[:, 128 * j:128 * (j + 1)]
            rot = jnp.where(rot_mask, pltpu.roll(x, 96, 1), pltpu.roll(x, 32, 1))
            qk_s[:, 128 * j:128 * (j + 1)] = (x * cos + rot * sin).astype(BF16)

    def attend(s):
        rows = slice(s * SUB, (s + 1) * SUB)
        k_pads, v_pads = [], []
        for g in range(KVH):
            c, side = divmod(25 + g, 2)
            x = qk_s[rows, 128 * c:128 * (c + 1)].astype(F32)
            y = pltpu.roll(x, 64, 1)
            at_low, at_high = (y, x) if side else (x, y)
            k_pads.append((jnp.where(low_half, at_low, 0.0).astype(BF16), jnp.where(low_half, 0.0, at_high).astype(BF16)))
            c, side = divmod(g, 2)
            if c < 2:
                x = qkv_s[rows, 1920 + 128 * c:2048 + 128 * c]
            else:
                x = jnp.concatenate([qkv_s[rows, 2176:2240], jnp.zeros((SUB, 64), F32)], axis=1)
            y = pltpu.roll(x, 64, 1)
            at_low, at_high = (y, x) if side else (x, y)
            v_pads.append((jnp.where(low_half, at_low, 0.0).astype(BF16), jnp.where(low_half, 0.0, at_high).astype(BF16)))
        heads = [((2 * j) // 5, min((2 * j + 1) // 5, KVH - 1)) for j in range(13)]
        for j, (ga, gb) in enumerate(heads):
            keys = jnp.concatenate([k_pads[ga][0], k_pads[gb][1]], axis=0)
            scores = dot_nt(qk_s[rows, 128 * j:128 * (j + 1)], keys) * (HEAD_DIM ** -0.5)
            sc_s[:, 2 * SUB * j:2 * SUB * (j + 1)] = jnp.where(keep, scores, -1e30)
        for i in range(QH):
            x = sc_s[:, SUB * i:SUB * (i + 1)]
            e = jnp.exp(x - jnp.max(x, axis=1, keepdims=True))
            p_s[:, SUB * i:SUB * (i + 1)] = (e * (1.0 / jnp.sum(e, axis=1, keepdims=True))).astype(BF16)
        for j, (ga, gb) in enumerate(heads):
            if j < 12:
                vals = jnp.concatenate([v_pads[ga][0], v_pads[gb][1]], axis=0)
                o_s[rows, 128 * j:128 * (j + 1)] = dot(p_s[:, 2 * SUB * j:2 * SUB * (j + 1)], vals).astype(BF16)
            else:
                o_s[rows, 1536:1600] = dot(p_s[:, 2 * SUB * j:2 * SUB * j + SUB], v_pads[ga][0]).astype(BF16)[:, :64]

    def block(b, carry):
        rows = pl.ds(pl.multiple_of(b * TB, TB), TB)
        project(b)
        for s in range(TB // SUB):
            attend(s)

        @pl.when(b == 0)
        def _():
            for copy in second:
                copy.wait()

        out_ref[rows, :] = (h_ref[rows, :].astype(F32) + dot(o_s[...], wo[...])).astype(BF16)
        return carry

    lax.fori_loop(0, h_ref.shape[0] // TB, block, 0)


def attention_block(h, gain, tabs, w_qkv, w_o, layer, core):
    n = len(w_qkv)
    t = h.shape[0]
    vm = pl.BlockSpec(memory_space=pltpu.VMEM)
    anym = pl.BlockSpec(memory_space=pl.ANY)
    return pl.pallas_call(
        functools.partial(attn_kernel, n, layer),
        out_shape=jax.ShapeDtypeStruct((t, D), BF16),
        in_specs=[pl.BlockSpec(memory_space=pltpu.SMEM), vm, vm, vm, vm] + [anym] * (2 * n),
        out_specs=vm,
        scratch_shapes=[
            pltpu.VMEM((D, QKV), BF16), pltpu.VMEM((D, D), BF16), pltpu.VMEM((TB, QKV), F32),
            pltpu.VMEM((TB, 1920), BF16), pltpu.VMEM((TB, D), BF16), pltpu.VMEM((SUB, 26 * SUB), F32), pltpu.VMEM((SUB, 26 * SUB), BF16),
            pltpu.SemaphoreType.DMA((2 * n,)),
        ],
        compiler_params=pltpu.CompilerParams(vmem_limit_bytes=VMEM_LIMIT),
        cost_estimate=pl.CostEstimate(flops=2 * t * D * (QKV + D), bytes_accessed=2 * D * (QKV + D), transcendentals=0),
        name="attn",
    )(core, h, gain, tabs[0], tabs[1], *w_qkv, *w_o)


def mlp_kernel(n, layer, last, core_ref, h_ref, gain_ref, fin_ref, *refs):
    gu_parts, dn_parts = refs[:n], refs[n:2 * n]
    out_ref, wg, wu, wd, c_s, act_s, acc, sems, dn_sems = refs[2 * n:]
    core = core_ref[0]
    steps = FF // FT
    half_subs = FF // 2 // 128

    def gu_copies(j, slot):
        out = []
        for p, part in enumerate(gu_parts):
            src = part if layer is None else part.at[layer]
            rows = src.shape[0]
            at = pl.multiple_of(jnp.bitwise_xor(core, p) * rows, 8) if n > 1 else 0
            for t, dst in enumerate((wg, wu)):
                cols = pl.ds(pl.multiple_of(t * FF + j * FT, 128), FT)
                out.append(pltpu.make_async_copy(src.at[:, cols], dst.at[slot, pl.ds(at, rows)], sems.at[slot, 2 * p + t]))
        return out

    def dn_copy(part, j, i):
        slot = lax.rem(j, 3)
        src = part if layer is None else part.at[layer]
        if n == 1:
            at = pl.multiple_of(j * FT, FT)
            return pltpu.make_async_copy(src.at[pl.ds(at, FT)], wd.at[slot], dn_sems.at[slot, 0])
        sub = 2 * j + i
        col = pl.multiple_of(jnp.where(sub >= half_subs, sub - half_subs, sub) * 128, 128)
        return pltpu.make_async_copy(src.at[:, pl.ds(col, 128)], wd.at[slot, :, pl.ds(128 * i, 128)], dn_sems.at[slot, i])

    def start(j):
        for copy in gu_copies(j, lax.rem(j, 2)):
            copy.start()
        if n == 1:
            dn_copy(dn_parts[0], j, 0).start()
        else:
            for i in range(2):
                half = (2 * j + i >= half_subs).astype(jnp.int32)
                mine = half == core

                @pl.when(mine)
                def _():
                    dn_copy(dn_parts[0], j, i).start()

                @pl.when(jnp.logical_not(mine))
                def _():
                    dn_copy(dn_parts[1], j, i).start()

    def wait_gu(j):
        for copy in gu_copies(j, lax.rem(j, 2)):
            copy.wait()

    def wait_dn(j):
        for i in range(n):
            dn_copy(dn_parts[0], j, i).wait()

    def gate_up(j):
        slot = lax.rem(j, 2)
        g = dot(c_s[...], wg[slot])
        u = dot(c_s[...], wu[slot])
        act_s[slot] = (g * jax.nn.sigmoid(g) * u).astype(BF16)

    def down(j):
        act, w = act_s[lax.rem(j, 2)], wd[lax.rem(j, 3)]
        acc[...] += dot(act, w) if n == 1 else dot_nt(act, w)

    zero = jnp.int32(0)
    start(zero)
    start(zero + 1)
    c_s[...] = rms(h_ref[...], gain_ref[...])
    acc[...] = h_ref[...].astype(F32)
    wait_gu(zero)
    gate_up(zero)

    def step(j, carry):
        @pl.when(j + 1 < steps)
        def _():
            start(j + 1)

        wait_gu(j)
        wait_dn(j - 1)
        gate_up(j)
        down(j - 1)
        return carry

    lax.fori_loop(1, steps, step, 0)
    wait_dn(zero + (steps - 1))
    down(zero + (steps - 1))
    out = acc[...].astype(BF16)
    out_ref[...] = rms(out, fin_ref[...]) if last else out


def mlp_block(h, gain, fin, w_gu, w_dn, layer, last, core):
    n = len(w_gu)
    t = h.shape[0]
    vm = pl.BlockSpec(memory_space=pltpu.VMEM)
    anym = pl.BlockSpec(memory_space=pl.ANY)
    return pl.pallas_call(
        functools.partial(mlp_kernel, n, layer, last),
        out_shape=jax.ShapeDtypeStruct((t, D), BF16),
        in_specs=[pl.BlockSpec(memory_space=pltpu.SMEM), vm, vm, vm] + [anym] * (2 * n),
        out_specs=vm,
        scratch_shapes=[
            pltpu.VMEM((2, D, FT), BF16), pltpu.VMEM((2, D, FT), BF16), pltpu.VMEM((3, FT, D) if n == 1 else (3, D, FT), BF16),
            pltpu.VMEM((t, D), BF16), pltpu.VMEM((2, t, FT), BF16), pltpu.VMEM((t, D), F32),
            pltpu.SemaphoreType.DMA((2, 4)), pltpu.SemaphoreType.DMA((3, 2)),
        ],
        compiler_params=pltpu.CompilerParams(vmem_limit_bytes=VMEM_LIMIT),
        cost_estimate=pl.CostEstimate(flops=6 * t * D * FF, bytes_accessed=6 * D * FF, transcendentals=0),
        name="mlp",
    )(core, h, gain, fin, *w_gu, *w_dn)


def head_kernel(vocab, x_ref, w_ref, tgt_ref, out_ref, m_s, s_s, p_s):
    j = pl.program_id(1)

    @pl.when(j == 0)
    def _():
        m_s[...] = jnp.full(m_s.shape, NEG, F32)
        s_s[...] = jnp.zeros(s_s.shape, F32)
        p_s[...] = jnp.zeros(p_s.shape, F32)

    lane = lax.broadcasted_iota(jnp.int32, m_s.shape, 1)
    rel = tgt_ref[...] - lane - j * VT
    held = vocab - j * VT
    for at in range(0, VT, 256):
        logits = dot(x_ref[...], w_ref[:, at:at + 256])
        cols = [logits[:, :128], logits[:, 128:]]
        if at + 256 > (vocab % VT or VT):
            cols = [jnp.where(lane < held - at - 128 * c, x, NEG) for c, x in enumerate(cols)]
        m_old = m_s[...]
        m_new = jnp.maximum(m_old, jnp.maximum(cols[0], cols[1]))
        s_s[...] = s_s[...] * jnp.exp(m_old - m_new) + (jnp.exp(cols[0] - m_new) + jnp.exp(cols[1] - m_new))
        m_s[...] = m_new
        p_s[...] += jnp.where(rel == at, cols[0], jnp.where(rel == at + 128, cols[1], 0.0))

    @pl.when(j == pl.num_programs(1) - 1)
    def _():
        m = m_s[...]
        top = jnp.max(m, axis=1, keepdims=True)
        lse = top + jnp.log(jnp.sum(s_s[...] * jnp.exp(m - top), axis=1, keepdims=True))
        picked = jnp.sum(p_s[...], axis=1, keepdims=True)
        out_ref[...] = jnp.where(lane == 0, lse, picked)


def head_block(x, w, tgt, tt=1024):
    t, v = x.shape[0], w.shape[1]
    tgt = jnp.broadcast_to(jnp.where((tgt >= 0) & (tgt < v), tgt, -1)[:, None], (t, 128))
    out = pl.pallas_call(
        functools.partial(head_kernel, v),
        out_shape=jax.ShapeDtypeStruct((t, 128), F32),
        grid=(t // tt, pl.cdiv(v, VT)),
        in_specs=[
            pl.BlockSpec((tt, D), lambda i, j: (i, 0)), pl.BlockSpec((D, VT), lambda i, j: (0, j)),
            pl.BlockSpec((tt, 128), lambda i, j: (i, 0)),
        ],
        out_specs=pl.BlockSpec((tt, 128), lambda i, j: (i, 0)),
        scratch_shapes=[pltpu.VMEM((tt, 128), F32)] * 3,
        compiler_params=pltpu.CompilerParams(vmem_limit_bytes=VMEM_LIMIT),
        cost_estimate=pl.CostEstimate(flops=2 * t * D * v, bytes_accessed=2 * D * (v * t // tt + t), transcendentals=t * v),
        name="head",
    )(x, w, tgt)
    return out[:, 0], out[:, 1]


def rope_tables():
    half = HEAD_DIM // 2
    inv_freq = ROPE_BASE ** (-jnp.arange(half, dtype=F32) / half)
    angles = jnp.arange(SEQ, dtype=F32)[:, None] * inv_freq[None, :]
    cos, sin = jnp.cos(angles), jnp.sin(angles)
    cos = jnp.tile(jnp.concatenate([cos, cos] * 2, axis=1), (TB // SEQ, 1))
    sin = jnp.tile(jnp.concatenate([-sin, sin] * 2, axis=1), (TB // SEQ, 1))
    return cos, sin


def running_count(flags):
    n = flags.shape[-1]
    upper = (jnp.arange(n)[:, None] <= jnp.arange(n)[None, :]).astype(BF16)
    return dot(flags.astype(BF16), upper).astype(jnp.int32)


def embed_rows(table, toks, me, size, cap, perms, axis, order):
    vocab, t = table.shape[0], toks.shape[1]
    local = toks - me * vocab
    owned = (local >= 0) & (local < vocab)
    rank = running_count(owned) - 1
    peers = jnp.bitwise_xor(me, jnp.arange(size))
    wanted = (toks[0] // vocab)[None, :] == peers[:, None]
    my_rank = running_count(wanted) - 1

    def one_round(r):
        slots = r * cap + jnp.arange(cap)
        hit = owned[:, None, :] & (rank[:, None, :] == slots[None, :, None])
        idx = jnp.sum(jnp.where(hit, local[:, None, :], 0), axis=2)
        got = [jnp.take(table, idx[0], axis=0)]
        rows = jnp.take(table, idx[1:].reshape(-1), axis=0).reshape(size - 1, cap, D)
        for k in range(1, size):
            got.append(lax.ppermute(rows[k - 1], axis, perms[k]))
        pick = wanted[:, :, None] & (my_rank[:, :, None] == slots[None, None, :])
        pick = jnp.swapaxes(pick, 0, 1).reshape(t, size * cap).astype(BF16)
        return dot(pick, jnp.concatenate(got, axis=0))

    counts = jnp.sum((order[:, None, :] // vocab) == jnp.arange(32000 // vocab)[None, :, None], axis=2)
    rounds = (jnp.max(counts) + cap - 1) // cap
    rows = one_round(0)
    rows = lax.fori_loop(1, rounds, lambda r, acc: acc + one_round(r), rows)
    return rows.astype(BF16)


def advantages(rewards, groups):
    same = (groups[:, None] == groups[None, :]).astype(F32)
    counts = jnp.sum(same, axis=1)
    means = jnp.sum(same * rewards[None, :], axis=1) / counts
    centred = rewards - means
    spread = jnp.sqrt(jnp.sum(same * (centred * centred)[None, :], axis=1) / counts)
    return centred / (spread + ADV_EPS)


def row_losses(logp, logp_ref, logp_old, weights, advantage):
    log_gap = logp_ref - logp
    kl_est = jnp.exp(log_gap) - log_gap - 1.0
    ratio = jnp.exp(logp - logp_old)
    adv_row = advantage[:, None]
    surrogate = jnp.minimum(ratio * adv_row, jnp.clip(ratio, 1.0 - CLIP_EPS, 1.0 + CLIP_EPS) * adv_row)
    per_token = -surrogate + BETA * kl_est
    return jnp.sum(per_token * weights, axis=1) / jnp.sum(weights, axis=1)


def solution(mesh):
    both = ('rep', 'fsdp')
    row_spec = P(both, None)
    n_dev = mesh.shape['rep'] * mesh.shape['fsdp']
    swap = [(0, 1), (1, 0)]
    xors = [[(d, d ^ k) for d in range(n_dev)] for k in range(n_dev)]

    def weight_specs(axes):
        return [P(None, axes, None)] * 5 + [P(None, axes), P(axes, None), P(axes, None)]

    in_specs = tuple([row_spec, row_spec, row_spec, P(both), P(both)] + weight_specs('fsdp') + weight_specs(both))
    out_specs = (P(), row_spec, row_spec)

    def device_step(tokens, resp_mask, logp_old, rewards, group_id, *weights):
        p_q, p_kv, p_o, p_gu, p_dn, p_norms, p_embed, p_head = weights[:8]
        r_q, r_kv, r_o, r_gu, r_dn, r_norms, r_embed, r_head = weights[8:]
        core = lax.axis_index('fsdp')
        me = lax.axis_index('rep') * 2 + core
        core_arr = core.astype(jnp.int32).reshape(1)
        rows = tokens.shape[0]
        t = rows * SEQ
        layers = p_q.shape[0]
        tabs = rope_tables()

        small = jnp.concatenate([x.astype(F32).reshape(-1) for x in (tokens, resp_mask, logp_old, rewards, group_id, p_norms, r_norms)])
        size = -small.size % 1024
        small = lax.all_gather(jnp.pad(small, (0, size)).reshape(-1, 128), both).reshape(n_dev, -1)
        cuts, at = [], 0
        for x in (tokens, resp_mask, logp_old, rewards, group_id, p_norms, r_norms):
            cuts.append(small[:, at:at + x.size].reshape((n_dev,) + x.shape))
            at += x.size
        tok_all = cuts[0].astype(jnp.int32).reshape(n_dev, t)
        mask_all, old_all = (x.reshape(n_dev * rows, SEQ) for x in cuts[1:3])
        reward_all = cuts[3].reshape(-1)
        group_all = cuts[4].reshape(-1)
        p_gains = jnp.swapaxes(cuts[5][:2], 0, 1).reshape(2 * layers + 1, 1, D)
        r_gains = jnp.swapaxes(cuts[6], 0, 1).reshape(2 * layers + 1, 1, D)
        tgt_all = jnp.roll(tok_all.reshape(n_dev * rows, SEQ), -1, axis=1).reshape(n_dev, t)

        p_qkv = jnp.concatenate([p_q, p_kv], axis=2)
        p_qkv, p_wo, p_wgu, p_wdn = ([w, lax.ppermute(w, 'fsdp', swap)] for w in (p_qkv, p_o, p_gu, jnp.swapaxes(p_dn, 1, 2)))
        p_head, r_head = p_head.T, r_head.T

        r_full = []
        for layer in range(layers):
            att = lax.all_gather(jnp.concatenate([r_q[layer], r_kv[layer]], axis=1), both, axis=0, tiled=True)
            r_full.append([att] + [lax.all_gather(w[layer], both, axis=0, tiled=True) for w in (r_o, r_gu, r_dn)])

        chip_tok = tok_all[jnp.bitwise_xor(me, jnp.arange(2))]
        h = embed_rows(p_embed, chip_tok, core, 2, 640, [None, swap], 'fsdp', tok_all)

        def policy_layer(h, layer):
            h = attention_block(h, p_gains[2 * layer], tabs, p_qkv, p_wo, layer, core_arr)
            return mlp_block(h, p_gains[2 * layer + 1], p_gains[2 * layers], p_wgu, p_wdn, layer, layer == layers - 1, core_arr)

        def ref_layer(h, layer):
            w_qkv, w_o, w_gu, w_dn = r_full[layer]
            h = attention_block(h, r_gains[2 * layer], tabs, [w_qkv], [w_o], None, core_arr)
            return mlp_block(h, r_gains[2 * layer + 1], r_gains[2 * layers], [w_gu], [w_dn], None, layer == layers - 1, core_arr)

        h = policy_layer(h, 0)
        order, h = lax.optimization_barrier((tok_all[jnp.bitwise_xor(me, jnp.arange(n_dev))], h))
        h_ref = embed_rows(r_embed, order, me, n_dev, 192, xors, both, tok_all)
        h, h_ref = lax.optimization_barrier((h, h_ref))
        x = policy_layer(h, 1)
        x_peer = lax.ppermute(x, 'fsdp', swap)
        tgt_own = tgt_all[me] - core * p_head.shape[1]
        tgt_peer = tgt_all[jnp.bitwise_xor(me, 1)] - core * p_head.shape[1]

        h_ref, x = lax.optimization_barrier((h_ref, x))
        h_ref = ref_layer(h_ref, 0)
        x, h_ref = lax.optimization_barrier((x, h_ref))
        own = head_block(x, p_head, tgt_own)
        h_ref, own = lax.optimization_barrier((h_ref, own))
        x_ref = ref_layer(h_ref, 1)
        x_peer, x_ref = lax.optimization_barrier((x_peer, x_ref))
        x_all = [lax.all_gather(x_ref[at:at + t // 2], both, axis=0, tiled=True) for at in (0, t // 2)]
        peer = head_block(x_peer, p_head, tgt_peer)

        x_all[0], peer = lax.optimization_barrier((x_all[0], peer))
        parts = [jnp.stack(own + peer)]
        for half in range(2):
            tgt = tgt_all[:, half * (t // 2):(half + 1) * (t // 2)].reshape(-1) - me * r_head.shape[1]
            parts += [out.reshape(n_dev // 2, t) for out in head_block(x_all[half], r_head, tgt)]
        parts = lax.all_gather(jnp.concatenate(parts, axis=0), both)
        p_part = parts[:, :4]
        r_part = parts[:, 4:].reshape(n_dev, 2, 2, n_dev, t // 2)
        r_part = jnp.transpose(r_part, (2, 0, 3, 1, 4)).reshape(2, n_dev, n_dev, t)

        def finish(lse, picked):
            next_lp = (jnp.sum(picked, axis=0) - jax.nn.logsumexp(lse, axis=0)).reshape(n_dev * rows, SEQ)
            return jnp.where(jnp.arange(SEQ)[None, :] == 0, 0.0, jnp.roll(next_lp, 1, axis=1))

        logp_ref = finish(r_part[0], r_part[1])
        by_peer = p_part.reshape(n_dev // 2, 2, 4, t)[:, ::-1].reshape(n_dev, 4, t)
        lse = jnp.stack([p_part[:, 0], by_peer[:, 2]])
        picked = jnp.stack([p_part[:, 1], by_peer[:, 3]])
        logp = finish(lse, picked)
        row_part = row_losses(logp, logp_ref, old_all, mask_all, advantages(reward_all, group_all))
        loss = jnp.sum(row_part) / row_part.shape[0]
        return loss, lax.dynamic_slice_in_dim(logp, me * rows, rows), lax.dynamic_slice_in_dim(logp_ref, me * rows, rows)

    return jax.shard_map(device_step, mesh=mesh, in_specs=in_specs, out_specs=out_specs, check_vma=False)
```

time: 2710 us -> 1670 us (0.62)
  matrix products: 758 us -> 69 us
  Pallas kernels: 0 us -> 679 us
  waiting for transfers between devices: 828 us -> 272 us
  local copies, waits for them, and re-layouts: 829 us -> 413 us
  other arithmetic: 174 us -> 64.5 us
  starting transfers between devices: 0.95 us -> 69.3 us
    all_gather x24 -> x10, waiting for transfers between devices: 820 us -> 0.13 us  [the longest x6 0.08 us: device_step(): lax.all_gather(w[layer], both, axis=0, tiled=True)]
    pallas_call x0 -> x12, Pallas kernels: none -> 679 us  [the longest x4 289 us: head_block(): pl.pallas_call(functools.partial(head_kernel, v), out_shape=jax.ShapeDtyp...]
    dot_general x26 -> x11, matrix products: 688 us -> 69 us  [dot(): lax.dot_general(lhs, rhs, (((1,), (0,)), ((), ())), preferred_element_typ...]
    ppermute x0 -> x42, waiting for transfers between devices: none -> 270 us  [the longest x37 270 us: one_round(): got.append(lax.ppermute(rows[k - 1], axis, perms[k]))]
    all_gather x4 -> x0, local copies, waits for them, and re-layouts: 213 us -> none  [the longest x1 127 us: run_model(): table = lax.all_gather(embed, axes, axis=0, tiled=True)]
    unnamed x133 -> x65, local copies, waits for them, and re-layouts: 245 us -> 87.4 us
    reshape x12 -> x19, local copies, waits for them, and re-layouts: 121 us -> 1.49 us  [the longest x10 0.76 us: one_round(): idx[1:].reshape(-1)]
    gather x10 -> x16, local copies, waits for them, and re-layouts: 73.4 us -> 186 us  [the longest x7 115 us: one_round(): jnp.take(table, idx[1:].reshape(-1), axis=0).reshape(size - 1, cap, D)]
  transfers between devices with their start and end apart: 24 -> 52, of which waited for: 3 -> 19; matrix products, arithmetic and copies ran while one was open for 56% -> 32% of each run, Pallas kernels for 0% -> 37%
where the time goes in v1:
time: 1670 us; the launch traced here: 1650 us
  Pallas kernels  679 us (41%)
  local copies, waits for them, and re-layouts  413 us (25%)
  waiting for transfers between devices  272 us (16%)
  starting transfers between devices  69.3 us (4%)
  matrix products  69 us (4%)
  blocking collectives  67.6 us (4%)
  other arithmetic  64.5 us (4%)
  between operations  18.8 us (1%)
    pallas_call x4, Pallas kernels, head_block(): pl.pallas_call(functools.partial(head_kernel, v), out_shape=jax.ShapeDtyp...  289 us
    ppermute x37, waiting for transfers between devices, one_round(): got.append(lax.ppermute(rows[k - 1], axis, perms[k]))  270 us
    pallas_call x4, Pallas kernels, mlp_block(): pl.pallas_call(functools.partial(mlp_kernel, n, layer, last), out_shape=j...  247 us
    pallas_call x4, Pallas kernels, attention_block(): pl.pallas_call(functools.partial(attn_kernel, n, layer), out_shape=jax.Sh...  144 us
    gather x7, local copies, waits for them, and re-layouts, one_round(): jnp.take(table, idx[1:].reshape(-1), axis=0).reshape(size - 1, cap, D)  115 us
    unnamed x65, local copies, waits for them, and re-layouts  87.4 us
    gather x7, local copies, waits for them, and re-layouts, one_round(): got = [jnp.take(table, idx[0], axis=0)]  70.1 us
    dot_general x11, matrix products, dot(): lax.dot_general(lhs, rhs, (((1,), (0,)), ((), ())), preferred_element_typ...  69 us
  transfers between devices with their start and end apart: 52, of which 19 were waited for; matrix products, arithmetic and copies ran while one was open for 32% of the time, Pallas kernels for 37%

profile of v1, /device:TPU:0, one launch (start us, length us, event | category | flops | bytes accessed | tf_op | source)
XLA Modules:
  0.0 1654.6 jit_solution(16613848563105757856)
XLA Ops:
  26.8 54.3 %all_gather.39 = f32[8,64,128]{2,1,0:T(8,128)S(1)} all-gather(f32[1,64,128]{2,1,0:T(8,128)S(1)} %pad_bitcast_fusion), channel_id=1, replica_groups=mesh['rep'=4,'fsdp'=2] {'rep','fsdp'}, dimensions={0}, use_global_device_ids=true | all-gather | bytes 294912 | tf_op jit(solution)/shard_map/all_gather | solution.py:413
  81.3 66.4 %copy.95 = bf16[16000,1600]{1,0:T(8,128)(2,1)} copy(bf16[16000,1600]{0,1:T(8,128)(2,1)} %param.40) | data formatting | bytes 102400000 | tf_op args[11]
  202.6 17.8 %copy.101 = bf16[4000,1600]{1,0:T(8,128)(2,1)} copy(bf16[4000,1600]{0,1:T(8,128)(2,1)} %param.48) | data formatting | bytes 25600000 | tf_op args[19]
  254.4 65.4 %while.22 = (s32[]{:T(128)}, f32[1024,1600]{0,1:T(8,128)}, s32[]{:T(128)}, s32[2,1024]{1,0:T(2,128)S(1)}, pred[2,1024]{1,0:T(4,128)(4,1)S(1)}, /*index=5*/s32[2,...) while((s32[]{:T(128)}, f32[1024,1600]{0,1:T(8,128)}, ...), condition=%wide.region_5.8_spmd.clone, body=%wide.region_3.7_spmd.clone.sunk | while | flops 4214061824 | bytes 52707508 | solution.py:364
  256.1 17.1 %gather_fusion = bf16[640,1600]{1,0:T(8,128)(2,1)} fusion(bf16[16000,1600]{1,0:T(8,128)(2,1)} %get-tuple-element.591, s32[1024]{0:T(1024)S(1)} %pad_clamp_fusion.14), kind=kCustom, calls=%fused_computation.5.clone.clone.1 | custom fusion | bytes 4098560 | tf_op jit(solution)/shard_map/while/body/jit(_take)/gather | solution.py:354
  287.1 17.7 %gather_fusion.1 = bf16[640,1600]{1,0:T(8,128)(2,1)S(1)} fusion(bf16[16000,1600]{1,0:T(8,128)(2,1)} %get-tuple-element.591, s32[1024]{0:T(1024)S(1)} %pad_clamp_fusion.15), kind=kCustom, calls=%fused_computation.1.clone.clone.1 | custom fusion | bytes 4098560 | tf_op jit(solution)/shard_map/while/body/jit(_take)/gather | solution.py:353
  328.1 35.9 %attn.4.h_ref = bf16[1024,1600]{1,0:T(8,128)(2,1)} custom-call(s32[1]{0:T(128)} %bitcast.2.core_ref, bf16[1024,1600]{1,0:T(8,128)(2,1)} %copy.100.h_ref, f32[1,1600]{1,0:T(1,128)} %squeeze.111.gain_ref, f32[256,128]{1,0:T(8,128)} %bitcast.166, f32[256,128]{1,0:T(8,128)} %bitcast.162, bf16[2,800,2240]{2,1,0:T(8,128)(2,1)} %pad_maximum_fusion.refs_0_, ...), custom_call_target="tpu_custom_call" | custom-call | flops 12582912000 | bytes 12288000 | tf_op jit(solution)/shard_map/attn/pallas_call | solution.py:145
  364.0 61.7 %mlp.4.h_ref = bf16[1024,1600]{1,0:T(8,128)(2,1)} custom-call(s32[1]{0:T(128)} %bitcast.2.core_ref, bf16[1024,1600]{1,0:T(8,128)(2,1)} %attn.4.h_ref, f32[1,1600]{1,0:T(1,128)} %squeeze.112.gain_ref, f32[1,1600]{1,0:T(1,128)} %squeeze.113.fin_ref, bf16[2,800,8704]{2,1,0:T(8,128)(2,1)} %refs_0_.3, bf16[2,800,8704]{2,1,0:T(8,128)(2,1)} %collective-permute-done.11.refs_1_, ...), custom_call_target="tpu_custom_call" | custom-call | flops 42781900800 | bytes 41779200 | tf_op jit(solution)/shard_map/mlp/pallas_call | solution.py:256
  427.6 17.3 %gather_fusion.7 = bf16[1344,1600]{1,0:T(8,128)(2,1)} fusion(bf16[4000,1600]{1,0:T(8,128)(2,1)} %copy.101, s32[2048]{0:T(1024)S(1)} %pad_clamp_fusion.4), kind=kCustom, calls=%fused_computation.9 | custom fusion | bytes 8606976 | tf_op jit(solution)/shard_map/jit(_take)/gather | solution.py:354
  489.0 24.5 %collective-permute-done.15 = bf16[192,1600]{1,0:T(8,128)(2,1)S(1)} collective-permute-done((bf16[192,1600]{1,0:T(8,128)(2,1)}, bf16[192,1600]{1,0:T(8,128)(2,1)S(1)}, u32[]{:S(2)}, u32[]{:S(2)}) %collective-permute-start.15) | collective-permute-done | bytes 614432 | tf_op jit(solution)/shard_map/ppermute | solution.py:356
  541.0 17.5 %collective-permute-done.19 = bf16[192,1600]{1,0:T(8,128)(2,1)S(1)} collective-permute-done((bf16[192,1600]{1,0:T(8,128)(2,1)S(1)}, bf16[192,1600]{1,0:T(8,128)(2,1)S(1)}, u32[]{:S(2)}, u32[]{:S(2)}) %collective-permute-start.19) | collective-permute-done | bytes 614432 | tf_op jit(solution)/shard_map/ppermute | solution.py:356
  566.0 433.1 %while.23 = (s32[]{:T(128)}, f32[1024,1600]{0,1:T(8,128)}, s32[]{:T(128)}, s32[8,1024]{1,0:T(8,128)S(1)}, pred[8,1024]{1,0:T(8,128)(4,1)S(1)}, /*index=5*/s32[8,...) while((s32[]{:T(128)}, f32[1024,1600]{0,1:T(8,128)}, ...), condition=%wide.region_11.14_spmd.clone, body=%wide.region_9.13_spmd.clone.sunk | while | flops 5046721536 | bytes 75821040 | solution.py:364
  567.6 17.1 %gather_fusion.3 = bf16[1344,1600]{1,0:T(8,128)(2,1)} fusion(bf16[4000,1600]{1,0:T(8,128)(2,1)} %get-tuple-element.627, s32[2048]{0:T(1024)S(1)} %pad_clamp_fusion.17), kind=kCustom, calls=%fused_computation.3.clone.clone.1 | custom fusion | bytes 8606976 | tf_op jit(solution)/shard_map/while/body/jit(_take)/gather | solution.py:354
  623.6 23.5 %collective-permute-done.3 = bf16[192,1600]{1,0:T(8,128)(2,1)} collective-permute-done((bf16[192,1600]{1,0:T(8,128)(2,1)}, bf16[192,1600]{1,0:T(8,128)(2,1)}, u32[]{:S(2)}, u32[]{:S(2)}) %collective-permute-start.3) | collective-permute-done | bytes 614432 | tf_op jit(solution)/shard_map/while/body/ppermute | solution.py:356
  654.9 22.7 %collective-permute-done.6 = bf16[192,1600]{1,0:T(8,128)(2,1)S(1)} collective-permute-done((bf16[192,1600]{1,0:T(8,128)(2,1)S(1)}, bf16[192,1600]{1,0:T(8,128)(2,1)S(1)}, u32[]{:S(2)}, u32[]{:S(2)}) %collective-permute-start.6) | collective-permute-done | bytes 614432 | tf_op jit(solution)/shard_map/while/body/ppermute | solution.py:356
  678.5 17.7 %collective-permute-done.7 = bf16[192,1600]{1,0:T(8,128)(2,1)S(1)} collective-permute-done((bf16[192,1600]{1,0:T(8,128)(2,1)S(1)}, bf16[192,1600]{1,0:T(8,128)(2,1)S(1)}, u32[]{:S(2)}, u32[]{:S(2)}) %collective-permute-start.7) | collective-permute-done | bytes 614432 | tf_op jit(solution)/shard_map/while/body/ppermute | solution.py:356
  709.5 17.1 %gather_fusion.3 = bf16[1344,1600]{1,0:T(8,128)(2,1)} fusion(bf16[4000,1600]{1,0:T(8,128)(2,1)} %get-tuple-element.627, s32[2048]{0:T(1024)S(1)} %pad_clamp_fusion.17), kind=kCustom, calls=%fused_computation.3.clone.clone.1 | custom fusion | bytes 8606976 | tf_op jit(solution)/shard_map/while/body/jit(_take)/gather | solution.py:354
  764.5 25.8 %collective-permute-done.5 = bf16[192,1600]{1,0:T(8,128)(2,1)} collective-permute-done((bf16[192,1600]{1,0:T(8,128)(2,1)S(1)}, bf16[192,1600]{1,0:T(8,128)(2,1)}, u32[]{:S(2)}, u32[]{:S(2)}) %collective-permute-start.5) | collective-permute-done | bytes 614432 | tf_op jit(solution)/shard_map/while/body/ppermute | solution.py:356
  806.5 17.1 %gather_fusion.3 = bf16[1344,1600]{1,0:T(8,128)(2,1)} fusion(bf16[4000,1600]{1,0:T(8,128)(2,1)} %get-tuple-element.627, s32[2048]{0:T(1024)S(1)} %pad_clamp_fusion.17), kind=kCustom, calls=%fused_computation.3.clone.clone.1 | custom fusion | bytes 8606976 | tf_op jit(solution)/shard_map/while/body/jit(_take)/gather | solution.py:354
  861.6 25.5 %collective-permute-done.5 = bf16[192,1600]{1,0:T(8,128)(2,1)} collective-permute-done((bf16[192,1600]{1,0:T(8,128)(2,1)S(1)}, bf16[192,1600]{1,0:T(8,128)(2,1)}, u32[]{:S(2)}, u32[]{:S(2)}) %collective-permute-start.5) | collective-permute-done | bytes 614432 | tf_op jit(solution)/shard_map/while/body/ppermute | solution.py:356
  903.4 17.1 %gather_fusion.3 = bf16[1344,1600]{1,0:T(8,128)(2,1)} fusion(bf16[4000,1600]{1,0:T(8,128)(2,1)} %get-tuple-element.627, s32[2048]{0:T(1024)S(1)} %pad_clamp_fusion.17), kind=kCustom, calls=%fused_computation.3.clone.clone.1 | custom fusion | bytes 8606976 | tf_op jit(solution)/shard_map/while/body/jit(_take)/gather | solution.py:354
  958.4 25.7 %collective-permute-done.5 = bf16[192,1600]{1,0:T(8,128)(2,1)} collective-permute-done((bf16[192,1600]{1,0:T(8,128)(2,1)S(1)}, bf16[192,1600]{1,0:T(8,128)(2,1)}, u32[]{:S(2)}, u32[]{:S(2)}) %collective-permute-start.5) | collective-permute-done | bytes 614432 | tf_op jit(solution)/shard_map/while/body/ppermute | solution.py:356
  1005.3 35.9 %attn.5.h_ref = bf16[1024,1600]{1,0:T(8,128)(2,1)} custom-call(s32[1]{0:T(128)} %bitcast.2.core_ref, bf16[1024,1600]{1,0:T(8,128)(2,1)} %mlp.4.h_ref, f32[1,1600]{1,0:T(1,128)} %squeeze.116.gain_ref, f32[256,128]{1,0:T(8,128)} %bitcast.167, f32[256,128]{1,0:T(8,128)} %bitcast.163, bf16[2,800,2240]{2,1,0:T(8,128)(2,1)} %pad_maximum_fusion.refs_0_, ...), custom_call_target="tpu_custom_call" | custom-call | flops 12582912000 | bytes 12288000 | tf_op jit(solution)/shard_map/attn/pallas_call | solution.py:145
  1041.2 62.3 %mlp.5.x_ref = bf16[1024,1600]{1,0:T(8,128)(2,1)} custom-call(s32[1]{0:T(128)} %bitcast.2.core_ref, bf16[1024,1600]{1,0:T(8,128)(2,1)} %attn.5.h_ref, f32[1,1600]{1,0:T(1,128)} %squeeze.117.gain_ref, f32[1,1600]{1,0:T(1,128)} %squeeze.113.fin_ref, bf16[2,800,8704]{2,1,0:T(8,128)(2,1)} %refs_0_.3, bf16[2,800,8704]{2,1,0:T(8,128)(2,1)} %collective-permute-done.11.refs_1_, ...), custom_call_target="tpu_custom_call" | custom-call | flops 42781900800 | bytes 41779200 | tf_op jit(solution)/shard_map/mlp/pallas_call | solution.py:256
  1109.3 35.8 %attn.6.h_ref = bf16[1024,1600]{1,0:T(8,128)(2,1)} custom-call(s32[1]{0:T(128)} %bitcast.2.core_ref, bf16[1024,1600]{1,0:T(8,128)(2,1)} %copy.104.h_ref, f32[1,1600]{1,0:T(1,128)} %squeeze.118.gain_ref, f32[256,128]{1,0:T(8,128)} %bitcast.168, f32[256,128]{1,0:T(8,128)} %bitcast.164, bf16[1600,2240]{1,0:T(8,128)(2,1)} %all-gather.19.cloned.1.call-done.refs_0_, ...), custom_call_target="tpu_custom_call" | custom-call | flops 12582912000 | bytes 12288000 | tf_op jit(solution)/shard_map/attn/pallas_call | solution.py:145
  1145.2 60.9 %mlp.6.h_ref = bf16[1024,1600]{1,0:T(8,128)(2,1)} custom-call(s32[1]{0:T(128)} %bitcast.2.core_ref, bf16[1024,1600]{1,0:T(8,128)(2,1)} %attn.6.h_ref, f32[1,1600]{1,0:T(1,128)} %squeeze.122.gain_ref, f32[1,1600]{1,0:T(1,128)} %squeeze.123.fin_ref, bf16[1600,8704]{1,0:T(8,128)(2,1)} %bitcast.183, bf16[4352,1600]{1,0:T(8,128)(2,1)} %bitcast.185), custom_call_target="tpu_custom_call" | custom-call | flops 42781900800 | bytes 41779200 | tf_op jit(solution)/shard_map/mlp/pallas_call | solution.py:256
  1207.1 71.3 %head.4 = f32[1024,128]{1,0:T(8,128)} custom-call(bf16[1024,1600]{1,0:T(8,128)(2,1)} %mlp.5.x_ref, bf16[1600,16000]{1,0:T(8,128)(2,1)} %bitcast.181, s32[1024,128]{1,0:T(8,128)} %broadcast_in_dim.221.tgt_ref), custom_call_target="tpu_custom_call" | custom-call | flops 52428800000 | bytes 54476800 | tf_op jit(solution)/shard_map/head/pallas_call | solution.py:307
  1280.8 36.2 %attn.7.h_ref = bf16[1024,1600]{1,0:T(8,128)(2,1)} custom-call(s32[1]{0:T(128)} %bitcast.2.core_ref, bf16[1024,1600]{1,0:T(8,128)(2,1)} %mlp.6.h_ref, f32[1,1600]{1,0:T(1,128)} %squeeze.128.gain_ref, f32[256,128]{1,0:T(8,128)} %bitcast.169, f32[256,128]{1,0:T(8,128)} %bitcast.165, bf16[1600,2240]{1,0:T(8,128)(2,1)} %all-gather.21.cloned.1.call-done.refs_0_, ...), custom_call_target="tpu_custom_call" | custom-call | flops 12582912000 | bytes 12288000 | tf_op jit(solution)/shard_map/attn/pallas_call | solution.py:145
  1317.1 61.8 %mlp.7 = bf16[1024,1600]{1,0:T(8,128)(2,1)} custom-call(s32[1]{0:T(128)} %bitcast.2.core_ref, bf16[1024,1600]{1,0:T(8,128)(2,1)} %attn.7.h_ref, f32[1,1600]{1,0:T(1,128)} %squeeze.132.gain_ref, f32[1,1600]{1,0:T(1,128)} %squeeze.123.fin_ref, bf16[1600,8704]{1,0:T(8,128)(2,1)} %bitcast.184, bf16[4352,1600]{1,0:T(8,128)(2,1)} %bitcast.186), custom_call_target="tpu_custom_call" | custom-call | flops 42781900800 | bytes 41779200 | tf_op jit(solution)/shard_map/mlp/pallas_call | solution.py:256
  1394.8 71.4 %head.5 = f32[1024,128]{1,0:T(8,128)} custom-call(bf16[1024,1600]{1,0:T(8,128)(2,1)} %copy.106.x_ref, bf16[1600,16000]{1,0:T(8,128)(2,1)} %bitcast.182, s32[1024,128]{1,0:T(8,128)} %broadcast_in_dim.222.tgt_ref), custom_call_target="tpu_custom_call" | custom-call | flops 52428800000 | bytes 54476800 | tf_op jit(solution)/shard_map/head/pallas_call | solution.py:307
  1470.9 73.0 %head.6 = f32[4096,128]{1,0:T(8,128)} custom-call(bf16[4096,1600]{1,0:T(8,128)(2,1)} %all-gather.23.cloned.1.call-done.x_ref, bf16[1600,4000]{1,0:T(8,128)(2,1)} %bitcast.190, s32[4096,128]{1,0:T(8,128)} %broadcast_in_dim.224.tgt_ref), custom_call_target="tpu_custom_call" | custom-call | flops 52428800000 | bytes 64307200 | tf_op jit(solution)/shard_map/head/pallas_call | solution.py:307
  1550.9 73.1 %head.7 = f32[4096,128]{1,0:T(8,128)} custom-call(bf16[4096,1600]{1,0:T(8,128)(2,1)} %all-gather.25.cloned.1.call-done.x_ref, bf16[1600,4000]{1,0:T(8,128)(2,1)} %bitcast.191, s32[4096,128]{1,0:T(8,128)} %broadcast_in_dim.225.tgt_ref), custom_call_target="tpu_custom_call" | custom-call | flops 52428800000 | bytes 64307200 | tf_op jit(solution)/shard_map/head/pallas_call | solution.py:307
  (489 shorter events, 513.1 us)
Async XLA Ops:
  7.2 1102.1 %all-gather.27.cloned.1.call-start = ((), (), s32[]{:S(2)}) async-start(), calls=%async_computation.4 | async-start | bytes 5990400 | tf_op jit(solution)/shard_map/all_gather | solution.py:433
  9.8 1099.5 %all-gather.19.cloned.1.call-start = ((), (), s32[]{:S(2)}) async-start(), calls=%async_computation | async-start | bytes 8294400 | tf_op jit(solution)/shard_map/all_gather | solution.py:432
  12.2 1133.0 %all-gather.31.cloned.1.call-start = ((), (), s32[]{:S(2)}) async-start(), calls=%async_computation.6 | async-start | bytes 16293888 | tf_op jit(solution)/shard_map/all_gather | solution.py:433
  16.4 1128.8 %all-gather.29.cloned.1.call-start = ((), (), s32[]{:S(2)}) async-start(), calls=%async_computation.5 | async-start | bytes 31334400 | tf_op jit(solution)/shard_map/all_gather | solution.py:433
  22.8 1258.0 %all-gather.33.cloned.1.call-start = ((), (), s32[]{:S(2)}) async-start(), calls=%async_computation.7 | async-start | bytes 5990400 | tf_op jit(solution)/shard_map/all_gather | solution.py:433
  23.4 1257.4 %all-gather.21.cloned.1.call-start = ((), (), s32[]{:S(2)}) async-start(), calls=%async_computation.1 | async-start | bytes 8294400 | tf_op jit(solution)/shard_map/all_gather | solution.py:432
  24.6 1292.4 %all-gather.37.cloned.1.call-start = ((), (), s32[]{:S(2)}) async-start(), calls=%async_computation.9 | async-start | bytes 16293888 | tf_op jit(solution)/shard_map/all_gather | solution.py:433
  25.3 1291.7 %all-gather.35.cloned.1.call-start = ((), (), s32[]{:S(2)}) async-start(), calls=%async_computation.8 | async-start | bytes 31334400 | tf_op jit(solution)/shard_map/all_gather | solution.py:433
  25.4 338.6 %collective-permute-start.11 = (bf16[2,800,8704]{2,1,0:T(8,128)(2,1)}, bf16[2,800,8704]{2,1,0:T(8,128)(2,1)}, u32[]{:S(2)}, u32[]{:S(2)}) collective-permute-start(bf16[2,800,8704]{2,1,0:T(8,128)(2,1)} %refs_0_.3), channel_id=1, source_target_pairs={{0,1},{1,0},{2,3},{3,2},{4,5},{5,4},{6,7},{7,6}} | collective-permute-start | bytes 83558408 | tf_op jit(solution)/shard_map/ppermute | solution.py:427
  166.6 76.6 %collective-permute-start.8 = (bf16[640,1600]{0,1:T(8,128)(2,1)}, bf16[640,1600]{0,1:T(8,128)(2,1)}, u32[]{:S(2)}, u32[]{:S(2)}) collective-permute-start(bf16[640,1600]{0,1:T(8,128)(2,1)} %copy.97), channel_id=1, source_target_pairs={{0,1},{1,0},{2,3},{3,2},{4,5},{5,4},{6,7},{7,6}} | collective-permute-start | bytes 6144008 | tf_op jit(solution)/shard_map/ppermute | solution.py:356
  183.8 143.0 %collective-permute-start.9 = (bf16[2,800,2240]{2,1,0:T(8,128)(2,1)}, bf16[2,800,2240]{2,1,0:T(8,128)(2,1)}, u32[]{:S(2)}, u32[]{:S(2)}) collective-permute-start(bf16[2,800,2240]{2,1,0:T(8,128)(2,1)} %pad_maximum_fusion.refs_0_), channel_id=1, source_target_pairs={{0,1},{1,0},{2,3},{3,2},{4,5},{5,4},{6,7},{7,6}} | collective-permute-start | bytes 21504008 | tf_op jit(solution)/shard_map/ppermute | solution.py:427
  183.8 142.9 %collective-permute-start.10 = (bf16[2,800,1600]{2,1,0:T(8,128)(2,1)}, bf16[2,800,1600]{2,1,0:T(8,128)(2,1)}, u32[]{:S(2)}, u32[]{:S(2)}) collective-permute-start(bf16[2,800,1600]{2,1,0:T(8,128)(2,1)} %refs_2_.3), channel_id=1, source_target_pairs={{0,1},{1,0},{2,3},{3,2},{4,5},{5,4},{6,7},{7,6}} | collective-permute-start | bytes 15360008 | tf_op jit(solution)/shard_map/ppermute | solution.py:427
  184.3 1283.6 %all-gather.23.cloned.1.call-start = ((), (), s32[]{:S(2)}) async-start(), calls=%async_computation.2 | async-start | bytes 15335424 | tf_op jit(solution)/shard_map/all_gather | solution.py:463
  231.4 132.6 %collective-permute-start.12 = (bf16[2,1600,2176]{2,1,0:T(8,128)(2,1)}, bf16[2,1600,2176]{2,1,0:T(8,128)(2,1)}, u32[]{:S(2)}, u32[]{:S(2)}) collective-permute-start(bf16[2,1600,2176]{2,1,0:T(8,128)(2,1)} %bitcast.187), channel_id=1, source_target_pairs={{0,1},{1,0},{2,3},{3,2},{4,5},{5,4},{6,7},{7,6}} | collective-permute-start | bytes 41779208 | tf_op jit(solution)/shard_map/ppermute | solution.py:427
  465.8 47.7 %collective-permute-start.15 = (bf16[192,1600]{1,0:T(8,128)(2,1)}, bf16[192,1600]{1,0:T(8,128)(2,1)S(1)}, u32[]{:S(2)}, u32[]{:S(2)}) collective-permute-start(bf16[192,1600]{1,0:T(8,128)(2,1)} %get-tuple-element.380), channel_id=1, source_target_pairs={{0,3},{1,2},{2,1},{3,0},{4,7},{5,6},{6,5},{7,4}} | collective-permute-start | bytes 1843208 | tf_op jit(solution)/shard_map/ppermute | solution.py:356
  467.1 46.4 %collective-permute-start.16 = (bf16[192,1600]{1,0:T(8,128)(2,1)S(1)}, bf16[192,1600]{1,0:T(8,128)(2,1)S(1)}, u32[]{:S(2)}, u32[]{:S(2)}) collective-permute-start(bf16[192,1600]{1,0:T(8,128)(2,1)S(1)} %get-tuple-element.379), channel_id=1, source_target_pairs={{0,4},{1,5},{2,6},{3,7},{4,0},{5,1},{6,2},{7,3}} | collective-permute-start | bytes 1843208 | tf_op jit(solution)/shard_map/ppermute | solution.py:356
  468.9 56.0 %collective-permute-start.17 = (bf16[192,1600]{1,0:T(8,128)(2,1)S(1)}, bf16[192,1600]{1,0:T(8,128)(2,1)S(1)}, u32[]{:S(2)}, u32[]{:S(2)}) collective-permute-start(bf16[192,1600]{1,0:T(8,128)(2,1)S(1)} %get-tuple-element.378), channel_id=1, source_target_pairs={{0,5},{1,4},{2,7},{3,6},{4,1},{5,0},{6,3},{7,2}} | collective-permute-start | bytes 1843208 | tf_op jit(solution)/shard_map/ppermute | solution.py:356
  472.2 68.7 %collective-permute-start.18 = (bf16[192,1600]{1,0:T(8,128)(2,1)S(1)}, bf16[192,1600]{1,0:T(8,128)(2,1)S(1)}, u32[]{:S(2)}, u32[]{:S(2)}) collective-permute-start(bf16[192,1600]{1,0:T(8,128)(2,1)S(1)} %get-tuple-element.377), channel_id=1, source_target_pairs={{0,6},{1,7},{2,4},{3,5},{4,2},{5,3},{6,0},{7,1}} | collective-permute-start | bytes 1843208 | tf_op jit(solution)/shard_map/ppermute | solution.py:356
  489.0 69.5 %collective-permute-start.19 = (bf16[192,1600]{1,0:T(8,128)(2,1)S(1)}, bf16[192,1600]{1,0:T(8,128)(2,1)S(1)}, u32[]{:S(2)}, u32[]{:S(2)}) collective-permute-start(bf16[192,1600]{1,0:T(8,128)(2,1)S(1)} %get-tuple-element.376), channel_id=1, source_target_pairs={{0,7},{1,6},{2,5},{3,4},{4,3},{5,2},{6,1},{7,0}} | collective-permute-start | bytes 1843208 | tf_op jit(solution)/shard_map/ppermute | solution.py:356
  591.3 55.8 %collective-permute-start.3 = (bf16[192,1600]{1,0:T(8,128)(2,1)}, bf16[192,1600]{1,0:T(8,128)(2,1)}, u32[]{:S(2)}, u32[]{:S(2)}) collective-permute-start(bf16[192,1600]{1,0:T(8,128)(2,1)} %get-tuple-element.555), channel_id=1, source_target_pairs={{0,3},{1,2},{2,1},{3,0},{4,7},{5,6},{6,5},{7,4}} | collective-permute-start | bytes 1843208 | tf_op jit(solution)/shard_map/while/body/ppermute | solution.py:356
  591.3 57.8 %collective-permute-start.4 = (bf16[192,1600]{1,0:T(8,128)(2,1)S(1)}, bf16[192,1600]{1,0:T(8,128)(2,1)}, u32[]{:S(2)}, u32[]{:S(2)}) collective-permute-start(bf16[192,1600]{1,0:T(8,128)(2,1)S(1)} %get-tuple-element.556), channel_id=1, source_target_pairs={{0,4},{1,5},{2,6},{3,7},{4,0},{5,1},{6,2},{7,3}} | collective-permute-start | bytes 1843208 | tf_op jit(solution)/shard_map/while/body/ppermute | solution.py:356
  593.8 59.2 %collective-permute-start.5 = (bf16[192,1600]{1,0:T(8,128)(2,1)S(1)}, bf16[192,1600]{1,0:T(8,128)(2,1)}, u32[]{:S(2)}, u32[]{:S(2)}) collective-permute-start(bf16[192,1600]{1,0:T(8,128)(2,1)S(1)} %get-tuple-element.557), channel_id=1, source_target_pairs={{0,5},{1,4},{2,7},{3,6},{4,1},{5,0},{6,3},{7,2}} | collective-permute-start | bytes 1843208 | tf_op jit(solution)/shard_map/while/body/ppermute | solution.py:356
  604.8 72.8 %collective-permute-start.6 = (bf16[192,1600]{1,0:T(8,128)(2,1)S(1)}, bf16[192,1600]{1,0:T(8,128)(2,1)S(1)}, u32[]{:S(2)}, u32[]{:S(2)}) collective-permute-start(bf16[192,1600]{1,0:T(8,128)(2,1)S(1)} %get-tuple-element.558), channel_id=1, source_target_pairs={{0,6},{1,7},{2,4},{3,5},{4,2},{5,3},{6,0},{7,1}} | collective-permute-start | bytes 1843208 | tf_op jit(solution)/shard_map/while/body/ppermute | solution.py:356
  620.5 75.7 %collective-permute-start.7 = (bf16[192,1600]{1,0:T(8,128)(2,1)S(1)}, bf16[192,1600]{1,0:T(8,128)(2,1)S(1)}, u32[]{:S(2)}, u32[]{:S(2)}) collective-permute-start(bf16[192,1600]{1,0:T(8,128)(2,1)S(1)} %get-tuple-element.559), channel_id=1, source_target_pairs={{0,7},{1,6},{2,5},{3,4},{4,3},{5,2},{6,1},{7,0}} | collective-permute-start | bytes 1843208 | tf_op jit(solution)/shard_map/while/body/ppermute | solution.py:356
  733.3 57.0 %collective-permute-start.5 = (bf16[192,1600]{1,0:T(8,128)(2,1)S(1)}, bf16[192,1600]{1,0:T(8,128)(2,1)}, u32[]{:S(2)}, u32[]{:S(2)}) collective-permute-start(bf16[192,1600]{1,0:T(8,128)(2,1)S(1)} %get-tuple-element.557), channel_id=1, source_target_pairs={{0,5},{1,4},{2,7},{3,6},{4,1},{5,0},{6,3},{7,2}} | collective-permute-start | bytes 1843208 | tf_op jit(solution)/shard_map/while/body/ppermute | solution.py:356
  745.2 47.0 %collective-permute-start.6 = (bf16[192,1600]{1,0:T(8,128)(2,1)S(1)}, bf16[192,1600]{1,0:T(8,128)(2,1)S(1)}, u32[]{:S(2)}, u32[]{:S(2)}) collective-permute-start(bf16[192,1600]{1,0:T(8,128)(2,1)S(1)} %get-tuple-element.558), channel_id=1, source_target_pairs={{0,6},{1,7},{2,4},{3,5},{4,2},{5,3},{6,0},{7,1}} | collective-permute-start | bytes 1843208 | tf_op jit(solution)/shard_map/while/body/ppermute | solution.py:356
  830.3 56.9 %collective-permute-start.5 = (bf16[192,1600]{1,0:T(8,128)(2,1)S(1)}, bf16[192,1600]{1,0:T(8,128)(2,1)}, u32[]{:S(2)}, u32[]{:S(2)}) collective-permute-start(bf16[192,1600]{1,0:T(8,128)(2,1)S(1)} %get-tuple-element.557), channel_id=1, source_target_pairs={{0,5},{1,4},{2,7},{3,6},{4,1},{5,0},{6,3},{7,2}} | collective-permute-start | bytes 1843208 | tf_op jit(solution)/shard_map/while/body/ppermute | solution.py:356
  842.2 46.9 %collective-permute-start.6 = (bf16[192,1600]{1,0:T(8,128)(2,1)S(1)}, bf16[192,1600]{1,0:T(8,128)(2,1)S(1)}, u32[]{:S(2)}, u32[]{:S(2)}) collective-permute-start(bf16[192,1600]{1,0:T(8,128)(2,1)S(1)} %get-tuple-element.558), channel_id=1, source_target_pairs={{0,6},{1,7},{2,4},{3,5},{4,2},{5,3},{6,0},{7,1}} | collective-permute-start | bytes 1843208 | tf_op jit(solution)/shard_map/while/body/ppermute | solution.py:356
  927.1 57.0 %collective-permute-start.5 = (bf16[192,1600]{1,0:T(8,128)(2,1)S(1)}, bf16[192,1600]{1,0:T(8,128)(2,1)}, u32[]{:S(2)}, u32[]{:S(2)}) collective-permute-start(bf16[192,1600]{1,0:T(8,128)(2,1)S(1)} %get-tuple-element.557), channel_id=1, source_target_pairs={{0,5},{1,4},{2,7},{3,6},{4,1},{5,0},{6,3},{7,2}} | collective-permute-start | bytes 1843208 | tf_op jit(solution)/shard_map/while/body/ppermute | solution.py:356
  939.1 47.0 %collective-permute-start.6 = (bf16[192,1600]{1,0:T(8,128)(2,1)S(1)}, bf16[192,1600]{1,0:T(8,128)(2,1)S(1)}, u32[]{:S(2)}, u32[]{:S(2)}) collective-permute-start(bf16[192,1600]{1,0:T(8,128)(2,1)S(1)} %get-tuple-element.558), channel_id=1, source_target_pairs={{0,6},{1,7},{2,4},{3,5},{4,2},{5,3},{6,0},{7,1}} | collective-permute-start | bytes 1843208 | tf_op jit(solution)/shard_map/while/body/ppermute | solution.py:356
  1109.1 269.8 %collective-permute-start.20 = (bf16[1024,1600]{0,1:T(8,128)(2,1)}, bf16[1024,1600]{0,1:T(8,128)(2,1)}, u32[]{:S(2)}, u32[]{:S(2)}) collective-permute-start(bf16[1024,1600]{0,1:T(8,128)(2,1)} %copy.105), channel_id=1, source_target_pairs={{0,1},{1,0},{2,3},{3,2},{4,5},{5,4},{6,7},{7,6}} | collective-permute-start | bytes 9830408 | tf_op jit(solution)/shard_map/ppermute | solution.py:452
  1382.8 165.1 %all-gather.25.cloned.1.call-start = ((), (), s32[]{:S(2)}) async-start(), calls=%async_computation.3 | async-start | bytes 15335424 | tf_op jit(solution)/shard_map/all_gather | solution.py:463
  (55 other events, 1126.8 us)
Sparse Core Ops, SparseCore 0:
  9.9 38.9 all-gather.26
  50.7 45.4 all-gather.18
  98.0 74.3 all-gather.30
  174.1 131.0 all-gather.28
  306.8 35.4 all-gather.32
  344.0 44.0 all-gather.20
  389.9 74.3 all-gather.36
  466.1 225.5 all-gather.34
  1382.9 69.8 all-gather.22
  1454.5 70.7 all-gather.24

commit v2 on v1

--- a/solution.py
+++ b/solution.py
@@ -7,6 +7,7 @@
 from jax.experimental.pallas import tpu as pltpu
 from jax.sharding import PartitionSpec as P
 
+
 HEAD_DIM = 64
 EPS = 1e-6
 ROPE_BASE = 10000.0
@@ -23,12 +24,14 @@
 QH = 25
 KVH = 5
 QKV = 2240
+O_AT = 2304
 FF = 4352
 SEQ = 32
 TB = 256
 SUB = 128
 FT = 256
 VT = 2048
+HT = 512
 
 
 def dot(lhs, rhs):
@@ -56,18 +59,16 @@
 
 
 def attn_kernel(n, layer, core_ref, h_ref, gain_ref, cos_ref, sin_ref, *refs):
-    qkv_parts, wo_parts = refs[:n], refs[n:2 * n]
-    out_ref, wqkv, wo, qkv_s, qk_s, o_s, sc_s, p_s, sems = refs[2 * n:]
+    out_ref, w_s, qkv_s, qk_s, o_s, sc_s, p_s, sems = refs[n:]
     core = core_ref[0]
 
     def half_of(p):
         return jnp.bitwise_xor(core, p)
 
-    first = row_copies(qkv_parts, layer, half_of, wqkv, sems, 0)
-    second = row_copies(wo_parts, layer, half_of, wo, sems, n)
-    for copy in first + second:
+    copies = row_copies(refs[:n], layer, half_of, w_s, sems, 0)
+    for copy in copies:
         copy.start()
-    for copy in first:
+    for copy in copies:
         copy.wait()
 
     lane = lax.broadcasted_iota(jnp.int32, (1, 128), 1)
@@ -80,7 +81,7 @@
 
     def project(b):
         rows = pl.ds(pl.multiple_of(b * TB, TB), TB)
-        qkv_s[...] = dot(rms(h_ref[rows, :], gain_ref[...]), wqkv[...])
+        qkv_s[...] = dot(rms(h_ref[rows, :], gain_ref[...]), w_s[:, :QKV])
         cos, sin = cos_ref[...], sin_ref[...]
         for j in range(15):
             x = qkv_s[:, 128 * j:128 * (j + 1)]
@@ -125,37 +126,31 @@
         project(b)
         for s in range(TB // SUB):
             attend(s)
-
-        @pl.when(b == 0)
-        def _():
-            for copy in second:
-                copy.wait()
-
-        out_ref[rows, :] = (h_ref[rows, :].astype(F32) + dot(o_s[...], wo[...])).astype(BF16)
+        out_ref[rows, :] = (h_ref[rows, :].astype(F32) + dot(o_s[...], w_s[:, O_AT:])).astype(BF16)
         return carry
 
     lax.fori_loop(0, h_ref.shape[0] // TB, block, 0)
 
 
-def attention_block(h, gain, tabs, w_qkv, w_o, layer, core):
-    n = len(w_qkv)
+def attention_block(h, gain, tabs, w_att, layer, core):
+    n = len(w_att)
     t = h.shape[0]
     vm = pl.BlockSpec(memory_space=pltpu.VMEM)
     anym = pl.BlockSpec(memory_space=pl.ANY)
     return pl.pallas_call(
         functools.partial(attn_kernel, n, layer),
         out_shape=jax.ShapeDtypeStruct((t, D), BF16),
-        in_specs=[pl.BlockSpec(memory_space=pltpu.SMEM), vm, vm, vm, vm] + [anym] * (2 * n),
+        in_specs=[pl.BlockSpec(memory_space=pltpu.SMEM), vm, vm, vm, vm] + [anym] * n,
         out_specs=vm,
         scratch_shapes=[
-            pltpu.VMEM((D, QKV), BF16), pltpu.VMEM((D, D), BF16), pltpu.VMEM((TB, QKV), F32),
+            pltpu.VMEM((D, O_AT + D), BF16), pltpu.VMEM((TB, QKV), F32),
             pltpu.VMEM((TB, 1920), BF16), pltpu.VMEM((TB, D), BF16), pltpu.VMEM((SUB, 26 * SUB), F32), pltpu.VMEM((SUB, 26 * SUB), BF16),
-            pltpu.SemaphoreType.DMA((2 * n,)),
+            pltpu.SemaphoreType.DMA((n,)),
         ],
         compiler_params=pltpu.CompilerParams(vmem_limit_bytes=VMEM_LIMIT),
         cost_estimate=pl.CostEstimate(flops=2 * t * D * (QKV + D), bytes_accessed=2 * D * (QKV + D), transcendentals=0),
         name="attn",
-    )(core, h, gain, tabs[0], tabs[1], *w_qkv, *w_o)
+    )(core, h, gain, tabs[0], tabs[1], *w_att)
 
 
 def mlp_kernel(n, layer, last, core_ref, h_ref, gain_ref, fin_ref, *refs):
@@ -269,7 +264,69 @@
     )(core, h, gain, fin, *w_gu, *w_dn)
 
 
-def head_kernel(vocab, x_ref, w_ref, tgt_ref, out_ref, m_s, s_s, p_s):
+def gate_up_kernel(h_ref, gain_ref, wg_ref, wu_ref, act_ref, c_s):
+    @pl.when(pl.program_id(0) == 0)
+    def _():
+        c_s[...] = rms(h_ref[...], gain_ref[...])
+
+    g = dot(c_s[...], wg_ref[...])
+    u = dot(c_s[...], wu_ref[...])
+    act_ref[...] = (g * jax.nn.sigmoid(g) * u).astype(BF16)
+
+
+def down_kernel(h_ref, act_ref, w_ref, fin_ref, out_ref, acc):
+    j = pl.program_id(0)
+
+    @pl.when(j == 0)
+    def _():
+        acc[...] = h_ref[...].astype(F32)
+
+    acc[...] += dot(act_ref[...], w_ref[...])
+
+    @pl.when(j == pl.num_programs(0) - 1)
+    def _():
+        out_ref[...] = rms(acc[...].astype(BF16), fin_ref[...])
+
+
+def gate_up(h, gain, w_gu):
+    t, steps = h.shape[0], FF // FT
+    fixed = lambda j: (0, 0)
+    return pl.pallas_call(
+        gate_up_kernel,
+        out_shape=jax.ShapeDtypeStruct((t, FF), BF16),
+        grid=(steps,),
+        in_specs=[
+            pl.BlockSpec((t, D), fixed), pl.BlockSpec((1, D), fixed),
+            pl.BlockSpec((D, FT), lambda j: (0, j)), pl.BlockSpec((D, FT), lambda j: (0, steps + j)),
+        ],
+        out_specs=pl.BlockSpec((t, FT), lambda j: (0, j)),
+        scratch_shapes=[pltpu.VMEM((t, D), BF16)],
+        compiler_params=pltpu.CompilerParams(vmem_limit_bytes=VMEM_LIMIT),
+        cost_estimate=pl.CostEstimate(flops=4 * t * D * FF, bytes_accessed=4 * D * FF, transcendentals=0),
+        name="gate_up",
+    )(h, gain, w_gu, w_gu)
+
+
+def down_norm(h, act, w_dn, fin):
+    t = h.shape[0]
+    fixed = lambda j: (0, 0)
+    return pl.pallas_call(
+        down_kernel,
+        out_shape=jax.ShapeDtypeStruct((t, D), BF16),
+        grid=(FF // FT,),
+        in_specs=[
+            pl.BlockSpec((t, D), fixed), pl.BlockSpec((t, FT), lambda j: (0, j)),
+            pl.BlockSpec((FT, D), lambda j: (j, 0)), pl.BlockSpec((1, D), fixed),
+        ],
+        out_specs=pl.BlockSpec((t, D), fixed),
+        scratch_shapes=[pltpu.VMEM((t, D), F32)],
+        compiler_params=pltpu.CompilerParams(vmem_limit_bytes=VMEM_LIMIT),
+        cost_estimate=pl.CostEstimate(flops=2 * t * D * FF, bytes_accessed=2 * D * FF, transcendentals=0),
+        name="down",
+    )(h, act, w_dn, fin)
+
+
+def head_kernel(vocab, x_ref, w_ref, tgt_ref, out_ref, lg_s, m_s, s_s, p_s):
     j = pl.program_id(1)
 
     @pl.when(j == 0)
@@ -281,16 +338,26 @@
     lane = lax.broadcasted_iota(jnp.int32, m_s.shape, 1)
     rel = tgt_ref[...] - lane - j * VT
     held = vocab - j * VT
-    for at in range(0, VT, 256):
-        logits = dot(x_ref[...], w_ref[:, at:at + 256])
-        cols = [logits[:, :128], logits[:, 128:]]
-        if at + 256 > (vocab % VT or VT):
+
+    def update(k):
+        at = k * HT
+        cols = [lg_s[k % 2, :, 128 * c:128 * (c + 1)] for c in range(HT // 128)]
+        if at + HT > (vocab % VT or VT):
             cols = [jnp.where(lane < held - at - 128 * c, x, NEG) for c, x in enumerate(cols)]
         m_old = m_s[...]
-        m_new = jnp.maximum(m_old, jnp.maximum(cols[0], cols[1]))
-        s_s[...] = s_s[...] * jnp.exp(m_old - m_new) + (jnp.exp(cols[0] - m_new) + jnp.exp(cols[1] - m_new))
+        m_new = functools.reduce(jnp.maximum, cols, m_old)
+        s_s[...] = s_s[...] * jnp.exp(m_old - m_new) + sum(jnp.exp(x - m_new) for x in cols)
         m_s[...] = m_new
-        p_s[...] += jnp.where(rel == at, cols[0], jnp.where(rel == at + 128, cols[1], 0.0))
+        picked = 0.0
+        for c, x in enumerate(cols):
+            picked = jnp.where(rel == at + 128 * c, x, picked)
+        p_s[...] += picked
+
+    for k in range(VT // HT):
+        lg_s[k % 2] = dot(x_ref[...], w_ref[:, k * HT:(k + 1) * HT])
+        if k:
+            update(k - 1)
+    update(VT // HT - 1)
 
     @pl.when(j == pl.num_programs(1) - 1)
     def _():
@@ -313,7 +380,7 @@
             pl.BlockSpec((tt, 128), lambda i, j: (i, 0)),
         ],
         out_specs=pl.BlockSpec((tt, 128), lambda i, j: (i, 0)),
-        scratch_shapes=[pltpu.VMEM((tt, 128), F32)] * 3,
+        scratch_shapes=[pltpu.VMEM((2, tt, HT), F32)] + [pltpu.VMEM((tt, 128), F32)] * 3,
         compiler_params=pltpu.CompilerParams(vmem_limit_bytes=VMEM_LIMIT),
         cost_estimate=pl.CostEstimate(flops=2 * t * D * v, bytes_accessed=2 * D * (v * t // tt + t), transcendentals=t * v),
         name="head",
@@ -337,32 +404,30 @@
     return dot(flags.astype(BF16), upper).astype(jnp.int32)
 
 
-def embed_rows(table, toks, me, size, cap, perms, axis, order):
-    vocab, t = table.shape[0], toks.shape[1]
+def embed_send(table, toks, me, cap, r):
+    size, vocab = toks.shape[0], table.shape[0]
     local = toks - me * vocab
     owned = (local >= 0) & (local < vocab)
     rank = running_count(owned) - 1
+    slots = r * cap + jnp.arange(cap)
+    hit = owned[:, None, :] & (rank[:, None, :] == slots[None, :, None])
+    idx = jnp.sum(jnp.where(hit, local[:, None, :], 0), axis=2)
+    rows = jnp.take(table, idx.reshape(-1), axis=0).reshape(size, cap, D)
+    return [rows[k] for k in range(size)]
+
+
+def embed_swap(rows, perms, axis):
+    return rows[:1] + [lax.ppermute(rows[k], axis, perms[k]) for k in range(1, len(rows))]
+
+
+def embed_pick(got, tok, vocab, me, cap, r):
+    size, t = len(got), tok.shape[0]
     peers = jnp.bitwise_xor(me, jnp.arange(size))
-    wanted = (toks[0] // vocab)[None, :] == peers[:, None]
-    my_rank = running_count(wanted) - 1
-
-    def one_round(r):
-        slots = r * cap + jnp.arange(cap)
-        hit = owned[:, None, :] & (rank[:, None, :] == slots[None, :, None])
-        idx = jnp.sum(jnp.where(hit, local[:, None, :], 0), axis=2)
-        got = [jnp.take(table, idx[0], axis=0)]
-        rows = jnp.take(table, idx[1:].reshape(-1), axis=0).reshape(size - 1, cap, D)
-        for k in range(1, size):
-            got.append(lax.ppermute(rows[k - 1], axis, perms[k]))
-        pick = wanted[:, :, None] & (my_rank[:, :, None] == slots[None, None, :])
-        pick = jnp.swapaxes(pick, 0, 1).reshape(t, size * cap).astype(BF16)
-        return dot(pick, jnp.concatenate(got, axis=0))
-
-    counts = jnp.sum((order[:, None, :] // vocab) == jnp.arange(32000 // vocab)[None, :, None], axis=2)
-    rounds = (jnp.max(counts) + cap - 1) // cap
-    rows = one_round(0)
-    rows = lax.fori_loop(1, rounds, lambda r, acc: acc + one_round(r), rows)
-    return rows.astype(BF16)
+    wanted = (tok // vocab)[None, :] == peers[:, None]
+    slot = running_count(wanted) - 1 - r * cap
+    pick = wanted[:, :, None] & (slot[:, :, None] == jnp.arange(cap)[None, None, :])
+    pick = jnp.swapaxes(pick, 0, 1).reshape(t, size * cap).astype(BF16)
+    return dot(pick, jnp.concatenate(got, axis=0)).astype(BF16)
 
 
 def advantages(rewards, groups):
@@ -408,57 +473,80 @@
         layers = p_q.shape[0]
         tabs = rope_tables()
 
-        small = jnp.concatenate([x.astype(F32).reshape(-1) for x in (tokens, resp_mask, logp_old, rewards, group_id, p_norms, r_norms)])
-        size = -small.size % 1024
-        small = lax.all_gather(jnp.pad(small, (0, size)).reshape(-1, 128), both).reshape(n_dev, -1)
+        tok = tokens.reshape(t)
+        tok_pair = jnp.stack([tok, lax.ppermute(tok, 'fsdp', swap)])
+        local = tok_pair - core * p_embed.shape[0]
+        looked = jnp.take(p_embed, jnp.clip(local, 0, p_embed.shape[0] - 1), axis=0)
+        from_peer = lax.ppermute(looked[1], 'fsdp', swap)
+        h = jnp.where(((local[0] >= 0) & (local[0] < p_embed.shape[0]))[:, None], looked[0], from_peer)
+        p_gains = jnp.stack([p_norms, lax.ppermute(p_norms, 'fsdp', swap)]).astype(F32)
+        p_gains = jnp.where(core == 0, p_gains, p_gains[::-1])
+        p_gains = jnp.swapaxes(p_gains, 0, 1).reshape(2 * layers + 1, 1, D)
+
+        smalls = (tokens, resp_mask, logp_old, rewards, group_id, r_norms)
+        small = jnp.concatenate([x.astype(F32).reshape(-1) for x in smalls])
+        small = jnp.pad(small, (0, -small.size % 1024)).reshape(-1, 128)
+        small = jnp.stack([small] + [lax.ppermute(small, both, xors[k]) for k in range(1, n_dev)])
+        xor_ids = jnp.bitwise_xor(me, jnp.arange(n_dev))
+        order = small.reshape(n_dev, -1)[:, :t].astype(jnp.int32)
+        small = small[xor_ids].reshape(n_dev, -1)
         cuts, at = [], 0
-        for x in (tokens, resp_mask, logp_old, rewards, group_id, p_norms, r_norms):
+        for x in smalls:
             cuts.append(small[:, at:at + x.size].reshape((n_dev,) + x.shape))
             at += x.size
         tok_all = cuts[0].astype(jnp.int32).reshape(n_dev, t)
         mask_all, old_all = (x.reshape(n_dev * rows, SEQ) for x in cuts[1:3])
         reward_all = cuts[3].reshape(-1)
         group_all = cuts[4].reshape(-1)
-        p_gains = jnp.swapaxes(cuts[5][:2], 0, 1).reshape(2 * layers + 1, 1, D)
-        r_gains = jnp.swapaxes(cuts[6], 0, 1).reshape(2 * layers + 1, 1, D)
+        r_gains = jnp.swapaxes(cuts[5], 0, 1).reshape(2 * layers + 1, 1, D)
         tgt_all = jnp.roll(tok_all.reshape(n_dev * rows, SEQ), -1, axis=1).reshape(n_dev, t)
 
-        p_qkv = jnp.concatenate([p_q, p_kv], axis=2)
-        p_qkv, p_wo, p_wgu, p_wdn = ([w, lax.ppermute(w, 'fsdp', swap)] for w in (p_qkv, p_o, p_gu, jnp.swapaxes(p_dn, 1, 2)))
+        def attention_weights(q, kv, o):
+            return jnp.concatenate([q, kv, jnp.zeros(q.shape[:-1] + (O_AT - QKV,), BF16), o], axis=-1)
+
+        p_att = attention_weights(p_q, p_kv, p_o)
+        p_parts = []
+        for w in (p_att, p_gu, jnp.swapaxes(p_dn, 1, 2)):
+            p_parts.append([w, lax.ppermute(w, 'fsdp', swap)])
+        p_att, p_wgu, p_wdn = p_parts
         p_head, r_head = p_head.T, r_head.T
 
-        r_full = []
-        for layer in range(layers):
-            att = lax.all_gather(jnp.concatenate([r_q[layer], r_kv[layer]], axis=1), both, axis=0, tiled=True)
-            r_full.append([att] + [lax.all_gather(w[layer], both, axis=0, tiled=True) for w in (r_o, r_gu, r_dn)])
-
-        chip_tok = tok_all[jnp.bitwise_xor(me, jnp.arange(2))]
-        h = embed_rows(p_embed, chip_tok, core, 2, 640, [None, swap], 'fsdp', tok_all)
+        def ref_weights(layer, dn):
+            att = attention_weights(r_q[layer], r_kv[layer], r_o[layer])
+            return [lax.all_gather(w, both, axis=0, tiled=True) for w in (att, r_gu[layer], dn)]
 
         def policy_layer(h, layer):
-            h = attention_block(h, p_gains[2 * layer], tabs, p_qkv, p_wo, layer, core_arr)
+            h = attention_block(h, p_gains[2 * layer], tabs, p_att, layer, core_arr)
             return mlp_block(h, p_gains[2 * layer + 1], p_gains[2 * layers], p_wgu, p_wdn, layer, layer == layers - 1, core_arr)
 
-        def ref_layer(h, layer):
-            w_qkv, w_o, w_gu, w_dn = r_full[layer]
-            h = attention_block(h, r_gains[2 * layer], tabs, [w_qkv], [w_o], None, core_arr)
-            return mlp_block(h, r_gains[2 * layer + 1], r_gains[2 * layers], [w_gu], [w_dn], None, layer == layers - 1, core_arr)
-
+        r_full = [ref_weights(0, r_dn[0])]
         h = policy_layer(h, 0)
-        order, h = lax.optimization_barrier((tok_all[jnp.bitwise_xor(me, jnp.arange(n_dev))], h))
-        h_ref = embed_rows(r_embed, order, me, n_dev, 192, xors, both, tok_all)
-        h, h_ref = lax.optimization_barrier((h, h_ref))
+        order, dn, h = lax.optimization_barrier((order, r_dn[1], h))
+        r_full.append(ref_weights(1, dn))
+        cap = 192
+        h, got = lax.optimization_barrier((h, embed_send(r_embed, order, me, cap, 0)))
+        got = embed_swap(got, xors, both)
         x = policy_layer(h, 1)
         x_peer = lax.ppermute(x, 'fsdp', swap)
+        got, x = lax.optimization_barrier((got, x))
+        h_ref = embed_pick(got, tok, r_embed.shape[0], me, cap, 0)
+        counts = jnp.sum((tok_all[:, None, :] // r_embed.shape[0]) == jnp.arange(n_dev)[None, :, None], axis=2)
+        h_ref = lax.fori_loop(1, (jnp.max(counts) + cap - 1) // cap, lambda r, acc: acc + embed_pick(
+            embed_swap(embed_send(r_embed, order, me, cap, r), xors, both), tok, r_embed.shape[0], me, cap, r), h_ref)
         tgt_own = tgt_all[me] - core * p_head.shape[1]
         tgt_peer = tgt_all[jnp.bitwise_xor(me, 1)] - core * p_head.shape[1]
 
         h_ref, x = lax.optimization_barrier((h_ref, x))
-        h_ref = ref_layer(h_ref, 0)
+        att, w_gu, w_dn = r_full[0]
+        h_ref = attention_block(h_ref, r_gains[0], tabs, [att], None, core_arr)
+        h_ref = mlp_block(h_ref, r_gains[1], r_gains[2 * layers], [w_gu], [w_dn], None, False, core_arr)
         x, h_ref = lax.optimization_barrier((x, h_ref))
         own = head_block(x, p_head, tgt_own)
         h_ref, own = lax.optimization_barrier((h_ref, own))
-        x_ref = ref_layer(h_ref, 1)
+        att, w_gu, w_dn = r_full[1]
+        h_ref = attention_block(h_ref, r_gains[2], tabs, [att], None, core_arr)
+        act = gate_up(h_ref, r_gains[3], w_gu)
+        x_ref = down_norm(h_ref, act, w_dn, r_gains[2 * layers])
         x_peer, x_ref = lax.optimization_barrier((x_peer, x_ref))
         x_all = [lax.all_gather(x_ref[at:at + t // 2], both, axis=0, tiled=True) for at in (0, t // 2)]
         peer = head_block(x_peer, p_head, tgt_peer)

time: 1670 us -> 1560 us (0.934)
  blocking collectives: 67.6 us -> 13.2 us
  waiting for transfers between devices: 272 us -> 235 us
  matrix products: 69 us -> 41.9 us
  starting transfers between devices: 69.3 us -> 90.3 us
  other arithmetic: 64.5 us -> 45 us
    pallas_call x0 -> x2, Pallas kernels: none -> 67.3 us  [the longest x1 40.4 us: gate_up(): pl.pallas_call(gate_up_kernel, out_shape=jax.ShapeDtypeStruct((t, FF), BF...]
    pallas_call x4 -> x3, Pallas kernels: 247 us -> 185 us  [mlp_block(): pl.pallas_call(functools.partial(mlp_kernel, n, layer, last), out_shape=j...]
    all_gather x1 -> x0, blocking collectives: 54.3 us -> none  [device_step(): lax.all_gather(jnp.pad(small, (0, size)).reshape(-1, 128), both)]
    gather x16 -> x7, local copies, waits for them, and re-layouts: 186 us -> 137 us  [the longest x5 86.8 us: embed_send(): rows = jnp.take(table, idx.reshape(-1), axis=0).reshape(size, cap, D)]
    ppermute x41 -> x48, waiting for transfers between devices: 270 us -> 233 us  [the longest x35 214 us: embed_swap(): lax.ppermute(rows[k], axis, perms[k])]
    dot_general x11, matrix products: 69 us -> 41.9 us  [dot(): lax.dot_general(lhs, rhs, (((1,), (0,)), ((), ())), preferred_element_typ...]
    concatenate x6 -> x9, local copies, waits for them, and re-layouts: 3.88 us -> 30.1 us  [the longest x3 25.3 us: attention_weights(): jnp.concatenate([q, kv, jnp.zeros(q.shape[:-1] + (O_AT - QKV,), BF16), o]...]
    ppermute x41 -> x48, starting transfers between devices: 68.5 us -> 89.5 us  [the longest x1 51.2 us: device_step(): from_peer = lax.ppermute(looked[1], 'fsdp', swap)]
  transfers between devices with their start and end apart: 52 -> 57, of which waited for: 19 -> 21; matrix products, arithmetic and copies ran while one was open for 32% -> 30% of each run, Pallas kernels for 37% -> 40%
where the time goes in v2:
time: 1560 us; the launch traced here: 1540 us
  Pallas kernels  693 us (44%)
  local copies, waits for them, and re-layouts  404 us (26%)
  waiting for transfers between devices  235 us (15%)
  starting transfers between devices  90.3 us (6%)
  other arithmetic  45 us (3%)
  matrix products  41.9 us (3%)
  between operations  18 us (1%)
    pallas_call x4, Pallas kernels, head_block(): pl.pallas_call(functools.partial(head_kernel, v), out_shape=jax.ShapeDtyp...  288 us
    ppermute x35, waiting for transfers between devices, embed_swap(): lax.ppermute(rows[k], axis, perms[k])  214 us
    pallas_call x3, Pallas kernels, mlp_block(): pl.pallas_call(functools.partial(mlp_kernel, n, layer, last), out_shape=j...  185 us
    pallas_call x4, Pallas kernels, attention_block(): pl.pallas_call(functools.partial(attn_kernel, n, layer), out_shape=jax.Sh...  152 us
    unnamed x75, local copies, waits for them, and re-layouts  101 us
    gather x5, local copies, waits for them, and re-layouts, embed_send(): rows = jnp.take(table, idx.reshape(-1), axis=0).reshape(size, cap, D)  86.8 us
    ppermute x1, starting transfers between devices, device_step(): from_peer = lax.ppermute(looked[1], 'fsdp', swap)  51.2 us
    while x40, local copies, waits for them, and re-layouts  49.6 us
  transfers between devices with their start and end apart: 57, of which 21 were waited for; matrix products, arithmetic and copies ran while one was open for 30% of the time, Pallas kernels for 40%

profile of v2, /device:TPU:0, one launch (start us, length us, event | category | flops | bytes accessed | tf_op | source)
XLA Modules:
  0.0 1540.8 jit_solution(414163262029322475)
XLA Ops:
  30.1 19.2 %concatenate.58.refs_0_ = bf16[2,800,3904]{2,1,0:T(8,128)(2,1)} concatenate(bf16[2,800,1600]{2,1,0:T(8,128)(2,1)} %param.28, bf16[2,800,640]{2,1,0:T(8,128)(2,1)S(1)} %copy-done.3, bf16[2,800,64]{2,1,0:T(8,128)(2,1)S(1)} %broadcast_in_dim.186, bf16[2,800,1600]{2,1,0:T(8,128)(2,1)} %param.30), dimensions={2} | concatenate | bytes 24985600 | tf_op jit(solution)/shard_map/concatenate | solution.py:505
  51.7 66.8 %copy.68 = bf16[16000,1600]{1,0:T(8,128)(2,1)} copy(bf16[16000,1600]{0,1:T(8,128)(2,1)} %param.34) | data formatting | bytes 102400000 | tf_op args[11]
  118.6 18.4 %copy.71 = bf16[4000,1600]{1,0:T(8,128)(2,1)} copy(bf16[4000,1600]{0,1:T(8,128)(2,1)} %param.42) | data formatting | bytes 25600000 | tf_op args[19]
  140.8 49.0 %gather_fusion.1 = bf16[2048,1600]{1,0:T(8,128)(2,1)} fusion(bf16[16000,1600]{1,0:T(8,128)(2,1)} %copy.68, s32[2048]{0:T(1024)S(1)} %broadcast_clamp_fusion), kind=kCustom, calls=%fused_computation.1 | custom fusion | bytes 13115392 | tf_op jit(solution)/shard_map/jit(_take)/gather | solution.py:479
  200.3 51.2 %collective-permute-start.15 = (bf16[1024,1600]{0,1:T(8,128)(2,1)}, bf16[1024,1600]{0,1:T(8,128)(2,1)}, u32[]{:S(2)}, u32[]{:S(2)}) collective-permute-start(bf16[1024,1600]{0,1:T(8,128)(2,1)} %copy.69), channel_id=1, source_target_pairs={{0,1},{1,0},{2,3},{3,2},{4,5},{5,4},{6,7},{7,6}} | collective-permute-start | bytes 9830408 | tf_op jit(solution)/shard_map/ppermute | solution.py:480
  306.3 38.0 %attn.4.h_ref = bf16[1024,1600]{1,0:T(8,128)(2,1)} custom-call(s32[1]{0:T(128)} %bitcast.14.core_ref, bf16[1024,1600]{1,0:T(8,128)(2,1)} %fusion.15.h_ref, f32[1,1600]{1,0:T(1,128)} %squeeze.105.gain_ref, f32[256,128]{1,0:T(8,128)} %bitcast.135, f32[256,128]{1,0:T(8,128)} %bitcast.139, bf16[2,800,3904]{2,1,0:T(8,128)(2,1)} %concatenate.58.refs_0_, ...), custom_call_target="tpu_custom_call" | custom-call | flops 12582912000 | bytes 12288000 | tf_op jit(solution)/shard_map/attn/pallas_call | solution.py:140
  344.3 61.9 %mlp.3.h_ref = bf16[1024,1600]{1,0:T(8,128)(2,1)} custom-call(s32[1]{0:T(128)} %bitcast.14.core_ref, bf16[1024,1600]{1,0:T(8,128)(2,1)} %attn.4.h_ref, f32[1,1600]{1,0:T(1,128)} %squeeze.106.gain_ref, f32[1,1600]{1,0:T(1,128)} %squeeze.107.fin_ref, bf16[2,800,8704]{2,1,0:T(8,128)(2,1)} %refs_0_.3, bf16[2,800,8704]{2,1,0:T(8,128)(2,1)} %collective-permute-done.18.refs_1_, ...), custom_call_target="tpu_custom_call" | custom-call | flops 42781900800 | bytes 41779200 | tf_op jit(solution)/shard_map/mlp/pallas_call | solution.py:251
  408.1 17.4 %gather_fusion.2 = bf16[1536,1600]{1,0:T(8,128)(2,1)} fusion(bf16[4000,1600]{1,0:T(8,128)(2,1)} %copy.71, s32[2048]{0:T(1024)S(1)} %pad_clamp_fusion.1), kind=kCustom, calls=%fused_computation.2 | custom fusion | bytes 9836544 | tf_op jit(solution)/shard_map/jit(_take)/gather | solution.py:415
  433.3 37.9 %attn.5.h_ref = bf16[1024,1600]{1,0:T(8,128)(2,1)} custom-call(s32[1]{0:T(128)} %bitcast.14.core_ref, bf16[1024,1600]{1,0:T(8,128)(2,1)} %mlp.3.h_ref, f32[1,1600]{1,0:T(1,128)} %squeeze.108.gain_ref, f32[256,128]{1,0:T(8,128)} %bitcast.136, f32[256,128]{1,0:T(8,128)} %bitcast.140, bf16[2,800,3904]{2,1,0:T(8,128)(2,1)} %concatenate.58.refs_0_, ...), custom_call_target="tpu_custom_call" | custom-call | flops 12582912000 | bytes 12288000 | tf_op jit(solution)/shard_map/attn/pallas_call | solution.py:140
  475.0 62.5 %mlp.4.x_ref = bf16[1024,1600]{1,0:T(8,128)(2,1)} custom-call(s32[1]{0:T(128)} %bitcast.14.core_ref, bf16[1024,1600]{1,0:T(8,128)(2,1)} %attn.5.h_ref, f32[1,1600]{1,0:T(1,128)} %squeeze.109.gain_ref, f32[1,1600]{1,0:T(1,128)} %squeeze.107.fin_ref, bf16[2,800,8704]{2,1,0:T(8,128)(2,1)} %refs_0_.3, bf16[2,800,8704]{2,1,0:T(8,128)(2,1)} %collective-permute-done.18.refs_1_, ...), custom_call_target="tpu_custom_call" | custom-call | flops 42781900800 | bytes 41779200 | tf_op jit(solution)/shard_map/mlp/pallas_call | solution.py:251
  559.2 421.7 %while.16 = (s32[]{:T(128)}, bf16[1024,1600]{0,1:T(8,128)(2,1)}, s32[]{:T(128)}, s32[1,1024]{1,0:T(1,128)S(1)}, s32[1024]{0:T(1024)S(1)}, /*index=5*/s32[]{:T(12...) while((s32[]{:T(128)}, bf16[1024,1600]{0,1:T(8,128)(2,1)}, ...), condition=%wide.region_5.6_spmd, body=%wide.region_3.5_spmd.sunk | while | flops 5066265600 | bytes 96910400 | solution.py:534
  560.8 17.4 %gather_fusion = bf16[1536,1600]{1,0:T(8,128)(2,1)} fusion(bf16[4000,1600]{1,0:T(8,128)(2,1)} %get-tuple-element.596, s32[2048]{0:T(1024)S(1)} %pad_clamp_fusion.4), kind=kCustom, calls=%fused_computation.clone.1 | custom fusion | bytes 9836544 | tf_op jit(solution)/shard_map/while/body/jit(_take)/gather | solution.py:415
  592.5 21.4 %collective-permute-done.1 = bf16[192,1600]{1,0:T(8,128)(2,1)} collective-permute-done((bf16[192,1600]{1,0:T(8,128)(2,1)}, bf16[192,1600]{1,0:T(8,128)(2,1)}, u32[]{:S(2)}, u32[]{:S(2)}) %collective-permute-start.1) | collective-permute-done | bytes 614432 | tf_op jit(solution)/shard_map/while/body/ppermute | solution.py:420
  617.1 23.6 %collective-permute-done.2 = bf16[192,1600]{1,0:T(8,128)(2,1)} collective-permute-done((bf16[192,1600]{1,0:T(8,128)(2,1)S(1)}, bf16[192,1600]{1,0:T(8,128)(2,1)}, u32[]{:S(2)}, u32[]{:S(2)}) %collective-permute-start.2) | collective-permute-done | bytes 614432 | tf_op jit(solution)/shard_map/while/body/ppermute | solution.py:420
  646.7 20.4 %collective-permute-done.5 = bf16[192,1600]{1,0:T(8,128)(2,1)S(1)} collective-permute-done((bf16[192,1600]{1,0:T(8,128)(2,1)S(1)}, bf16[192,1600]{1,0:T(8,128)(2,1)S(1)}, u32[]{:S(2)}, u32[]{:S(2)}) %collective-permute-start.5) | collective-permute-done | bytes 614432 | tf_op jit(solution)/shard_map/while/body/ppermute | solution.py:420
  668.0 12.1 collective-permute-done.6
  692.5 17.4 %gather_fusion = bf16[1536,1600]{1,0:T(8,128)(2,1)} fusion(bf16[4000,1600]{1,0:T(8,128)(2,1)} %get-tuple-element.596, s32[2048]{0:T(1024)S(1)} %pad_clamp_fusion.4), kind=kCustom, calls=%fused_computation.clone.1 | custom fusion | bytes 9836544 | tf_op jit(solution)/shard_map/while/body/jit(_take)/gather | solution.py:415
  748.6 25.1 %collective-permute-done.4 = bf16[192,1600]{1,0:T(8,128)(2,1)} collective-permute-done((bf16[192,1600]{1,0:T(8,128)(2,1)S(1)}, bf16[192,1600]{1,0:T(8,128)(2,1)}, u32[]{:S(2)}, u32[]{:S(2)}) %collective-permute-start.4) | collective-permute-done | bytes 614432 | tf_op jit(solution)/shard_map/while/body/ppermute | solution.py:420
  789.0 17.4 %gather_fusion = bf16[1536,1600]{1,0:T(8,128)(2,1)} fusion(bf16[4000,1600]{1,0:T(8,128)(2,1)} %get-tuple-element.596, s32[2048]{0:T(1024)S(1)} %pad_clamp_fusion.4), kind=kCustom, calls=%fused_computation.clone.1 | custom fusion | bytes 9836544 | tf_op jit(solution)/shard_map/while/body/jit(_take)/gather | solution.py:415
  844.8 25.7 %collective-permute-done.4 = bf16[192,1600]{1,0:T(8,128)(2,1)} collective-permute-done((bf16[192,1600]{1,0:T(8,128)(2,1)S(1)}, bf16[192,1600]{1,0:T(8,128)(2,1)}, u32[]{:S(2)}, u32[]{:S(2)}) %collective-permute-start.4) | collective-permute-done | bytes 614432 | tf_op jit(solution)/shard_map/while/body/ppermute | solution.py:420
  885.9 17.4 %gather_fusion = bf16[1536,1600]{1,0:T(8,128)(2,1)} fusion(bf16[4000,1600]{1,0:T(8,128)(2,1)} %get-tuple-element.596, s32[2048]{0:T(1024)S(1)} %pad_clamp_fusion.4), kind=kCustom, calls=%fused_computation.clone.1 | custom fusion | bytes 9836544 | tf_op jit(solution)/shard_map/while/body/jit(_take)/gather | solution.py:415
  942.0 25.0 %collective-permute-done.4 = bf16[192,1600]{1,0:T(8,128)(2,1)} collective-permute-done((bf16[192,1600]{1,0:T(8,128)(2,1)S(1)}, bf16[192,1600]{1,0:T(8,128)(2,1)}, u32[]{:S(2)}, u32[]{:S(2)}) %collective-permute-start.4) | collective-permute-done | bytes 614432 | tf_op jit(solution)/shard_map/while/body/ppermute | solution.py:420
  986.7 37.7 %attn.6.h_ref = bf16[1024,1600]{1,0:T(8,128)(2,1)} custom-call(s32[1]{0:T(128)} %bitcast.14.core_ref, bf16[1024,1600]{1,0:T(8,128)(2,1)} %copy.73.h_ref, f32[1,1600]{1,0:T(1,128)} %squeeze.110.gain_ref, f32[256,128]{1,0:T(8,128)} %bitcast.137, f32[256,128]{1,0:T(8,128)} %bitcast.141, bf16[1600,3904]{1,0:T(8,128)(2,1)} %all-gather.14.cloned.1.call-done.refs_0_), custom_call_target="tpu_custom_call" | custom-call | flops 12582912000 | bytes 12288000 | tf_op jit(solution)/shard_map/attn/pallas_call | solution.py:140
  1024.5 60.9 %mlp.5.h_ref = bf16[1024,1600]{1,0:T(8,128)(2,1)} custom-call(s32[1]{0:T(128)} %bitcast.14.core_ref, bf16[1024,1600]{1,0:T(8,128)(2,1)} %attn.6.h_ref, f32[1,1600]{1,0:T(1,128)} %squeeze.114.gain_ref, f32[1,1600]{1,0:T(1,128)} %squeeze.115.fin_ref, bf16[1600,8704]{1,0:T(8,128)(2,1)} %bitcast.168, bf16[4352,1600]{1,0:T(8,128)(2,1)} %bitcast.169), custom_call_target="tpu_custom_call" | custom-call | flops 42781900800 | bytes 41779200 | tf_op jit(solution)/shard_map/mlp/pallas_call | solution.py:251
  1086.4 71.0 %head.4 = f32[1024,128]{1,0:T(8,128)} custom-call(bf16[1024,1600]{1,0:T(8,128)(2,1)} %mlp.4.x_ref, bf16[1600,16000]{1,0:T(8,128)(2,1)} %bitcast.164, s32[1024,128]{1,0:T(8,128)} %broadcast_in_dim.191.tgt_ref), custom_call_target="tpu_custom_call" | custom-call | flops 52428800000 | bytes 54476800 | tf_op jit(solution)/shard_map/head/pallas_call | solution.py:374
  1159.7 38.2 %attn.7.h_ref = bf16[1024,1600]{1,0:T(8,128)(2,1)} custom-call(s32[1]{0:T(128)} %bitcast.14.core_ref, bf16[1024,1600]{1,0:T(8,128)(2,1)} %mlp.5.h_ref, f32[1,1600]{1,0:T(1,128)} %squeeze.120.gain_ref, f32[256,128]{1,0:T(8,128)} %bitcast.138, f32[256,128]{1,0:T(8,128)} %bitcast.142, bf16[1600,3904]{1,0:T(8,128)(2,1)} %all-gather.16.cloned.1.call-done.refs_0_), custom_call_target="tpu_custom_call" | custom-call | flops 12582912000 | bytes 12288000 | tf_op jit(solution)/shard_map/attn/pallas_call | solution.py:140
  1197.9 40.4 %gate_up.1.act_ref = bf16[1024,4352]{1,0:T(8,128)(2,1)} custom-call(bf16[1024,1600]{1,0:T(8,128)(2,1)} %attn.7.h_ref, f32[1,1600]{1,0:T(1,128)} %squeeze.124.gain_ref, bf16[1600,8704]{1,0:T(8,128)(2,1)} %bitcast.166, bf16[1600,8704]{1,0:T(8,128)(2,1)} %bitcast.167), custom_call_target="tpu_custom_call" | custom-call | flops 28521267200 | bytes 27852800 | tf_op jit(solution)/shard_map/gate_up/pallas_call | solution.py:294
  1238.3 26.9 %down.1 = bf16[1024,1600]{1,0:T(8,128)(2,1)} custom-call(bf16[1024,1600]{1,0:T(8,128)(2,1)} %attn.7.h_ref, bf16[1024,4352]{1,0:T(8,128)(2,1)} %gate_up.1.act_ref, bf16[4352,1600]{1,0:T(8,128)(2,1)} %all-gather.18.cloned.1.call-done.w_ref, f32[1,1600]{1,0:T(1,128)} %squeeze.115.fin_ref), custom_call_target="tpu_custom_call" | custom-call | flops 14260633600 | bytes 13926400 | tf_op jit(solution)/shard_map/down/pallas_call | solution.py:313
  1281.3 71.1 %head.5 = f32[1024,128]{1,0:T(8,128)} custom-call(bf16[1024,1600]{1,0:T(8,128)(2,1)} %copy.75.x_ref, bf16[1600,16000]{1,0:T(8,128)(2,1)} %bitcast.165, s32[1024,128]{1,0:T(8,128)} %broadcast_in_dim.192.tgt_ref), custom_call_target="tpu_custom_call" | custom-call | flops 52428800000 | bytes 54476800 | tf_op jit(solution)/shard_map/head/pallas_call | solution.py:374
  1357.1 73.0 %head.7 = f32[4096,128]{1,0:T(8,128)} custom-call(bf16[4096,1600]{1,0:T(8,128)(2,1)} %all-gather.22.cloned.1.call-done.x_ref, bf16[1600,4000]{1,0:T(8,128)(2,1)} %bitcast.173, s32[4096,128]{1,0:T(8,128)} %broadcast_in_dim.195.tgt_ref), custom_call_target="tpu_custom_call" | custom-call | flops 52428800000 | bytes 64307200 | tf_op jit(solution)/shard_map/head/pallas_call | solution.py:374
  1437.1 73.1 %head.6 = f32[4096,128]{1,0:T(8,128)} custom-call(bf16[4096,1600]{1,0:T(8,128)(2,1)} %all-gather.20.cloned.1.call-done.x_ref, bf16[1600,4000]{1,0:T(8,128)(2,1)} %bitcast.174, s32[4096,128]{1,0:T(8,128)} %broadcast_in_dim.194.tgt_ref), custom_call_target="tpu_custom_call" | custom-call | flops 52428800000 | bytes 64307200 | tf_op jit(solution)/shard_map/head/pallas_call | solution.py:374
  1514.3 13.2 all-gather.4
  (466 shorter events, 371.7 us)
Async XLA Ops:
  7.2 979.6 %all-gather.14.cloned.1.call-start = ((), (), s32[]{:S(2)}) async-start(), calls=%async_computation | async-start | bytes 14284800 | tf_op jit(solution)/shard_map/all_gather | solution.py:516
  13.4 1011.1 %all-gather.26.cloned.1.call-start = ((), (), s32[]{:S(2)}) async-start(), calls=%async_computation.6 | async-start | bytes 16293888 | tf_op jit(solution)/shard_map/all_gather | solution.py:516
  17.6 1006.9 %all-gather.24.cloned.1.call-start = ((), (), s32[]{:S(2)}) async-start(), calls=%async_computation.5 | async-start | bytes 31334400 | tf_op jit(solution)/shard_map/all_gather | solution.py:516
  24.6 1135.1 %all-gather.16.cloned.1.call-start = ((), (), s32[]{:S(2)}) async-start(), calls=%async_computation.1 | async-start | bytes 14284800 | tf_op jit(solution)/shard_map/all_gather | solution.py:516
  28.3 1169.6 %all-gather.28.cloned.1.call-start = ((), (), s32[]{:S(2)}) async-start(), calls=%async_computation.7 | async-start | bytes 31334400 | tf_op jit(solution)/shard_map/all_gather | solution.py:516
  28.9 1209.4 %all-gather.18.cloned.1.call-start = ((), (), s32[]{:S(2)}) async-start(), calls=%async_computation.2 | async-start | bytes 16293888 | tf_op jit(solution)/shard_map/all_gather | solution.py:516
  28.9 315.3 %collective-permute-start.18 = (bf16[2,800,8704]{2,1,0:T(8,128)(2,1)}, bf16[2,800,8704]{2,1,0:T(8,128)(2,1)}, u32[]{:S(2)}, u32[]{:S(2)}) collective-permute-start(bf16[2,800,8704]{2,1,0:T(8,128)(2,1)} %refs_0_.3), channel_id=1, source_target_pairs={{0,1},{1,0},{2,3},{3,2},{4,5},{5,4},{6,7},{7,6}} | collective-permute-start | bytes 83558408 | tf_op jit(solution)/shard_map/ppermute | solution.py:510
  29.9 314.4 %collective-permute-start.19 = (bf16[2,1600,2176]{2,1,0:T(8,128)(2,1)}, bf16[2,1600,2176]{2,1,0:T(8,128)(2,1)}, u32[]{:S(2)}, u32[]{:S(2)}) collective-permute-start(bf16[2,1600,2176]{2,1,0:T(8,128)(2,1)} %bitcast.170), channel_id=1, source_target_pairs={{0,1},{1,0},{2,3},{3,2},{4,5},{5,4},{6,7},{7,6}} | collective-permute-start | bytes 41779208 | tf_op jit(solution)/shard_map/ppermute | solution.py:510
  49.3 255.7 %collective-permute-start.17 = (bf16[2,800,3904]{2,1,0:T(8,128)(2,1)}, bf16[2,800,3904]{2,1,0:T(8,128)(2,1)}, u32[]{:S(2)}, u32[]{:S(2)}) collective-permute-start(bf16[2,800,3904]{2,1,0:T(8,128)(2,1)} %concatenate.58.refs_0_), channel_id=1, source_target_pairs={{0,1},{1,0},{2,3},{3,2},{4,5},{5,4},{6,7},{7,6}} | collective-permute-start | bytes 37478408 | tf_op jit(solution)/shard_map/ppermute | solution.py:510
  49.8 90.9 %collective-permute-start.14 = (s32[1024]{0:T(1024)S(1)}, s32[1024]{0:T(1024)S(1)}, u32[]{:S(2)}, u32[]{:S(2)}) collective-permute-start(s32[1024]{0:T(1024)S(1)} %reshape.647), channel_id=1, source_target_pairs={{0,1},{1,0},{2,3},{3,2},{4,5},{5,4},{6,7},{7,6}} | collective-permute-start | bytes 12296 | tf_op jit(solution)/shard_map/ppermute | solution.py:477
  139.9 111.7 %collective-permute-start.16 = (bf16[5,800]{1,0:T(8,128)(2,1)S(1)}, bf16[5,800]{1,0:T(8,128)(2,1)S(1)}, u32[]{:S(2)}, u32[]{:S(2)}) collective-permute-start(bf16[5,800]{1,0:T(8,128)(2,1)S(1)} %copy-done.22), channel_id=1, source_target_pairs={{0,1},{1,0},{2,3},{3,2},{4,5},{5,4},{6,7},{7,6}} | collective-permute-start | bytes 24008 | tf_op jit(solution)/shard_map/ppermute | solution.py:482
  200.3 96.1 %collective-permute-start.15 = (bf16[1024,1600]{0,1:T(8,128)(2,1)}, bf16[1024,1600]{0,1:T(8,128)(2,1)}, u32[]{:S(2)}, u32[]{:S(2)}) collective-permute-start(bf16[1024,1600]{0,1:T(8,128)(2,1)} %copy.69), channel_id=1, source_target_pairs={{0,1},{1,0},{2,3},{3,2},{4,5},{5,4},{6,7},{7,6}} | collective-permute-start | bytes 9830408 | tf_op jit(solution)/shard_map/ppermute | solution.py:480
  432.2 111.0 %collective-permute-start.22 = (bf16[192,1600]{1,0:T(8,128)(2,1)}, bf16[192,1600]{1,0:T(8,128)(2,1)}, u32[]{:S(2)}, u32[]{:S(2)}) collective-permute-start(bf16[192,1600]{1,0:T(8,128)(2,1)} %get-tuple-element.293), channel_id=1, source_target_pairs={{0,3},{1,2},{2,1},{3,0},{4,7},{5,6},{6,5},{7,4}} | collective-permute-start | bytes 1843208 | tf_op jit(solution)/shard_map/ppermute | solution.py:420
  432.4 110.8 %collective-permute-start.23 = (bf16[192,1600]{1,0:T(8,128)(2,1)}, bf16[192,1600]{1,0:T(8,128)(2,1)}, u32[]{:S(2)}, u32[]{:S(2)}) collective-permute-start(bf16[192,1600]{1,0:T(8,128)(2,1)} %get-tuple-element.294), channel_id=1, source_target_pairs={{0,4},{1,5},{2,6},{3,7},{4,0},{5,1},{6,2},{7,3}} | collective-permute-start | bytes 1843208 | tf_op jit(solution)/shard_map/ppermute | solution.py:420
  471.2 72.0 %collective-permute-start.24 = (bf16[192,1600]{1,0:T(8,128)(2,1)}, bf16[192,1600]{1,0:T(8,128)(2,1)}, u32[]{:S(2)}, u32[]{:S(2)}) collective-permute-start(bf16[192,1600]{1,0:T(8,128)(2,1)} %get-tuple-element.295), channel_id=1, source_target_pairs={{0,5},{1,4},{2,7},{3,6},{4,1},{5,0},{6,3},{7,2}} | collective-permute-start | bytes 1843208 | tf_op jit(solution)/shard_map/ppermute | solution.py:420
  472.3 70.9 %collective-permute-start.25 = (bf16[192,1600]{1,0:T(8,128)(2,1)}, bf16[192,1600]{1,0:T(8,128)(2,1)}, u32[]{:S(2)}, u32[]{:S(2)}) collective-permute-start(bf16[192,1600]{1,0:T(8,128)(2,1)} %get-tuple-element.296), channel_id=1, source_target_pairs={{0,6},{1,7},{2,4},{3,5},{4,2},{5,3},{6,0},{7,1}} | collective-permute-start | bytes 1843208 | tf_op jit(solution)/shard_map/ppermute | solution.py:420
  474.5 69.3 %collective-permute-start.26 = (bf16[192,1600]{1,0:T(8,128)(2,1)S(1)}, bf16[192,1600]{1,0:T(8,128)(2,1)}, u32[]{:S(2)}, u32[]{:S(2)}) collective-permute-start(bf16[192,1600]{1,0:T(8,128)(2,1)S(1)} %get-tuple-element.297), channel_id=1, source_target_pairs={{0,7},{1,6},{2,5},{3,4},{4,3},{5,2},{6,1},{7,0}} | collective-permute-start | bytes 1843208 | tf_op jit(solution)/shard_map/ppermute | solution.py:420
  543.1 811.0 %all-gather.22.cloned.1.call-start = ((), (), s32[]{:S(2)}) async-start(), calls=%async_computation.4 | async-start | bytes 15335424 | tf_op jit(solution)/shard_map/all_gather | solution.py:551
  584.7 56.0 %collective-permute-start.2 = (bf16[192,1600]{1,0:T(8,128)(2,1)S(1)}, bf16[192,1600]{1,0:T(8,128)(2,1)}, u32[]{:S(2)}, u32[]{:S(2)}) collective-permute-start(bf16[192,1600]{1,0:T(8,128)(2,1)S(1)} %get-tuple-element.558), channel_id=1, source_target_pairs={{0,3},{1,2},{2,1},{3,0},{4,7},{5,6},{6,5},{7,4}} | collective-permute-start | bytes 1843208 | tf_op jit(solution)/shard_map/while/body/ppermute | solution.py:420
  584.7 58.0 %collective-permute-start.3 = (bf16[192,1600]{1,0:T(8,128)(2,1)S(1)}, bf16[192,1600]{1,0:T(8,128)(2,1)}, u32[]{:S(2)}, u32[]{:S(2)}) collective-permute-start(bf16[192,1600]{1,0:T(8,128)(2,1)S(1)} %get-tuple-element.559), channel_id=1, source_target_pairs={{0,4},{1,5},{2,6},{3,7},{4,0},{5,1},{6,2},{7,3}} | collective-permute-start | bytes 1843208 | tf_op jit(solution)/shard_map/while/body/ppermute | solution.py:420
  586.0 58.7 %collective-permute-start.4 = (bf16[192,1600]{1,0:T(8,128)(2,1)S(1)}, bf16[192,1600]{1,0:T(8,128)(2,1)}, u32[]{:S(2)}, u32[]{:S(2)}) collective-permute-start(bf16[192,1600]{1,0:T(8,128)(2,1)S(1)} %get-tuple-element.560), channel_id=1, source_target_pairs={{0,5},{1,4},{2,7},{3,6},{4,1},{5,0},{6,3},{7,2}} | collective-permute-start | bytes 1843208 | tf_op jit(solution)/shard_map/while/body/ppermute | solution.py:420
  588.1 79.0 %collective-permute-start.5 = (bf16[192,1600]{1,0:T(8,128)(2,1)S(1)}, bf16[192,1600]{1,0:T(8,128)(2,1)S(1)}, u32[]{:S(2)}, u32[]{:S(2)}) collective-permute-start(bf16[192,1600]{1,0:T(8,128)(2,1)S(1)} %get-tuple-element.561), channel_id=1, source_target_pairs={{0,6},{1,7},{2,4},{3,5},{4,2},{5,3},{6,0},{7,1}} | collective-permute-start | bytes 1843208 | tf_op jit(solution)/shard_map/while/body/ppermute | solution.py:420
  613.9 66.2 %collective-permute-start.6 = (bf16[192,1600]{1,0:T(8,128)(2,1)S(1)}, bf16[192,1600]{1,0:T(8,128)(2,1)S(1)}, u32[]{:S(2)}, u32[]{:S(2)}) collective-permute-start(bf16[192,1600]{1,0:T(8,128)(2,1)S(1)} %get-tuple-element.562), channel_id=1, source_target_pairs={{0,7},{1,6},{2,5},{3,4},{4,3},{5,2},{6,1},{7,0}} | collective-permute-start | bytes 1843208 | tf_op jit(solution)/shard_map/while/body/ppermute | solution.py:420
  717.1 56.5 %collective-permute-start.4 = (bf16[192,1600]{1,0:T(8,128)(2,1)S(1)}, bf16[192,1600]{1,0:T(8,128)(2,1)}, u32[]{:S(2)}, u32[]{:S(2)}) collective-permute-start(bf16[192,1600]{1,0:T(8,128)(2,1)S(1)} %get-tuple-element.560), channel_id=1, source_target_pairs={{0,5},{1,4},{2,7},{3,6},{4,1},{5,0},{6,3},{7,2}} | collective-permute-start | bytes 1843208 | tf_op jit(solution)/shard_map/while/body/ppermute | solution.py:420
  719.7 55.9 %collective-permute-start.5 = (bf16[192,1600]{1,0:T(8,128)(2,1)S(1)}, bf16[192,1600]{1,0:T(8,128)(2,1)S(1)}, u32[]{:S(2)}, u32[]{:S(2)}) collective-permute-start(bf16[192,1600]{1,0:T(8,128)(2,1)S(1)} %get-tuple-element.561), channel_id=1, source_target_pairs={{0,6},{1,7},{2,4},{3,5},{4,2},{5,3},{6,0},{7,1}} | collective-permute-start | bytes 1843208 | tf_op jit(solution)/shard_map/while/body/ppermute | solution.py:420
  813.5 57.1 %collective-permute-start.4 = (bf16[192,1600]{1,0:T(8,128)(2,1)S(1)}, bf16[192,1600]{1,0:T(8,128)(2,1)}, u32[]{:S(2)}, u32[]{:S(2)}) collective-permute-start(bf16[192,1600]{1,0:T(8,128)(2,1)S(1)} %get-tuple-element.560), channel_id=1, source_target_pairs={{0,5},{1,4},{2,7},{3,6},{4,1},{5,0},{6,3},{7,2}} | collective-permute-start | bytes 1843208 | tf_op jit(solution)/shard_map/while/body/ppermute | solution.py:420
  816.4 56.1 %collective-permute-start.5 = (bf16[192,1600]{1,0:T(8,128)(2,1)S(1)}, bf16[192,1600]{1,0:T(8,128)(2,1)S(1)}, u32[]{:S(2)}, u32[]{:S(2)}) collective-permute-start(bf16[192,1600]{1,0:T(8,128)(2,1)S(1)} %get-tuple-element.561), channel_id=1, source_target_pairs={{0,6},{1,7},{2,4},{3,5},{4,2},{5,3},{6,0},{7,1}} | collective-permute-start | bytes 1843208 | tf_op jit(solution)/shard_map/while/body/ppermute | solution.py:420
  828.8 44.6 %collective-permute-start.6 = (bf16[192,1600]{1,0:T(8,128)(2,1)S(1)}, bf16[192,1600]{1,0:T(8,128)(2,1)S(1)}, u32[]{:S(2)}, u32[]{:S(2)}) collective-permute-start(bf16[192,1600]{1,0:T(8,128)(2,1)S(1)} %get-tuple-element.562), channel_id=1, source_target_pairs={{0,7},{1,6},{2,5},{3,4},{4,3},{5,2},{6,1},{7,0}} | collective-permute-start | bytes 1843208 | tf_op jit(solution)/shard_map/while/body/ppermute | solution.py:420
  910.5 56.5 %collective-permute-start.4 = (bf16[192,1600]{1,0:T(8,128)(2,1)S(1)}, bf16[192,1600]{1,0:T(8,128)(2,1)}, u32[]{:S(2)}, u32[]{:S(2)}) collective-permute-start(bf16[192,1600]{1,0:T(8,128)(2,1)S(1)} %get-tuple-element.560), channel_id=1, source_target_pairs={{0,5},{1,4},{2,7},{3,6},{4,1},{5,0},{6,3},{7,2}} | collective-permute-start | bytes 1843208 | tf_op jit(solution)/shard_map/while/body/ppermute | solution.py:420
  913.1 55.9 %collective-permute-start.5 = (bf16[192,1600]{1,0:T(8,128)(2,1)S(1)}, bf16[192,1600]{1,0:T(8,128)(2,1)S(1)}, u32[]{:S(2)}, u32[]{:S(2)}) collective-permute-start(bf16[192,1600]{1,0:T(8,128)(2,1)S(1)} %get-tuple-element.561), channel_id=1, source_target_pairs={{0,6},{1,7},{2,4},{3,5},{4,2},{5,3},{6,0},{7,1}} | collective-permute-start | bytes 1843208 | tf_op jit(solution)/shard_map/while/body/ppermute | solution.py:420
  980.9 284.4 %collective-permute-start.27 = (bf16[1024,1600]{0,1:T(8,128)(2,1)}, bf16[1024,1600]{0,1:T(8,128)(2,1)}, u32[]{:S(2)}, u32[]{:S(2)}) collective-permute-start(bf16[1024,1600]{0,1:T(8,128)(2,1)} %copy.74), channel_id=1, source_target_pairs={{0,1},{1,0},{2,3},{3,2},{4,5},{5,4},{6,7},{7,6}} | collective-permute-start | bytes 9830408 | tf_op jit(solution)/shard_map/ppermute | solution.py:530
  1269.3 164.8 %all-gather.20.cloned.1.call-start = ((), (), s32[]{:S(2)}) async-start(), calls=%async_computation.3 | async-start | bytes 15335424 | tf_op jit(solution)/shard_map/all_gather | solution.py:551
  (60 other events, 1356.2 us)
Sparse Core Ops, SparseCore 0:
  13.5 70.5 all-gather.13
  85.9 74.4 all-gather.25
  162.3 132.7 all-gather.23
  296.7 66.9 all-gather.15
  365.3 185.7 all-gather.27
  552.8 112.8 all-gather.17
  1269.4 70.2 all-gather.21
  1341.5 70.8 all-gather.19

commit v3 on v2

--- a/solution.py
+++ b/solution.py
@@ -30,6 +30,7 @@
 TB = 256
 SUB = 128
 FT = 256
+RT = 640
 VT = 2048
 HT = 512
 
@@ -404,6 +405,27 @@
     return dot(flags.astype(BF16), upper).astype(jnp.int32)
 
 
+def relayout_kernel(w_ref, out_ref):
+    for at in range(0, RT, 256):
+        n = min(256, RT - at)
+        eye = (lax.broadcasted_iota(jnp.int32, (n, n), 0) == lax.broadcasted_iota(jnp.int32, (n, n), 1)).astype(BF16)
+        out_ref[at:at + n, :] = dot_nt(eye, w_ref[:, at:at + n]).astype(BF16)
+
+
+def row_major(table_t):
+    v = table_t.shape[1]
+    return pl.pallas_call(
+        relayout_kernel,
+        out_shape=jax.ShapeDtypeStruct((v, D), BF16),
+        grid=(v // RT,),
+        in_specs=[pl.BlockSpec((D, RT), lambda j: (0, j))],
+        out_specs=pl.BlockSpec((RT, D), lambda j: (j, 0)),
+        compiler_params=pltpu.CompilerParams(vmem_limit_bytes=VMEM_LIMIT),
+        cost_estimate=pl.CostEstimate(flops=2 * v * D * 256, bytes_accessed=4 * v * D, transcendentals=0),
+        name="row_major",
+    )(table_t)
+
+
 def embed_send(table, toks, me, cap, r):
     size, vocab = toks.shape[0], table.shape[0]
     local = toks - me * vocab
@@ -476,9 +498,12 @@
         tok = tokens.reshape(t)
         tok_pair = jnp.stack([tok, lax.ppermute(tok, 'fsdp', swap)])
         local = tok_pair - core * p_embed.shape[0]
-        looked = jnp.take(p_embed, jnp.clip(local, 0, p_embed.shape[0] - 1), axis=0)
-        from_peer = lax.ppermute(looked[1], 'fsdp', swap)
-        h = jnp.where(((local[0] >= 0) & (local[0] < p_embed.shape[0]))[:, None], looked[0], from_peer)
+        index = jnp.clip(local, 0, p_embed.shape[0] - 1)
+        table = row_major(p_embed.T)
+        for_peer = jnp.take(table, index[1], axis=0)
+        from_peer = lax.ppermute(for_peer, 'fsdp', swap)
+        index, for_peer = lax.optimization_barrier((index[0], for_peer))
+        for_own = jnp.take(table, index, axis=0)
         p_gains = jnp.stack([p_norms, lax.ppermute(p_norms, 'fsdp', swap)]).astype(F32)
         p_gains = jnp.where(core == 0, p_gains, p_gains[::-1])
         p_gains = jnp.swapaxes(p_gains, 0, 1).reshape(2 * layers + 1, 1, D)
@@ -520,15 +545,14 @@
             return mlp_block(h, p_gains[2 * layer + 1], p_gains[2 * layers], p_wgu, p_wdn, layer, layer == layers - 1, core_arr)
 
         r_full = [ref_weights(0, r_dn[0])]
+        cap = 192
+        order, for_own = lax.optimization_barrier((order, for_own))
+        for_own, got = lax.optimization_barrier((for_own, embed_send(r_embed, order, me, cap, 0)))
+        got = embed_swap(got, xors, both)
+        h = jnp.where(((local[0] >= 0) & (local[0] < p_embed.shape[0]))[:, None], for_own, from_peer)
         h = policy_layer(h, 0)
-        order, dn, h = lax.optimization_barrier((order, r_dn[1], h))
+        got, dn, h = lax.optimization_barrier((got, r_dn[1], h))
         r_full.append(ref_weights(1, dn))
-        cap = 192
-        h, got = lax.optimization_barrier((h, embed_send(r_embed, order, me, cap, 0)))
-        got = embed_swap(got, xors, both)
-        x = policy_layer(h, 1)
-        x_peer = lax.ppermute(x, 'fsdp', swap)
-        got, x = lax.optimization_barrier((got, x))
         h_ref = embed_pick(got, tok, r_embed.shape[0], me, cap, 0)
         counts = jnp.sum((tok_all[:, None, :] // r_embed.shape[0]) == jnp.arange(n_dev)[None, :, None], axis=2)
         h_ref = lax.fori_loop(1, (jnp.max(counts) + cap - 1) // cap, lambda r, acc: acc + embed_pick(
@@ -536,11 +560,13 @@
         tgt_own = tgt_all[me] - core * p_head.shape[1]
         tgt_peer = tgt_all[jnp.bitwise_xor(me, 1)] - core * p_head.shape[1]
 
-        h_ref, x = lax.optimization_barrier((h_ref, x))
+        h_ref, h = lax.optimization_barrier((h_ref, h))
         att, w_gu, w_dn = r_full[0]
         h_ref = attention_block(h_ref, r_gains[0], tabs, [att], None, core_arr)
         h_ref = mlp_block(h_ref, r_gains[1], r_gains[2 * layers], [w_gu], [w_dn], None, False, core_arr)
-        x, h_ref = lax.optimization_barrier((x, h_ref))
+        h, h_ref = lax.optimization_barrier((h, h_ref))
+        x = policy_layer(h, 1)
+        x_peer = lax.ppermute(x, 'fsdp', swap)
         own = head_block(x, p_head, tgt_own)
         h_ref, own = lax.optimization_barrier((h_ref, own))
         att, w_gu, w_dn = r_full[1]

time: 1560 us -> 1580 us (1.013)
  local copies, waits for them, and re-layouts: 404 us -> 336 us
  Pallas kernels: 693 us -> 743 us
  waiting for transfers between devices: 235 us -> 264 us
    unnamed x75 -> x76, local copies, waits for them, and re-layouts: 101 us -> 31.1 us
    ppermute x1, starting transfers between devices: 0.87 us -> 52.2 us  [device_step(): lax.ppermute(p_norms, 'fsdp', swap)]
    ppermute x1, starting transfers between devices: 51.2 us -> 0.01 us  [device_step(): from_peer = lax.ppermute(for_peer, 'fsdp', swap)]
    pallas_call x0 -> x1, Pallas kernels: none -> 51 us  [row_major(): pl.pallas_call(relayout_kernel, out_shape=jax.ShapeDtypeStruct((v, D), BF...]
    ppermute x35, waiting for transfers between devices: 214 us -> 257 us  [embed_swap(): lax.ppermute(rows[k], axis, perms[k])]
    gather x1 -> x2, local copies, waits for them, and re-layouts: 49 us -> 49 us  [the longest x1 25.1 us: device_step(): for_own = jnp.take(table, index, axis=0)]
  transfers between devices with their start and end apart: 57 -> 57, of which waited for: 21 -> 21; matrix products, arithmetic and copies ran while one was open for 30% -> 25% of each run, Pallas kernels for 40% -> 43%
where the time goes in v3:
time: 1580 us; the launch traced here: 1560 us
  Pallas kernels  743 us (47%)
  local copies, waits for them, and re-layouts  336 us (21%)
  waiting for transfers between devices  264 us (17%)
  starting transfers between devices  94.6 us (6%)
  other arithmetic  48.5 us (3%)
  matrix products  41.8 us (3%)
  between operations  17.7 us (1%)
    pallas_call x4, Pallas kernels, head_block(): pl.pallas_call(functools.partial(head_kernel, v), out_shape=jax.ShapeDtyp...  288 us
    ppermute x35, waiting for transfers between devices, embed_swap(): lax.ppermute(rows[k], axis, perms[k])  257 us
    pallas_call x3, Pallas kernels, mlp_block(): pl.pallas_call(functools.partial(mlp_kernel, n, layer, last), out_shape=j...  184 us
    pallas_call x4, Pallas kernels, attention_block(): pl.pallas_call(functools.partial(attn_kernel, n, layer), out_shape=jax.Sh...  152 us
    gather x5, local copies, waits for them, and re-layouts, embed_send(): rows = jnp.take(table, idx.reshape(-1), axis=0).reshape(size, cap, D)  87.4 us
    ppermute x1, starting transfers between devices, device_step(): lax.ppermute(p_norms, 'fsdp', swap)  52.2 us
    pallas_call x1, Pallas kernels, row_major(): pl.pallas_call(relayout_kernel, out_shape=jax.ShapeDtypeStruct((v, D), BF...  51 us
    while x40, local copies, waits for them, and re-layouts  50.1 us
  transfers between devices with their start and end apart: 57, of which 21 were waited for; matrix products, arithmetic and copies ran while one was open for 25% of the time, Pallas kernels for 43%

profile of v3, /device:TPU:0, one launch (start us, length us, event | category | flops | bytes accessed | tf_op | source)
XLA Modules:
  0.0 1562.4 jit_solution(4971130622892445487)
XLA Ops:
  30.1 19.2 %concatenate.49.refs_0_ = bf16[2,800,3904]{2,1,0:T(8,128)(2,1)} concatenate(bf16[2,800,1600]{2,1,0:T(8,128)(2,1)} %param.30, bf16[2,800,640]{2,1,0:T(8,128)(2,1)S(1)} %copy-done.3, bf16[2,800,64]{2,1,0:T(8,128)(2,1)S(1)} %broadcast_in_dim.187, bf16[2,800,1600]{2,1,0:T(8,128)(2,1)} %param.32), dimensions={2} | concatenate | bytes 24985600 | tf_op jit(solution)/shard_map/concatenate | solution.py:530
  51.5 51.0 %row_major.1 = bf16[16000,1600]{1,0:T(8,128)(2,1)} custom-call(bf16[1600,16000]{1,0:T(8,128)(2,1)} %bitcast.114), custom_call_target="tpu_custom_call" | custom-call | flops 13107200000 | bytes 102400000 | tf_op jit(solution)/shard_map/row_major/pallas_call | solution.py:417
  102.6 18.2 %copy.64 = bf16[4000,1600]{1,0:T(8,128)(2,1)} copy(bf16[4000,1600]{0,1:T(8,128)(2,1)} %param.44) | data formatting | bytes 25600000 | tf_op args[19]
  126.6 23.9 %gather_fusion.3 = bf16[1024,1600]{1,0:T(8,128)(2,1)} fusion(bf16[16000,1600]{1,0:T(8,128)(2,1)} %row_major.1, s32[1024]{0:T(1024)S(1)} %fusion.45), kind=kCustom, calls=%fused_computation.clone | custom fusion | bytes 6557696 | tf_op jit(solution)/shard_map/jit(_take)/gather | solution.py:503
  152.9 25.1 %gather_fusion.4 = bf16[1024,1600]{1,0:T(8,128)(2,1)} fusion(bf16[16000,1600]{1,0:T(8,128)(2,1)} %row_major.1, s32[1024]{0:T(1024)S(1)} %fusion.46), kind=kCustom, calls=%fused_computation.2.clone | custom fusion | bytes 6557696 | tf_op jit(solution)/shard_map/jit(_take)/gather | solution.py:506
  182.2 52.2 %collective-permute-start.23 = (bf16[5,800]{1,0:T(8,128)(2,1)S(1)}, bf16[5,800]{1,0:T(8,128)(2,1)}, u32[]{:S(2)}, u32[]{:S(2)}) collective-permute-start(bf16[5,800]{1,0:T(8,128)(2,1)S(1)} %copy-done.22), channel_id=1, source_target_pairs={{0,1},{1,0},{2,3},{3,2},{4,5},{5,4},{6,7},{7,6}} | collective-permute-start | bytes 24008 | tf_op jit(solution)/shard_map/ppermute | solution.py:507
  263.6 18.0 %gather_fusion.1 = bf16[1536,1600]{1,0:T(8,128)(2,1)} fusion(bf16[4000,1600]{1,0:T(8,128)(2,1)} %copy.64, s32[2048]{0:T(1024)S(1)} %pad_clamp_fusion.1), kind=kCustom, calls=%fused_computation.3 | custom fusion | bytes 9836544 | tf_op jit(solution)/shard_map/jit(_take)/gather | solution.py:437
  304.2 38.4 %attn.4.h_ref = bf16[1024,1600]{1,0:T(8,128)(2,1)} custom-call(s32[1]{0:T(128)} %bitcast.18.core_ref, bf16[1024,1600]{1,0:T(8,128)(2,1)} %broadcast_select_fusion.4.h_ref, f32[1,1600]{1,0:T(1,128)} %squeeze.105.gain_ref, f32[256,128]{1,0:T(8,128)} %bitcast.129, f32[256,128]{1,0:T(8,128)} %bitcast.133, bf16[2,800,3904]{2,1,0:T(8,128)(2,1)} %concatenate.49.refs_0_, ...), custom_call_target="tpu_custom_call" | custom-call | flops 12582912000 | bytes 12288000 | tf_op jit(solution)/shard_map/attn/pallas_call | solution.py:141
  347.4 61.2 %mlp.3.h_ref = bf16[1024,1600]{1,0:T(8,128)(2,1)} custom-call(s32[1]{0:T(128)} %bitcast.18.core_ref, bf16[1024,1600]{1,0:T(8,128)(2,1)} %attn.4.h_ref, f32[1,1600]{1,0:T(1,128)} %squeeze.106.gain_ref, f32[1,1600]{1,0:T(1,128)} %squeeze.107.fin_ref, bf16[2,800,8704]{2,1,0:T(8,128)(2,1)} %refs_0_.3, bf16[2,800,8704]{2,1,0:T(8,128)(2,1)} %collective-permute-done.25.refs_1_, ...), custom_call_target="tpu_custom_call" | custom-call | flops 42781900800 | bytes 41779200 | tf_op jit(solution)/shard_map/mlp/pallas_call | solution.py:252
  408.7 20.0 %collective-permute-done.19 = bf16[192,1600]{1,0:T(8,128)(2,1)} collective-permute-done((bf16[192,1600]{1,0:T(8,128)(2,1)}, bf16[192,1600]{1,0:T(8,128)(2,1)}, u32[]{:S(2)}, u32[]{:S(2)}) %collective-permute-start.19) | collective-permute-done | bytes 614432 | tf_op jit(solution)/shard_map/ppermute | solution.py:442
  444.3 450.5 %while.16 = (s32[]{:T(128)}, bf16[1024,1600]{0,1:T(8,128)(2,1)}, s32[]{:T(128)}, s32[1,1024]{1,0:T(1,128)S(1)}, s32[1024]{0:T(1024)S(1)}, /*index=5*/s32[]{:T(12...) while((s32[]{:T(128)}, bf16[1024,1600]{0,1:T(8,128)(2,1)}, ...), condition=%wide.region_5.7_spmd, body=%wide.region_3.6_spmd.sunk | while | flops 5066265600 | bytes 96910400 | solution.py:558
  446.0 17.4 %gather_fusion = bf16[1536,1600]{1,0:T(8,128)(2,1)} fusion(bf16[4000,1600]{1,0:T(8,128)(2,1)} %get-tuple-element.601, s32[2048]{0:T(1024)S(1)} %pad_clamp_fusion.4), kind=kCustom, calls=%fused_computation.1.clone.1 | custom fusion | bytes 9836544 | tf_op jit(solution)/shard_map/while/body/jit(_take)/gather | solution.py:437
  476.2 18.1 %collective-permute-done.1 = bf16[192,1600]{1,0:T(8,128)(2,1)} collective-permute-done((bf16[192,1600]{1,0:T(8,128)(2,1)}, bf16[192,1600]{1,0:T(8,128)(2,1)}, u32[]{:S(2)}, u32[]{:S(2)}) %collective-permute-start.1) | collective-permute-done | bytes 614432 | tf_op jit(solution)/shard_map/while/body/ppermute | solution.py:442
  497.3 22.1 %collective-permute-done.2 = bf16[192,1600]{1,0:T(8,128)(2,1)} collective-permute-done((bf16[192,1600]{1,0:T(8,128)(2,1)S(1)}, bf16[192,1600]{1,0:T(8,128)(2,1)}, u32[]{:S(2)}, u32[]{:S(2)}) %collective-permute-start.2) | collective-permute-done | bytes 614432 | tf_op jit(solution)/shard_map/while/body/ppermute | solution.py:442
  525.4 22.8 %collective-permute-done.5 = bf16[192,1600]{1,0:T(8,128)(2,1)S(1)} collective-permute-done((bf16[192,1600]{1,0:T(8,128)(2,1)S(1)}, bf16[192,1600]{1,0:T(8,128)(2,1)S(1)}, u32[]{:S(2)}, u32[]{:S(2)}) %collective-permute-start.5) | collective-permute-done | bytes 614432 | tf_op jit(solution)/shard_map/while/body/ppermute | solution.py:442
  549.0 25.9 %collective-permute-done.6 = bf16[192,1600]{1,0:T(8,128)(2,1)S(1)} collective-permute-done((bf16[192,1600]{1,0:T(8,128)(2,1)S(1)}, bf16[192,1600]{1,0:T(8,128)(2,1)S(1)}, u32[]{:S(2)}, u32[]{:S(2)}) %collective-permute-start.6) | collective-permute-done | bytes 614432 | tf_op jit(solution)/shard_map/while/body/ppermute | solution.py:442
  587.5 17.4 %gather_fusion = bf16[1536,1600]{1,0:T(8,128)(2,1)} fusion(bf16[4000,1600]{1,0:T(8,128)(2,1)} %get-tuple-element.601, s32[2048]{0:T(1024)S(1)} %pad_clamp_fusion.4), kind=kCustom, calls=%fused_computation.1.clone.1 | custom fusion | bytes 9836544 | tf_op jit(solution)/shard_map/while/body/jit(_take)/gather | solution.py:437
  632.5 23.9 %collective-permute-done.2 = bf16[192,1600]{1,0:T(8,128)(2,1)} collective-permute-done((bf16[192,1600]{1,0:T(8,128)(2,1)S(1)}, bf16[192,1600]{1,0:T(8,128)(2,1)}, u32[]{:S(2)}, u32[]{:S(2)}) %collective-permute-start.2) | collective-permute-done | bytes 614432 | tf_op jit(solution)/shard_map/while/body/ppermute | solution.py:442
  698.9 17.4 %gather_fusion = bf16[1536,1600]{1,0:T(8,128)(2,1)} fusion(bf16[4000,1600]{1,0:T(8,128)(2,1)} %get-tuple-element.601, s32[2048]{0:T(1024)S(1)} %pad_clamp_fusion.4), kind=kCustom, calls=%fused_computation.1.clone.1 | custom fusion | bytes 9836544 | tf_op jit(solution)/shard_map/while/body/jit(_take)/gather | solution.py:437
  799.3 17.4 %gather_fusion = bf16[1536,1600]{1,0:T(8,128)(2,1)} fusion(bf16[4000,1600]{1,0:T(8,128)(2,1)} %get-tuple-element.601, s32[2048]{0:T(1024)S(1)} %pad_clamp_fusion.4), kind=kCustom, calls=%fused_computation.1.clone.1 | custom fusion | bytes 9836544 | tf_op jit(solution)/shard_map/while/body/jit(_take)/gather | solution.py:437
  855.4 25.2 %collective-permute-done.4 = bf16[192,1600]{1,0:T(8,128)(2,1)} collective-permute-done((bf16[192,1600]{1,0:T(8,128)(2,1)S(1)}, bf16[192,1600]{1,0:T(8,128)(2,1)}, u32[]{:S(2)}, u32[]{:S(2)}) %collective-permute-start.4) | collective-permute-done | bytes 614432 | tf_op jit(solution)/shard_map/while/body/ppermute | solution.py:442
  900.2 37.7 %attn.5.h_ref = bf16[1024,1600]{1,0:T(8,128)(2,1)} custom-call(s32[1]{0:T(128)} %bitcast.18.core_ref, bf16[1024,1600]{1,0:T(8,128)(2,1)} %copy.68.h_ref, f32[1,1600]{1,0:T(1,128)} %squeeze.108.gain_ref, f32[256,128]{1,0:T(8,128)} %bitcast.130, f32[256,128]{1,0:T(8,128)} %bitcast.134, bf16[1600,3904]{1,0:T(8,128)(2,1)} %all-gather.14.cloned.1.call-done.refs_0_), custom_call_target="tpu_custom_call" | custom-call | flops 12582912000 | bytes 12288000 | tf_op jit(solution)/shard_map/attn/pallas_call | solution.py:141
  938.0 60.8 %mlp.4.h_ref = bf16[1024,1600]{1,0:T(8,128)(2,1)} custom-call(s32[1]{0:T(128)} %bitcast.18.core_ref, bf16[1024,1600]{1,0:T(8,128)(2,1)} %attn.5.h_ref, f32[1,1600]{1,0:T(1,128)} %squeeze.112.gain_ref, f32[1,1600]{1,0:T(1,128)} %squeeze.113.fin_ref, bf16[1600,8704]{1,0:T(8,128)(2,1)} %bitcast.163, bf16[4352,1600]{1,0:T(8,128)(2,1)} %bitcast.164), custom_call_target="tpu_custom_call" | custom-call | flops 42781900800 | bytes 41779200 | tf_op jit(solution)/shard_map/mlp/pallas_call | solution.py:252
  998.8 38.2 %attn.6.h_ref = bf16[1024,1600]{1,0:T(8,128)(2,1)} custom-call(s32[1]{0:T(128)} %bitcast.18.core_ref, bf16[1024,1600]{1,0:T(8,128)(2,1)} %mlp.3.h_ref, f32[1,1600]{1,0:T(1,128)} %squeeze.116.gain_ref, f32[256,128]{1,0:T(8,128)} %bitcast.131, f32[256,128]{1,0:T(8,128)} %bitcast.135, bf16[2,800,3904]{2,1,0:T(8,128)(2,1)} %concatenate.49.refs_0_, ...), custom_call_target="tpu_custom_call" | custom-call | flops 12582912000 | bytes 12288000 | tf_op jit(solution)/shard_map/attn/pallas_call | solution.py:141
  1037.0 62.1 %mlp.5.x_ref = bf16[1024,1600]{1,0:T(8,128)(2,1)} custom-call(s32[1]{0:T(128)} %bitcast.18.core_ref, bf16[1024,1600]{1,0:T(8,128)(2,1)} %attn.6.h_ref, f32[1,1600]{1,0:T(1,128)} %squeeze.117.gain_ref, f32[1,1600]{1,0:T(1,128)} %squeeze.107.fin_ref, bf16[2,800,8704]{2,1,0:T(8,128)(2,1)} %refs_0_.3, bf16[2,800,8704]{2,1,0:T(8,128)(2,1)} %collective-permute-done.25.refs_1_, ...), custom_call_target="tpu_custom_call" | custom-call | flops 42781900800 | bytes 41779200 | tf_op jit(solution)/shard_map/mlp/pallas_call | solution.py:252
  1105.6 70.9 %head.4 = f32[1024,128]{1,0:T(8,128)} custom-call(bf16[1024,1600]{1,0:T(8,128)(2,1)} %mlp.5.x_ref, bf16[1600,16000]{1,0:T(8,128)(2,1)} %bitcast.159, s32[1024,128]{1,0:T(8,128)} %broadcast_in_dim.188.tgt_ref), custom_call_target="tpu_custom_call" | custom-call | flops 52428800000 | bytes 54476800 | tf_op jit(solution)/shard_map/head/pallas_call | solution.py:375
  1178.8 38.0 %attn.7.h_ref = bf16[1024,1600]{1,0:T(8,128)(2,1)} custom-call(s32[1]{0:T(128)} %bitcast.18.core_ref, bf16[1024,1600]{1,0:T(8,128)(2,1)} %mlp.4.h_ref, f32[1,1600]{1,0:T(1,128)} %squeeze.120.gain_ref, f32[256,128]{1,0:T(8,128)} %bitcast.132, f32[256,128]{1,0:T(8,128)} %bitcast.136, bf16[1600,3904]{1,0:T(8,128)(2,1)} %all-gather.16.cloned.1.call-done.refs_0_), custom_call_target="tpu_custom_call" | custom-call | flops 12582912000 | bytes 12288000 | tf_op jit(solution)/shard_map/attn/pallas_call | solution.py:141
  1216.8 40.4 %gate_up.1.act_ref = bf16[1024,4352]{1,0:T(8,128)(2,1)} custom-call(bf16[1024,1600]{1,0:T(8,128)(2,1)} %attn.7.h_ref, f32[1,1600]{1,0:T(1,128)} %squeeze.124.gain_ref, bf16[1600,8704]{1,0:T(8,128)(2,1)} %bitcast.161, bf16[1600,8704]{1,0:T(8,128)(2,1)} %bitcast.162), custom_call_target="tpu_custom_call" | custom-call | flops 28521267200 | bytes 27852800 | tf_op jit(solution)/shard_map/gate_up/pallas_call | solution.py:295
  1257.2 27.0 %down.1 = bf16[1024,1600]{1,0:T(8,128)(2,1)} custom-call(bf16[1024,1600]{1,0:T(8,128)(2,1)} %attn.7.h_ref, bf16[1024,4352]{1,0:T(8,128)(2,1)} %gate_up.1.act_ref, bf16[4352,1600]{1,0:T(8,128)(2,1)} %all-gather.18.cloned.1.call-done.w_ref, f32[1,1600]{1,0:T(1,128)} %squeeze.113.fin_ref), custom_call_target="tpu_custom_call" | custom-call | flops 14260633600 | bytes 13926400 | tf_op jit(solution)/shard_map/down/pallas_call | solution.py:314
  1300.6 71.1 %head.5 = f32[1024,128]{1,0:T(8,128)} custom-call(bf16[1024,1600]{1,0:T(8,128)(2,1)} %copy.70.x_ref, bf16[1600,16000]{1,0:T(8,128)(2,1)} %bitcast.160, s32[1024,128]{1,0:T(8,128)} %broadcast_in_dim.189.tgt_ref), custom_call_target="tpu_custom_call" | custom-call | flops 52428800000 | bytes 54476800 | tf_op jit(solution)/shard_map/head/pallas_call | solution.py:375
  1376.4 73.2 %head.7 = f32[4096,128]{1,0:T(8,128)} custom-call(bf16[4096,1600]{1,0:T(8,128)(2,1)} %all-gather.22.cloned.1.call-done.x_ref, bf16[1600,4000]{1,0:T(8,128)(2,1)} %bitcast.168, s32[4096,128]{1,0:T(8,128)} %broadcast_in_dim.192.tgt_ref), custom_call_target="tpu_custom_call" | custom-call | flops 52428800000 | bytes 64307200 | tf_op jit(solution)/shard_map/head/pallas_call | solution.py:375
  1456.5 73.0 %head.6 = f32[4096,128]{1,0:T(8,128)} custom-call(bf16[4096,1600]{1,0:T(8,128)(2,1)} %all-gather.20.cloned.1.call-done.x_ref, bf16[1600,4000]{1,0:T(8,128)(2,1)} %bitcast.169, s32[4096,128]{1,0:T(8,128)} %broadcast_in_dim.191.tgt_ref), custom_call_target="tpu_custom_call" | custom-call | flops 52428800000 | bytes 64307200 | tf_op jit(solution)/shard_map/head/pallas_call | solution.py:375
  (471 shorter events, 416.9 us)
Async XLA Ops:
  7.2 893.1 %all-gather.14.cloned.1.call-start = ((), (), s32[]{:S(2)}) async-start(), calls=%async_computation | async-start | bytes 14284800 | tf_op jit(solution)/shard_map/all_gather | solution.py:541
  13.4 924.5 %all-gather.26.cloned.1.call-start = ((), (), s32[]{:S(2)}) async-start(), calls=%async_computation.6 | async-start | bytes 16293888 | tf_op jit(solution)/shard_map/all_gather | solution.py:541
  17.6 920.4 %all-gather.24.cloned.1.call-start = ((), (), s32[]{:S(2)}) async-start(), calls=%async_computation.5 | async-start | bytes 31334400 | tf_op jit(solution)/shard_map/all_gather | solution.py:541
  24.6 1154.2 %all-gather.16.cloned.1.call-start = ((), (), s32[]{:S(2)}) async-start(), calls=%async_computation.1 | async-start | bytes 14284800 | tf_op jit(solution)/shard_map/all_gather | solution.py:541
  28.3 1188.6 %all-gather.28.cloned.1.call-start = ((), (), s32[]{:S(2)}) async-start(), calls=%async_computation.7 | async-start | bytes 31334400 | tf_op jit(solution)/shard_map/all_gather | solution.py:541
  28.9 1228.4 %all-gather.18.cloned.1.call-start = ((), (), s32[]{:S(2)}) async-start(), calls=%async_computation.2 | async-start | bytes 16293888 | tf_op jit(solution)/shard_map/all_gather | solution.py:541
  28.9 317.0 %collective-permute-start.25 = (bf16[2,800,8704]{2,1,0:T(8,128)(2,1)}, bf16[2,800,8704]{2,1,0:T(8,128)(2,1)}, u32[]{:S(2)}, u32[]{:S(2)}) collective-permute-start(bf16[2,800,8704]{2,1,0:T(8,128)(2,1)} %refs_0_.3), channel_id=1, source_target_pairs={{0,1},{1,0},{2,3},{3,2},{4,5},{5,4},{6,7},{7,6}} | collective-permute-start | bytes 83558408 | tf_op jit(solution)/shard_map/ppermute | solution.py:535
  30.0 96.5 %collective-permute-start.14 = (s32[1024]{0:T(1024)S(1)}, s32[1024]{0:T(1024)S(1)}, u32[]{:S(2)}, u32[]{:S(2)}) collective-permute-start(s32[1024]{0:T(1024)S(1)} %reshape.597), channel_id=1, source_target_pairs={{0,1},{1,0},{2,3},{3,2},{4,5},{5,4},{6,7},{7,6}} | collective-permute-start | bytes 12296 | tf_op jit(solution)/shard_map/ppermute | solution.py:499
  49.3 253.5 %collective-permute-start.24 = (bf16[2,800,3904]{2,1,0:T(8,128)(2,1)}, bf16[2,800,3904]{2,1,0:T(8,128)(2,1)}, u32[]{:S(2)}, u32[]{:S(2)}) collective-permute-start(bf16[2,800,3904]{2,1,0:T(8,128)(2,1)} %concatenate.49.refs_0_), channel_id=1, source_target_pairs={{0,1},{1,0},{2,3},{3,2},{4,5},{5,4},{6,7},{7,6}} | collective-permute-start | bytes 37478408 | tf_op jit(solution)/shard_map/ppermute | solution.py:535
  49.8 295.5 %collective-permute-start.26 = (bf16[2,1600,2176]{2,1,0:T(8,128)(2,1)}, bf16[2,1600,2176]{2,1,0:T(8,128)(2,1)}, u32[]{:S(2)}, u32[]{:S(2)}) collective-permute-start(bf16[2,1600,2176]{2,1,0:T(8,128)(2,1)} %bitcast.165), channel_id=1, source_target_pairs={{0,1},{1,0},{2,3},{3,2},{4,5},{5,4},{6,7},{7,6}} | collective-permute-start | bytes 41779208 | tf_op jit(solution)/shard_map/ppermute | solution.py:535
  123.1 116.7 %collective-permute-start.11 = (f32[40,128]{1,0:T(8,128)S(1)}, f32[40,128]{1,0:T(8,128)S(1)}, u32[]{:S(2)}, u32[]{:S(2)}) collective-permute-start(f32[40,128]{1,0:T(8,128)S(1)} %get-tuple-element.474), channel_id=1, source_target_pairs={{0,5},{1,4},{2,7},{3,6},{4,1},{5,0},{6,3},{7,2}} | collective-permute-start | bytes 61448 | tf_op jit(solution)/shard_map/ppermute | solution.py:514
  182.2 56.4 %collective-permute-start.23 = (bf16[5,800]{1,0:T(8,128)(2,1)S(1)}, bf16[5,800]{1,0:T(8,128)(2,1)}, u32[]{:S(2)}, u32[]{:S(2)}) collective-permute-start(bf16[5,800]{1,0:T(8,128)(2,1)S(1)} %copy-done.22), channel_id=1, source_target_pairs={{0,1},{1,0},{2,3},{3,2},{4,5},{5,4},{6,7},{7,6}} | collective-permute-start | bytes 24008 | tf_op jit(solution)/shard_map/ppermute | solution.py:507
  292.9 50.2 %collective-permute-start.15 = (bf16[192,1600]{1,0:T(8,128)(2,1)}, bf16[192,1600]{1,0:T(8,128)(2,1)}, u32[]{:S(2)}, u32[]{:S(2)}) collective-permute-start(bf16[192,1600]{1,0:T(8,128)(2,1)} %get-tuple-element.294), channel_id=1, source_target_pairs={{0,1},{1,0},{2,3},{3,2},{4,5},{5,4},{6,7},{7,6}} | collective-permute-start | bytes 1843208 | tf_op jit(solution)/shard_map/ppermute | solution.py:442
  342.6 66.1 %collective-permute-start.17 = (bf16[192,1600]{1,0:T(8,128)(2,1)}, bf16[192,1600]{1,0:T(8,128)(2,1)}, u32[]{:S(2)}, u32[]{:S(2)}) collective-permute-start(bf16[192,1600]{1,0:T(8,128)(2,1)} %get-tuple-element.296), channel_id=1, source_target_pairs={{0,3},{1,2},{2,1},{3,0},{4,7},{5,6},{6,5},{7,4}} | collective-permute-start | bytes 1843208 | tf_op jit(solution)/shard_map/ppermute | solution.py:442
  343.0 65.7 %collective-permute-start.18 = (bf16[192,1600]{1,0:T(8,128)(2,1)}, bf16[192,1600]{1,0:T(8,128)(2,1)}, u32[]{:S(2)}, u32[]{:S(2)}) collective-permute-start(bf16[192,1600]{1,0:T(8,128)(2,1)} %get-tuple-element.297), channel_id=1, source_target_pairs={{0,4},{1,5},{2,6},{3,7},{4,0},{5,1},{6,2},{7,3}} | collective-permute-start | bytes 1843208 | tf_op jit(solution)/shard_map/ppermute | solution.py:442
  344.1 84.6 %collective-permute-start.19 = (bf16[192,1600]{1,0:T(8,128)(2,1)}, bf16[192,1600]{1,0:T(8,128)(2,1)}, u32[]{:S(2)}, u32[]{:S(2)}) collective-permute-start(bf16[192,1600]{1,0:T(8,128)(2,1)} %get-tuple-element.298), channel_id=1, source_target_pairs={{0,5},{1,4},{2,7},{3,6},{4,1},{5,0},{6,3},{7,2}} | collective-permute-start | bytes 1843208 | tf_op jit(solution)/shard_map/ppermute | solution.py:442
  345.3 83.5 %collective-permute-start.20 = (bf16[192,1600]{1,0:T(8,128)(2,1)}, bf16[192,1600]{1,0:T(8,128)(2,1)}, u32[]{:S(2)}, u32[]{:S(2)}) collective-permute-start(bf16[192,1600]{1,0:T(8,128)(2,1)} %get-tuple-element.299), channel_id=1, source_target_pairs={{0,6},{1,7},{2,4},{3,5},{4,2},{5,3},{6,0},{7,1}} | collective-permute-start | bytes 1843208 | tf_op jit(solution)/shard_map/ppermute | solution.py:442
  345.9 82.8 %collective-permute-start.21 = (bf16[192,1600]{1,0:T(8,128)(2,1)S(1)}, bf16[192,1600]{1,0:T(8,128)(2,1)}, u32[]{:S(2)}, u32[]{:S(2)}) collective-permute-start(bf16[192,1600]{1,0:T(8,128)(2,1)S(1)} %copy-done.6), channel_id=1, source_target_pairs={{0,7},{1,6},{2,5},{3,4},{4,3},{5,2},{6,1},{7,0}} | collective-permute-start | bytes 1843208 | tf_op jit(solution)/shard_map/ppermute | solution.py:442
  444.2 929.2 %all-gather.22.cloned.1.call-start = ((), (), s32[]{:S(2)}) async-start(), calls=%async_computation.4 | async-start | bytes 15335424 | tf_op jit(solution)/shard_map/all_gather | solution.py:577
  469.2 50.3 %collective-permute-start.2 = (bf16[192,1600]{1,0:T(8,128)(2,1)S(1)}, bf16[192,1600]{1,0:T(8,128)(2,1)}, u32[]{:S(2)}, u32[]{:S(2)}) collective-permute-start(bf16[192,1600]{1,0:T(8,128)(2,1)S(1)} %get-tuple-element.563), channel_id=1, source_target_pairs={{0,3},{1,2},{2,1},{3,0},{4,7},{5,6},{6,5},{7,4}} | collective-permute-start | bytes 1843208 | tf_op jit(solution)/shard_map/while/body/ppermute | solution.py:442
  469.8 51.7 %collective-permute-start.3 = (bf16[192,1600]{1,0:T(8,128)(2,1)S(1)}, bf16[192,1600]{1,0:T(8,128)(2,1)}, u32[]{:S(2)}, u32[]{:S(2)}) collective-permute-start(bf16[192,1600]{1,0:T(8,128)(2,1)S(1)} %get-tuple-element.564), channel_id=1, source_target_pairs={{0,4},{1,5},{2,6},{3,7},{4,0},{5,1},{6,2},{7,3}} | collective-permute-start | bytes 1843208 | tf_op jit(solution)/shard_map/while/body/ppermute | solution.py:442
  469.8 53.6 %collective-permute-start.4 = (bf16[192,1600]{1,0:T(8,128)(2,1)S(1)}, bf16[192,1600]{1,0:T(8,128)(2,1)}, u32[]{:S(2)}, u32[]{:S(2)}) collective-permute-start(bf16[192,1600]{1,0:T(8,128)(2,1)S(1)} %get-tuple-element.565), channel_id=1, source_target_pairs={{0,5},{1,4},{2,7},{3,6},{4,1},{5,0},{6,3},{7,2}} | collective-permute-start | bytes 1843208 | tf_op jit(solution)/shard_map/while/body/ppermute | solution.py:442
  473.0 75.1 %collective-permute-start.5 = (bf16[192,1600]{1,0:T(8,128)(2,1)S(1)}, bf16[192,1600]{1,0:T(8,128)(2,1)S(1)}, u32[]{:S(2)}, u32[]{:S(2)}) collective-permute-start(bf16[192,1600]{1,0:T(8,128)(2,1)S(1)} %get-tuple-element.566), channel_id=1, source_target_pairs={{0,6},{1,7},{2,4},{3,5},{4,2},{5,3},{6,0},{7,1}} | collective-permute-start | bytes 1843208 | tf_op jit(solution)/shard_map/while/body/ppermute | solution.py:442
  494.3 80.6 %collective-permute-start.6 = (bf16[192,1600]{1,0:T(8,128)(2,1)S(1)}, bf16[192,1600]{1,0:T(8,128)(2,1)S(1)}, u32[]{:S(2)}, u32[]{:S(2)}) collective-permute-start(bf16[192,1600]{1,0:T(8,128)(2,1)S(1)} %get-tuple-element.567), channel_id=1, source_target_pairs={{0,7},{1,6},{2,5},{3,4},{4,3},{5,2},{6,1},{7,0}} | collective-permute-start | bytes 1843208 | tf_op jit(solution)/shard_map/while/body/ppermute | solution.py:442
  611.2 47.1 %collective-permute-start.3 = (bf16[192,1600]{1,0:T(8,128)(2,1)S(1)}, bf16[192,1600]{1,0:T(8,128)(2,1)}, u32[]{:S(2)}, u32[]{:S(2)}) collective-permute-start(bf16[192,1600]{1,0:T(8,128)(2,1)S(1)} %get-tuple-element.564), channel_id=1, source_target_pairs={{0,4},{1,5},{2,6},{3,7},{4,0},{5,1},{6,2},{7,3}} | collective-permute-start | bytes 1843208 | tf_op jit(solution)/shard_map/while/body/ppermute | solution.py:442
  611.9 49.7 %collective-permute-start.4 = (bf16[192,1600]{1,0:T(8,128)(2,1)S(1)}, bf16[192,1600]{1,0:T(8,128)(2,1)}, u32[]{:S(2)}, u32[]{:S(2)}) collective-permute-start(bf16[192,1600]{1,0:T(8,128)(2,1)S(1)} %get-tuple-element.565), channel_id=1, source_target_pairs={{0,5},{1,4},{2,7},{3,6},{4,1},{5,0},{6,3},{7,2}} | collective-permute-start | bytes 1843208 | tf_op jit(solution)/shard_map/while/body/ppermute | solution.py:442
  614.8 59.1 %collective-permute-start.5 = (bf16[192,1600]{1,0:T(8,128)(2,1)S(1)}, bf16[192,1600]{1,0:T(8,128)(2,1)S(1)}, u32[]{:S(2)}, u32[]{:S(2)}) collective-permute-start(bf16[192,1600]{1,0:T(8,128)(2,1)S(1)} %get-tuple-element.566), channel_id=1, source_target_pairs={{0,6},{1,7},{2,4},{3,5},{4,2},{5,3},{6,0},{7,1}} | collective-permute-start | bytes 1843208 | tf_op jit(solution)/shard_map/while/body/ppermute | solution.py:442
  630.5 55.8 %collective-permute-start.6 = (bf16[192,1600]{1,0:T(8,128)(2,1)S(1)}, bf16[192,1600]{1,0:T(8,128)(2,1)S(1)}, u32[]{:S(2)}, u32[]{:S(2)}) collective-permute-start(bf16[192,1600]{1,0:T(8,128)(2,1)S(1)} %get-tuple-element.567), channel_id=1, source_target_pairs={{0,7},{1,6},{2,5},{3,4},{4,3},{5,2},{6,1},{7,0}} | collective-permute-start | bytes 1843208 | tf_op jit(solution)/shard_map/while/body/ppermute | solution.py:442
  825.6 55.0 %collective-permute-start.4 = (bf16[192,1600]{1,0:T(8,128)(2,1)S(1)}, bf16[192,1600]{1,0:T(8,128)(2,1)}, u32[]{:S(2)}, u32[]{:S(2)}) collective-permute-start(bf16[192,1600]{1,0:T(8,128)(2,1)S(1)} %get-tuple-element.565), channel_id=1, source_target_pairs={{0,5},{1,4},{2,7},{3,6},{4,1},{5,0},{6,3},{7,2}} | collective-permute-start | bytes 1843208 | tf_op jit(solution)/shard_map/while/body/ppermute | solution.py:442
  827.3 55.3 %collective-permute-start.5 = (bf16[192,1600]{1,0:T(8,128)(2,1)S(1)}, bf16[192,1600]{1,0:T(8,128)(2,1)S(1)}, u32[]{:S(2)}, u32[]{:S(2)}) collective-permute-start(bf16[192,1600]{1,0:T(8,128)(2,1)S(1)} %get-tuple-element.566), channel_id=1, source_target_pairs={{0,6},{1,7},{2,4},{3,5},{4,2},{5,3},{6,0},{7,1}} | collective-permute-start | bytes 1843208 | tf_op jit(solution)/shard_map/while/body/ppermute | solution.py:442
  1178.8 105.5 %collective-permute-start.27 = (bf16[1024,1600]{0,1:T(8,128)(2,1)}, bf16[1024,1600]{0,1:T(8,128)(2,1)}, u32[]{:S(2)}, u32[]{:S(2)}) collective-permute-start(bf16[1024,1600]{0,1:T(8,128)(2,1)} %copy.69), channel_id=1, source_target_pairs={{0,1},{1,0},{2,3},{3,2},{4,5},{5,4},{6,7},{7,6}} | collective-permute-start | bytes 9830408 | tf_op jit(solution)/shard_map/ppermute | solution.py:569
  1288.3 165.3 %all-gather.20.cloned.1.call-start = ((), (), s32[]{:S(2)}) async-start(), calls=%async_computation.3 | async-start | bytes 15335424 | tf_op jit(solution)/shard_map/all_gather | solution.py:577
  (61 other events, 1494.5 us)
Sparse Core Ops, SparseCore 0:
  13.5 70.5 all-gather.13
  86.0 74.8 all-gather.25
  162.7 132.6 all-gather.23
  297.1 133.7 all-gather.15
  432.5 181.1 all-gather.27
  615.4 124.6 all-gather.17
  1288.4 73.2 all-gather.21
  1363.5 70.8 all-gather.19

commit v4 on v3

--- a/solution.py
+++ b/solution.py
@@ -43,6 +43,10 @@
     return lax.dot_general(lhs, rhs, (((1,), (1,)), ((), ())), preferred_element_type=F32)
 
 
+def dot_tn(lhs, rhs):
+    return lax.dot_general(lhs, rhs, (((0,), (0,)), ((), ())), preferred_element_type=F32)
+
+
 def rms(x, gain):
     x = x.astype(F32)
     inv = lax.rsqrt(jnp.sum(x * x, axis=-1, keepdims=True) * (1.0 / D) + EPS)
@@ -75,10 +79,10 @@
     lane = lax.broadcasted_iota(jnp.int32, (1, 128), 1)
     low_half = lane < 64
     rot_mask = (lane % 64) < 32
-    q_idx = lax.broadcasted_iota(jnp.int32, (SUB, 2 * SUB), 0)
-    k_idx = lax.broadcasted_iota(jnp.int32, (SUB, 2 * SUB), 1) % SUB
+    k_idx = lax.broadcasted_iota(jnp.int32, (2 * SUB, SUB), 0) % SUB
+    q_idx = lax.broadcasted_iota(jnp.int32, (2 * SUB, SUB), 1)
     keep = (q_idx // SEQ == k_idx // SEQ) & (k_idx <= q_idx)
-    zero = jnp.zeros((), BF16)
+    blank = jnp.zeros((HEAD_DIM, SUB), F32)
 
     def project(b):
         rows = pl.ds(pl.multiple_of(b * TB, TB), TB)
@@ -98,36 +102,37 @@
             y = pltpu.roll(x, 64, 1)
             at_low, at_high = (y, x) if side else (x, y)
             k_pads.append((jnp.where(low_half, at_low, 0.0).astype(BF16), jnp.where(low_half, 0.0, at_high).astype(BF16)))
-            c, side = divmod(g, 2)
+        for c in range(3):
             if c < 2:
                 x = qkv_s[rows, 1920 + 128 * c:2048 + 128 * c]
             else:
                 x = jnp.concatenate([qkv_s[rows, 2176:2240], jnp.zeros((SUB, 64), F32)], axis=1)
-            y = pltpu.roll(x, 64, 1)
-            at_low, at_high = (y, x) if side else (x, y)
-            v_pads.append((jnp.where(low_half, at_low, 0.0).astype(BF16), jnp.where(low_half, 0.0, at_high).astype(BF16)))
+            x = x.T
+            for side in range(2 if c < 2 else 1):
+                v = x[64 * side:64 * (side + 1)]
+                v_pads.append((jnp.concatenate([v, blank], axis=0).astype(BF16), jnp.concatenate([blank, v], axis=0).astype(BF16)))
         heads = [((2 * j) // 5, min((2 * j + 1) // 5, KVH - 1)) for j in range(13)]
         for j, (ga, gb) in enumerate(heads):
             keys = jnp.concatenate([k_pads[ga][0], k_pads[gb][1]], axis=0)
-            scores = dot_nt(qk_s[rows, 128 * j:128 * (j + 1)], keys) * (HEAD_DIM ** -0.5)
-            sc_s[:, 2 * SUB * j:2 * SUB * (j + 1)] = jnp.where(keep, scores, -1e30)
+            scores = dot_nt(keys, qk_s[rows, 128 * j:128 * (j + 1)]) * (HEAD_DIM ** -0.5)
+            sc_s[2 * SUB * j:2 * SUB * (j + 1), :] = jnp.where(keep, scores, -1e30)
         for i in range(QH):
-            x = sc_s[:, SUB * i:SUB * (i + 1)]
-            e = jnp.exp(x - jnp.max(x, axis=1, keepdims=True))
-            p_s[:, SUB * i:SUB * (i + 1)] = (e * (1.0 / jnp.sum(e, axis=1, keepdims=True))).astype(BF16)
+            x = sc_s[SUB * i:SUB * (i + 1), :]
+            e = jnp.exp(x - jnp.max(x, axis=0, keepdims=True))
+            p_s[SUB * i:SUB * (i + 1), :] = (e * (1.0 / jnp.sum(e, axis=0, keepdims=True))).astype(BF16)
         for j, (ga, gb) in enumerate(heads):
             if j < 12:
-                vals = jnp.concatenate([v_pads[ga][0], v_pads[gb][1]], axis=0)
-                o_s[rows, 128 * j:128 * (j + 1)] = dot(p_s[:, 2 * SUB * j:2 * SUB * (j + 1)], vals).astype(BF16)
+                vals = jnp.concatenate([v_pads[ga][0], v_pads[gb][1]], axis=1)
+                o_s[128 * j:128 * (j + 1), rows] = dot(vals, p_s[2 * SUB * j:2 * SUB * (j + 1), :]).astype(BF16)
             else:
-                o_s[rows, 1536:1600] = dot(p_s[:, 2 * SUB * j:2 * SUB * j + SUB], v_pads[ga][0]).astype(BF16)[:, :64]
+                o_s[1536:1600, rows] = dot(v_pads[ga][0], p_s[2 * SUB * j:2 * SUB * j + SUB, :])[:64].astype(BF16)
 
     def block(b, carry):
         rows = pl.ds(pl.multiple_of(b * TB, TB), TB)
         project(b)
         for s in range(TB // SUB):
             attend(s)
-        out_ref[rows, :] = (h_ref[rows, :].astype(F32) + dot(o_s[...], w_s[:, O_AT:])).astype(BF16)
+        out_ref[rows, :] = (h_ref[rows, :].astype(F32) + dot_tn(o_s[...], w_s[:, O_AT:])).astype(BF16)
         return carry
 
     lax.fori_loop(0, h_ref.shape[0] // TB, block, 0)
@@ -145,7 +150,7 @@
         out_specs=vm,
         scratch_shapes=[
             pltpu.VMEM((D, O_AT + D), BF16), pltpu.VMEM((TB, QKV), F32),
-            pltpu.VMEM((TB, 1920), BF16), pltpu.VMEM((TB, D), BF16), pltpu.VMEM((SUB, 26 * SUB), F32), pltpu.VMEM((SUB, 26 * SUB), BF16),
+            pltpu.VMEM((TB, 1920), BF16), pltpu.VMEM((D, TB), BF16), pltpu.VMEM((26 * SUB, SUB), F32), pltpu.VMEM((26 * SUB, SUB), BF16),
             pltpu.SemaphoreType.DMA((n,)),
         ],
         compiler_params=pltpu.CompilerParams(vmem_limit_bytes=VMEM_LIMIT),
@@ -426,6 +431,11 @@
     )(table_t)
 
 
+def take_rows(table, index):
+    parts = [table.at[part].get(mode='promise_in_bounds') for part in jnp.split(index, index.shape[0] // 512)]
+    return jnp.concatenate(parts, axis=0)
+
+
 def embed_send(table, toks, me, cap, r):
     size, vocab = toks.shape[0], table.shape[0]
     local = toks - me * vocab
@@ -434,7 +444,7 @@
     slots = r * cap + jnp.arange(cap)
     hit = owned[:, None, :] & (rank[:, None, :] == slots[None, :, None])
     idx = jnp.sum(jnp.where(hit, local[:, None, :], 0), axis=2)
-    rows = jnp.take(table, idx.reshape(-1), axis=0).reshape(size, cap, D)
+    rows = table.at[idx.reshape(-1)].get(mode='promise_in_bounds').reshape(size, cap, D)
     return [rows[k] for k in range(size)]
 
 
@@ -500,10 +510,10 @@
         local = tok_pair - core * p_embed.shape[0]
         index = jnp.clip(local, 0, p_embed.shape[0] - 1)
         table = row_major(p_embed.T)
-        for_peer = jnp.take(table, index[1], axis=0)
+        for_peer = take_rows(table, index[1])
         from_peer = lax.ppermute(for_peer, 'fsdp', swap)
         index, for_peer = lax.optimization_barrier((index[0], for_peer))
-        for_own = jnp.take(table, index, axis=0)
+        for_own = take_rows(table, index)
         p_gains = jnp.stack([p_norms, lax.ppermute(p_norms, 'fsdp', swap)]).astype(F32)
         p_gains = jnp.where(core == 0, p_gains, p_gains[::-1])
         p_gains = jnp.swapaxes(p_gains, 0, 1).reshape(2 * layers + 1, 1, D)

time: 1580 us -> 1560 us (0.987)
  waiting for transfers between devices: 264 us -> 290 us
  other arithmetic: 48.5 us -> 29.2 us
  Pallas kernels: 743 us -> 724 us
    ppermute x7, starting transfers between devices: 8.48 us -> 64.3 us  [device_step(): lax.ppermute(small, both, xors[k])]
    ppermute x1, starting transfers between devices: 52.2 us -> 0.43 us  [device_step(): lax.ppermute(p_norms, 'fsdp', swap)]
    ppermute x35, waiting for transfers between devices: 257 us -> 282 us  [embed_swap(): lax.ppermute(rows[k], axis, perms[k])]
    gather x7 -> x9, local copies, waits for them, and re-layouts: 136 us -> 114 us  [the longest x5 87.1 us: embed_send(): table.at[idx.reshape(-1)].get(mode='promise_in_bounds')]
    select_n x12 -> x7, other arithmetic: 22.1 us -> 0.14 us  [the longest x5 0.13 us: embed_send(): table.at[idx.reshape(-1)].get(mode='promise_in_bounds')]
    pallas_call x4, Pallas kernels: 152 us -> 133 us  [attention_block(): pl.pallas_call(functools.partial(attn_kernel, n, layer), out_shape=jax.Sh...]
    unnamed x76 -> x77, local copies, waits for them, and re-layouts: 31.1 us -> 33 us
  transfers between devices with their start and end apart: 57 -> 57, of which waited for: 21 -> 22; matrix products, arithmetic and copies ran while one was open for 25% -> 24% of each run, Pallas kernels for 43% -> 42%
where the time goes in v4:
time: 1560 us; the launch traced here: 1550 us
  Pallas kernels  724 us (46%)
  local copies, waits for them, and re-layouts  330 us (21%)
  waiting for transfers between devices  290 us (19%)
  starting transfers between devices  102 us (7%)
  matrix products  42.8 us (3%)
  other arithmetic  29.2 us (2%)
  between operations  17.8 us (1%)
    pallas_call x4, Pallas kernels, head_block(): pl.pallas_call(functools.partial(head_kernel, v), out_shape=jax.ShapeDtyp...  288 us
    ppermute x35, waiting for transfers between devices, embed_swap(): lax.ppermute(rows[k], axis, perms[k])  282 us
    pallas_call x3, Pallas kernels, mlp_block(): pl.pallas_call(functools.partial(mlp_kernel, n, layer, last), out_shape=j...  185 us
    pallas_call x4, Pallas kernels, attention_block(): pl.pallas_call(functools.partial(attn_kernel, n, layer), out_shape=jax.Sh...  133 us
    gather x5, local copies, waits for them, and re-layouts, embed_send(): table.at[idx.reshape(-1)].get(mode='promise_in_bounds')  87.1 us
    ppermute x7, starting transfers between devices, device_step(): lax.ppermute(small, both, xors[k])  64.3 us
    while x40, local copies, waits for them, and re-layouts  51 us
    pallas_call x1, Pallas kernels, row_major(): pl.pallas_call(relayout_kernel, out_shape=jax.ShapeDtypeStruct((v, D), BF...  51 us
  transfers between devices with their start and end apart: 57, of which 22 were waited for; matrix products, arithmetic and copies ran while one was open for 24% of the time, Pallas kernels for 42%

profile of v4, /device:TPU:0, one launch (start us, length us, event | category | flops | bytes accessed | tf_op | source)
XLA Modules:
  0.0 1549.7 jit_solution(12856001087909674375)
XLA Ops:
  30.0 19.2 %concatenate.57.refs_0_ = bf16[2,800,3904]{2,1,0:T(8,128)(2,1)} concatenate(bf16[2,800,1600]{2,1,0:T(8,128)(2,1)} %param.28, bf16[2,800,640]{2,1,0:T(8,128)(2,1)S(1)} %copy-done.4, bf16[2,800,64]{2,1,0:T(8,128)(2,1)S(1)} %broadcast_in_dim.154, bf16[2,800,1600]{2,1,0:T(8,128)(2,1)} %param.30), dimensions={2} | concatenate | bytes 24985600 | tf_op jit(solution)/shard_map/concatenate | solution.py:540
  51.5 51.0 %row_major.1 = bf16[16000,1600]{1,0:T(8,128)(2,1)} custom-call(bf16[1600,16000]{1,0:T(8,128)(2,1)} %bitcast.123), custom_call_target="tpu_custom_call" | custom-call | flops 13107200000 | bytes 102400000 | tf_op jit(solution)/shard_map/row_major/pallas_call | solution.py:422
  102.6 18.2 %copy.64 = bf16[4000,1600]{1,0:T(8,128)(2,1)} copy(bf16[4000,1600]{0,1:T(8,128)(2,1)} %param.42) | data formatting | bytes 25600000 | tf_op args[19]
  160.6 52.9 %collective-permute-start.7 = (f32[40,128]{1,0:T(8,128)S(1)}, f32[40,128]{1,0:T(8,128)S(1)}, u32[]{:S(2)}, u32[]{:S(2)}) collective-permute-start(f32[40,128]{1,0:T(8,128)S(1)} %get-tuple-element.473), channel_id=1, source_target_pairs={{0,1},{1,0},{2,3},{3,2},{4,5},{5,4},{6,7},{7,6}} | collective-permute-start | bytes 61448 | tf_op jit(solution)/shard_map/ppermute | solution.py:524
  244.3 17.5 %gather_fusion.5 = bf16[1536,1600]{1,0:T(8,128)(2,1)} fusion(bf16[4000,1600]{1,0:T(8,128)(2,1)} %copy.64, s32[2048]{0:T(1024)S(1)} %pad_clamp_fusion.1), kind=kCustom, calls=%fused_computation.5 | custom fusion | bytes 9836544 | tf_op jit(solution)/shard_map/gather | solution.py:447
  282.5 33.6 %attn.4.h_ref = bf16[1024,1600]{1,0:T(8,128)(2,1)} custom-call(s32[1]{0:T(128)} %bitcast.21.core_ref, bf16[1024,1600]{1,0:T(8,128)(2,1)} %broadcast_select_fusion.h_ref, f32[1,1600]{1,0:T(1,128)} %squeeze.102.gain_ref, f32[256,128]{1,0:T(8,128)} %bitcast.138, f32[256,128]{1,0:T(8,128)} %bitcast.142, bf16[2,800,3904]{2,1,0:T(8,128)(2,1)} %concatenate.57.refs_0_, ...), custom_call_target="tpu_custom_call" | custom-call | flops 12582912000 | bytes 12288000 | tf_op jit(solution)/shard_map/attn/pallas_call | solution.py:146
  322.2 61.5 %mlp.3.h_ref = bf16[1024,1600]{1,0:T(8,128)(2,1)} custom-call(s32[1]{0:T(128)} %bitcast.21.core_ref, bf16[1024,1600]{1,0:T(8,128)(2,1)} %attn.4.h_ref, f32[1,1600]{1,0:T(1,128)} %squeeze.103.gain_ref, f32[1,1600]{1,0:T(1,128)} %squeeze.104.fin_ref, bf16[2,800,8704]{2,1,0:T(8,128)(2,1)} %refs_0_.3, bf16[2,800,8704]{2,1,0:T(8,128)(2,1)} %collective-permute-done.25.refs_1_, ...), custom_call_target="tpu_custom_call" | custom-call | flops 42781900800 | bytes 41779200 | tf_op jit(solution)/shard_map/mlp/pallas_call | solution.py:257
  413.3 485.6 %while.16 = (s32[]{:T(128)}, bf16[1024,1600]{0,1:T(8,128)(2,1)}, s32[]{:T(128)}, s32[1,1024]{1,0:T(1,128)S(1)}, s32[1024]{0:T(1024)S(1)}, /*index=5*/s32[]{:T(12...) while((s32[]{:T(128)}, bf16[1024,1600]{0,1:T(8,128)(2,1)}, ...), condition=%wide.region_5.6_spmd, body=%wide.region_3.5_spmd.sunk | while | flops 5063798784 | bytes 87058496 | solution.py:568
  414.9 17.4 %gather_fusion = bf16[1536,1600]{1,0:T(8,128)(2,1)} fusion(bf16[4000,1600]{1,0:T(8,128)(2,1)} %get-tuple-element.604, s32[2048]{0:T(1024)S(1)} %pad_clamp_fusion.8), kind=kCustom, calls=%fused_computation.clone.1 | custom fusion | bytes 9836544 | tf_op jit(solution)/shard_map/while/body/gather | solution.py:447
  447.4 21.5 %collective-permute-done.1 = bf16[192,1600]{1,0:T(8,128)(2,1)} collective-permute-done((bf16[192,1600]{1,0:T(8,128)(2,1)}, bf16[192,1600]{1,0:T(8,128)(2,1)}, u32[]{:S(2)}, u32[]{:S(2)}) %collective-permute-start.1) | collective-permute-done | bytes 614432 | tf_op jit(solution)/shard_map/while/body/ppermute | solution.py:452
  472.4 23.4 %collective-permute-done.2 = bf16[192,1600]{1,0:T(8,128)(2,1)} collective-permute-done((bf16[192,1600]{1,0:T(8,128)(2,1)S(1)}, bf16[192,1600]{1,0:T(8,128)(2,1)}, u32[]{:S(2)}, u32[]{:S(2)}) %collective-permute-start.2) | collective-permute-done | bytes 614432 | tf_op jit(solution)/shard_map/while/body/ppermute | solution.py:452
  539.7 17.5 %gather_fusion = bf16[1536,1600]{1,0:T(8,128)(2,1)} fusion(bf16[4000,1600]{1,0:T(8,128)(2,1)} %get-tuple-element.604, s32[2048]{0:T(1024)S(1)} %pad_clamp_fusion.8), kind=kCustom, calls=%fused_computation.clone.1 | custom fusion | bytes 9836544 | tf_op jit(solution)/shard_map/while/body/gather | solution.py:447
  572.9 19.4 %collective-permute-done.1 = bf16[192,1600]{1,0:T(8,128)(2,1)} collective-permute-done((bf16[192,1600]{1,0:T(8,128)(2,1)}, bf16[192,1600]{1,0:T(8,128)(2,1)}, u32[]{:S(2)}, u32[]{:S(2)}) %collective-permute-start.1) | collective-permute-done | bytes 614432 | tf_op jit(solution)/shard_map/while/body/ppermute | solution.py:452
  597.6 21.7 %collective-permute-done.2 = bf16[192,1600]{1,0:T(8,128)(2,1)} collective-permute-done((bf16[192,1600]{1,0:T(8,128)(2,1)S(1)}, bf16[192,1600]{1,0:T(8,128)(2,1)}, u32[]{:S(2)}, u32[]{:S(2)}) %collective-permute-start.2) | collective-permute-done | bytes 614432 | tf_op jit(solution)/shard_map/while/body/ppermute | solution.py:452
  626.3 21.1 %collective-permute-done.5 = bf16[192,1600]{1,0:T(8,128)(2,1)S(1)} collective-permute-done((bf16[192,1600]{1,0:T(8,128)(2,1)S(1)}, bf16[192,1600]{1,0:T(8,128)(2,1)S(1)}, u32[]{:S(2)}, u32[]{:S(2)}) %collective-permute-start.5) | collective-permute-done | bytes 614432 | tf_op jit(solution)/shard_map/while/body/ppermute | solution.py:452
  673.3 17.3 %gather_fusion = bf16[1536,1600]{1,0:T(8,128)(2,1)} fusion(bf16[4000,1600]{1,0:T(8,128)(2,1)} %get-tuple-element.604, s32[2048]{0:T(1024)S(1)} %pad_clamp_fusion.8), kind=kCustom, calls=%fused_computation.clone.1 | custom fusion | bytes 9836544 | tf_op jit(solution)/shard_map/while/body/gather | solution.py:447
  703.2 22.6 %collective-permute-done.1 = bf16[192,1600]{1,0:T(8,128)(2,1)} collective-permute-done((bf16[192,1600]{1,0:T(8,128)(2,1)}, bf16[192,1600]{1,0:T(8,128)(2,1)}, u32[]{:S(2)}, u32[]{:S(2)}) %collective-permute-start.1) | collective-permute-done | bytes 614432 | tf_op jit(solution)/shard_map/while/body/ppermute | solution.py:452
  727.8 23.8 %collective-permute-done.2 = bf16[192,1600]{1,0:T(8,128)(2,1)} collective-permute-done((bf16[192,1600]{1,0:T(8,128)(2,1)S(1)}, bf16[192,1600]{1,0:T(8,128)(2,1)}, u32[]{:S(2)}, u32[]{:S(2)}) %collective-permute-start.2) | collective-permute-done | bytes 614432 | tf_op jit(solution)/shard_map/while/body/ppermute | solution.py:452
  757.7 21.1 %collective-permute-done.5 = bf16[192,1600]{1,0:T(8,128)(2,1)S(1)} collective-permute-done((bf16[192,1600]{1,0:T(8,128)(2,1)S(1)}, bf16[192,1600]{1,0:T(8,128)(2,1)S(1)}, u32[]{:S(2)}, u32[]{:S(2)}) %collective-permute-start.5) | collective-permute-done | bytes 614432 | tf_op jit(solution)/shard_map/while/body/ppermute | solution.py:452
  803.8 17.3 %gather_fusion = bf16[1536,1600]{1,0:T(8,128)(2,1)} fusion(bf16[4000,1600]{1,0:T(8,128)(2,1)} %get-tuple-element.604, s32[2048]{0:T(1024)S(1)} %pad_clamp_fusion.8), kind=kCustom, calls=%fused_computation.clone.1 | custom fusion | bytes 9836544 | tf_op jit(solution)/shard_map/while/body/gather | solution.py:447
  859.2 25.7 %collective-permute-done.4 = bf16[192,1600]{1,0:T(8,128)(2,1)} collective-permute-done((bf16[192,1600]{1,0:T(8,128)(2,1)S(1)}, bf16[192,1600]{1,0:T(8,128)(2,1)}, u32[]{:S(2)}, u32[]{:S(2)}) %collective-permute-start.4) | collective-permute-done | bytes 614432 | tf_op jit(solution)/shard_map/while/body/ppermute | solution.py:452
  904.3 33.0 %attn.5.h_ref = bf16[1024,1600]{1,0:T(8,128)(2,1)} custom-call(s32[1]{0:T(128)} %bitcast.21.core_ref, bf16[1024,1600]{1,0:T(8,128)(2,1)} %copy.68.h_ref, f32[1,1600]{1,0:T(1,128)} %squeeze.105.gain_ref, f32[256,128]{1,0:T(8,128)} %bitcast.139, f32[256,128]{1,0:T(8,128)} %bitcast.143, bf16[1600,3904]{1,0:T(8,128)(2,1)} %all-gather.14.cloned.1.call-done.refs_0_), custom_call_target="tpu_custom_call" | custom-call | flops 12582912000 | bytes 12288000 | tf_op jit(solution)/shard_map/attn/pallas_call | solution.py:146
  937.4 61.1 %mlp.4.h_ref = bf16[1024,1600]{1,0:T(8,128)(2,1)} custom-call(s32[1]{0:T(128)} %bitcast.21.core_ref, bf16[1024,1600]{1,0:T(8,128)(2,1)} %attn.5.h_ref, f32[1,1600]{1,0:T(1,128)} %squeeze.109.gain_ref, f32[1,1600]{1,0:T(1,128)} %squeeze.110.fin_ref, bf16[1600,8704]{1,0:T(8,128)(2,1)} %bitcast.172, bf16[4352,1600]{1,0:T(8,128)(2,1)} %bitcast.173), custom_call_target="tpu_custom_call" | custom-call | flops 42781900800 | bytes 41779200 | tf_op jit(solution)/shard_map/mlp/pallas_call | solution.py:257
  998.4 33.0 %attn.6.h_ref = bf16[1024,1600]{1,0:T(8,128)(2,1)} custom-call(s32[1]{0:T(128)} %bitcast.21.core_ref, bf16[1024,1600]{1,0:T(8,128)(2,1)} %mlp.3.h_ref, f32[1,1600]{1,0:T(1,128)} %squeeze.113.gain_ref, f32[256,128]{1,0:T(8,128)} %bitcast.140, f32[256,128]{1,0:T(8,128)} %bitcast.144, bf16[2,800,3904]{2,1,0:T(8,128)(2,1)} %concatenate.57.refs_0_, ...), custom_call_target="tpu_custom_call" | custom-call | flops 12582912000 | bytes 12288000 | tf_op jit(solution)/shard_map/attn/pallas_call | solution.py:146
  1031.4 62.2 %mlp.5.x_ref = bf16[1024,1600]{1,0:T(8,128)(2,1)} custom-call(s32[1]{0:T(128)} %bitcast.21.core_ref, bf16[1024,1600]{1,0:T(8,128)(2,1)} %attn.6.h_ref, f32[1,1600]{1,0:T(1,128)} %squeeze.114.gain_ref, f32[1,1600]{1,0:T(1,128)} %squeeze.104.fin_ref, bf16[2,800,8704]{2,1,0:T(8,128)(2,1)} %refs_0_.3, bf16[2,800,8704]{2,1,0:T(8,128)(2,1)} %collective-permute-done.25.refs_1_, ...), custom_call_target="tpu_custom_call" | custom-call | flops 42781900800 | bytes 41779200 | tf_op jit(solution)/shard_map/mlp/pallas_call | solution.py:257
  1100.2 70.9 %head.4 = f32[1024,128]{1,0:T(8,128)} custom-call(bf16[1024,1600]{1,0:T(8,128)(2,1)} %mlp.5.x_ref, bf16[1600,16000]{1,0:T(8,128)(2,1)} %bitcast.168, s32[1024,128]{1,0:T(8,128)} %broadcast_in_dim.155.tgt_ref), custom_call_target="tpu_custom_call" | custom-call | flops 52428800000 | bytes 54476800 | tf_op jit(solution)/shard_map/head/pallas_call | solution.py:380
  1173.5 33.3 %attn.7.h_ref = bf16[1024,1600]{1,0:T(8,128)(2,1)} custom-call(s32[1]{0:T(128)} %bitcast.21.core_ref, bf16[1024,1600]{1,0:T(8,128)(2,1)} %mlp.4.h_ref, f32[1,1600]{1,0:T(1,128)} %squeeze.117.gain_ref, f32[256,128]{1,0:T(8,128)} %bitcast.141, f32[256,128]{1,0:T(8,128)} %bitcast.145, bf16[1600,3904]{1,0:T(8,128)(2,1)} %all-gather.16.cloned.1.call-done.refs_0_), custom_call_target="tpu_custom_call" | custom-call | flops 12582912000 | bytes 12288000 | tf_op jit(solution)/shard_map/attn/pallas_call | solution.py:146
  1206.8 40.4 %gate_up.1.act_ref = bf16[1024,4352]{1,0:T(8,128)(2,1)} custom-call(bf16[1024,1600]{1,0:T(8,128)(2,1)} %attn.7.h_ref, f32[1,1600]{1,0:T(1,128)} %squeeze.121.gain_ref, bf16[1600,8704]{1,0:T(8,128)(2,1)} %bitcast.170, bf16[1600,8704]{1,0:T(8,128)(2,1)} %bitcast.171), custom_call_target="tpu_custom_call" | custom-call | flops 28521267200 | bytes 27852800 | tf_op jit(solution)/shard_map/gate_up/pallas_call | solution.py:300
  1247.2 26.8 %down.1 = bf16[1024,1600]{1,0:T(8,128)(2,1)} custom-call(bf16[1024,1600]{1,0:T(8,128)(2,1)} %attn.7.h_ref, bf16[1024,4352]{1,0:T(8,128)(2,1)} %gate_up.1.act_ref, bf16[4352,1600]{1,0:T(8,128)(2,1)} %all-gather.18.cloned.1.call-done.w_ref, f32[1,1600]{1,0:T(1,128)} %squeeze.110.fin_ref), custom_call_target="tpu_custom_call" | custom-call | flops 14260633600 | bytes 13926400 | tf_op jit(solution)/shard_map/down/pallas_call | solution.py:319
  1290.6 71.1 %head.5 = f32[1024,128]{1,0:T(8,128)} custom-call(bf16[1024,1600]{1,0:T(8,128)(2,1)} %copy.70.x_ref, bf16[1600,16000]{1,0:T(8,128)(2,1)} %bitcast.169, s32[1024,128]{1,0:T(8,128)} %broadcast_in_dim.156.tgt_ref), custom_call_target="tpu_custom_call" | custom-call | flops 52428800000 | bytes 54476800 | tf_op jit(solution)/shard_map/head/pallas_call | solution.py:380
  1366.4 72.9 %head.7 = f32[4096,128]{1,0:T(8,128)} custom-call(bf16[4096,1600]{1,0:T(8,128)(2,1)} %all-gather.22.cloned.1.call-done.x_ref, bf16[1600,4000]{1,0:T(8,128)(2,1)} %bitcast.177, s32[4096,128]{1,0:T(8,128)} %broadcast_in_dim.159.tgt_ref), custom_call_target="tpu_custom_call" | custom-call | flops 52428800000 | bytes 64307200 | tf_op jit(solution)/shard_map/head/pallas_call | solution.py:380
  1446.3 73.0 %head.6 = f32[4096,128]{1,0:T(8,128)} custom-call(bf16[4096,1600]{1,0:T(8,128)(2,1)} %all-gather.20.cloned.1.call-done.x_ref, bf16[1600,4000]{1,0:T(8,128)(2,1)} %bitcast.178, s32[4096,128]{1,0:T(8,128)} %broadcast_in_dim.158.tgt_ref), custom_call_target="tpu_custom_call" | custom-call | flops 52428800000 | bytes 64307200 | tf_op jit(solution)/shard_map/head/pallas_call | solution.py:380
  (460 shorter events, 430.0 us)
Async XLA Ops:
  7.2 897.2 %all-gather.14.cloned.1.call-start = ((), (), s32[]{:S(2)}) async-start(), calls=%async_computation | async-start | bytes 14284800 | tf_op jit(solution)/shard_map/all_gather | solution.py:551
  13.4 923.9 %all-gather.26.cloned.1.call-start = ((), (), s32[]{:S(2)}) async-start(), calls=%async_computation.6 | async-start | bytes 16293888 | tf_op jit(solution)/shard_map/all_gather | solution.py:551
  17.6 919.8 %all-gather.24.cloned.1.call-start = ((), (), s32[]{:S(2)}) async-start(), calls=%async_computation.5 | async-start | bytes 31334400 | tf_op jit(solution)/shard_map/all_gather | solution.py:551
  24.6 1149.0 %all-gather.16.cloned.1.call-start = ((), (), s32[]{:S(2)}) async-start(), calls=%async_computation.1 | async-start | bytes 14284800 | tf_op jit(solution)/shard_map/all_gather | solution.py:551
  28.2 1178.6 %all-gather.28.cloned.1.call-start = ((), (), s32[]{:S(2)}) async-start(), calls=%async_computation.7 | async-start | bytes 31334400 | tf_op jit(solution)/shard_map/all_gather | solution.py:551
  28.8 1218.4 %all-gather.18.cloned.1.call-start = ((), (), s32[]{:S(2)}) async-start(), calls=%async_computation.2 | async-start | bytes 16293888 | tf_op jit(solution)/shard_map/all_gather | solution.py:551
  28.9 292.0 %collective-permute-start.25 = (bf16[2,800,8704]{2,1,0:T(8,128)(2,1)}, bf16[2,800,8704]{2,1,0:T(8,128)(2,1)}, u32[]{:S(2)}, u32[]{:S(2)}) collective-permute-start(bf16[2,800,8704]{2,1,0:T(8,128)(2,1)} %refs_0_.3), channel_id=1, source_target_pairs={{0,1},{1,0},{2,3},{3,2},{4,5},{5,4},{6,7},{7,6}} | collective-permute-start | bytes 83558408 | tf_op jit(solution)/shard_map/ppermute | solution.py:545
  29.9 289.9 %collective-permute-start.26 = (bf16[2,1600,2176]{2,1,0:T(8,128)(2,1)}, bf16[2,1600,2176]{2,1,0:T(8,128)(2,1)}, u32[]{:S(2)}, u32[]{:S(2)}) collective-permute-start(bf16[2,1600,2176]{2,1,0:T(8,128)(2,1)} %bitcast.174), channel_id=1, source_target_pairs={{0,1},{1,0},{2,3},{3,2},{4,5},{5,4},{6,7},{7,6}} | collective-permute-start | bytes 41779208 | tf_op jit(solution)/shard_map/ppermute | solution.py:545
  49.2 232.0 %collective-permute-start.24 = (bf16[2,800,3904]{2,1,0:T(8,128)(2,1)}, bf16[2,800,3904]{2,1,0:T(8,128)(2,1)}, u32[]{:S(2)}, u32[]{:S(2)}) collective-permute-start(bf16[2,800,3904]{2,1,0:T(8,128)(2,1)} %concatenate.57.refs_0_), channel_id=1, source_target_pairs={{0,1},{1,0},{2,3},{3,2},{4,5},{5,4},{6,7},{7,6}} | collective-permute-start | bytes 37478408 | tf_op jit(solution)/shard_map/ppermute | solution.py:545
  49.8 73.7 %collective-permute-start.14 = (s32[1024]{0:T(1024)S(1)}, s32[1024]{0:T(1024)S(1)}, u32[]{:S(2)}, u32[]{:S(2)}) collective-permute-start(s32[1024]{0:T(1024)S(1)} %reshape.627), channel_id=1, source_target_pairs={{0,1},{1,0},{2,3},{3,2},{4,5},{5,4},{6,7},{7,6}} | collective-permute-start | bytes 12296 | tf_op jit(solution)/shard_map/ppermute | solution.py:509
  123.1 90.5 %collective-permute-start.23 = (bf16[5,800]{1,0:T(8,128)(2,1)S(1)}, bf16[5,800]{1,0:T(8,128)(2,1)S(1)}, u32[]{:S(2)}, u32[]{:S(2)}) collective-permute-start(bf16[5,800]{1,0:T(8,128)(2,1)S(1)} %copy-done.23), channel_id=1, source_target_pairs={{0,1},{1,0},{2,3},{3,2},{4,5},{5,4},{6,7},{7,6}} | collective-permute-start | bytes 24008 | tf_op jit(solution)/shard_map/ppermute | solution.py:517
  160.6 61.0 %collective-permute-start.7 = (f32[40,128]{1,0:T(8,128)S(1)}, f32[40,128]{1,0:T(8,128)S(1)}, u32[]{:S(2)}, u32[]{:S(2)}) collective-permute-start(f32[40,128]{1,0:T(8,128)S(1)} %get-tuple-element.473), channel_id=1, source_target_pairs={{0,1},{1,0},{2,3},{3,2},{4,5},{5,4},{6,7},{7,6}} | collective-permute-start | bytes 61448 | tf_op jit(solution)/shard_map/ppermute | solution.py:524
  316.2 67.5 %collective-permute-start.17 = (bf16[192,1600]{1,0:T(8,128)(2,1)}, bf16[192,1600]{1,0:T(8,128)(2,1)}, u32[]{:S(2)}, u32[]{:S(2)}) collective-permute-start(bf16[192,1600]{1,0:T(8,128)(2,1)} %get-tuple-element.295), channel_id=1, source_target_pairs={{0,3},{1,2},{2,1},{3,0},{4,7},{5,6},{6,5},{7,4}} | collective-permute-start | bytes 1843208 | tf_op jit(solution)/shard_map/ppermute | solution.py:452
  317.8 65.9 %collective-permute-start.18 = (bf16[192,1600]{1,0:T(8,128)(2,1)}, bf16[192,1600]{1,0:T(8,128)(2,1)}, u32[]{:S(2)}, u32[]{:S(2)}) collective-permute-start(bf16[192,1600]{1,0:T(8,128)(2,1)} %get-tuple-element.296), channel_id=1, source_target_pairs={{0,4},{1,5},{2,6},{3,7},{4,0},{5,1},{6,2},{7,3}} | collective-permute-start | bytes 1843208 | tf_op jit(solution)/shard_map/ppermute | solution.py:452
  318.0 79.9 %collective-permute-start.19 = (bf16[192,1600]{1,0:T(8,128)(2,1)}, bf16[192,1600]{1,0:T(8,128)(2,1)}, u32[]{:S(2)}, u32[]{:S(2)}) collective-permute-start(bf16[192,1600]{1,0:T(8,128)(2,1)} %get-tuple-element.297), channel_id=1, source_target_pairs={{0,5},{1,4},{2,7},{3,6},{4,1},{5,0},{6,3},{7,2}} | collective-permute-start | bytes 1843208 | tf_op jit(solution)/shard_map/ppermute | solution.py:452
  319.7 78.2 %collective-permute-start.20 = (bf16[192,1600]{1,0:T(8,128)(2,1)}, bf16[192,1600]{1,0:T(8,128)(2,1)}, u32[]{:S(2)}, u32[]{:S(2)}) collective-permute-start(bf16[192,1600]{1,0:T(8,128)(2,1)} %get-tuple-element.298), channel_id=1, source_target_pairs={{0,6},{1,7},{2,4},{3,5},{4,2},{5,3},{6,0},{7,1}} | collective-permute-start | bytes 1843208 | tf_op jit(solution)/shard_map/ppermute | solution.py:452
  320.9 77.1 %collective-permute-start.21 = (bf16[192,1600]{1,0:T(8,128)(2,1)S(1)}, bf16[192,1600]{1,0:T(8,128)(2,1)}, u32[]{:S(2)}, u32[]{:S(2)}) collective-permute-start(bf16[192,1600]{1,0:T(8,128)(2,1)S(1)} %copy-done.7), channel_id=1, source_target_pairs={{0,7},{1,6},{2,5},{3,4},{4,3},{5,2},{6,1},{7,0}} | collective-permute-start | bytes 1843208 | tf_op jit(solution)/shard_map/ppermute | solution.py:452
  413.2 950.2 %all-gather.22.cloned.1.call-start = ((), (), s32[]{:S(2)}) async-start(), calls=%async_computation.4 | async-start | bytes 15335424 | tf_op jit(solution)/shard_map/all_gather | solution.py:587
  439.7 58.0 %collective-permute-start.3 = (bf16[192,1600]{1,0:T(8,128)(2,1)S(1)}, bf16[192,1600]{1,0:T(8,128)(2,1)}, u32[]{:S(2)}, u32[]{:S(2)}) collective-permute-start(bf16[192,1600]{1,0:T(8,128)(2,1)S(1)} %get-tuple-element.567), channel_id=1, source_target_pairs={{0,4},{1,5},{2,6},{3,7},{4,0},{5,1},{6,2},{7,3}} | collective-permute-start | bytes 1843208 | tf_op jit(solution)/shard_map/while/body/ppermute | solution.py:452
  440.7 59.1 %collective-permute-start.4 = (bf16[192,1600]{1,0:T(8,128)(2,1)S(1)}, bf16[192,1600]{1,0:T(8,128)(2,1)}, u32[]{:S(2)}, u32[]{:S(2)}) collective-permute-start(bf16[192,1600]{1,0:T(8,128)(2,1)S(1)} %get-tuple-element.568), channel_id=1, source_target_pairs={{0,5},{1,4},{2,7},{3,6},{4,1},{5,0},{6,3},{7,2}} | collective-permute-start | bytes 1843208 | tf_op jit(solution)/shard_map/while/body/ppermute | solution.py:452
  442.9 69.8 %collective-permute-start.5 = (bf16[192,1600]{1,0:T(8,128)(2,1)S(1)}, bf16[192,1600]{1,0:T(8,128)(2,1)S(1)}, u32[]{:S(2)}, u32[]{:S(2)}) collective-permute-start(bf16[192,1600]{1,0:T(8,128)(2,1)S(1)} %get-tuple-element.569), channel_id=1, source_target_pairs={{0,6},{1,7},{2,4},{3,5},{4,2},{5,3},{6,0},{7,1}} | collective-permute-start | bytes 1843208 | tf_op jit(solution)/shard_map/while/body/ppermute | solution.py:452
  469.0 57.3 %collective-permute-start.6 = (bf16[192,1600]{1,0:T(8,128)(2,1)S(1)}, bf16[192,1600]{1,0:T(8,128)(2,1)S(1)}, u32[]{:S(2)}, u32[]{:S(2)}) collective-permute-start(bf16[192,1600]{1,0:T(8,128)(2,1)S(1)} %get-tuple-element.570), channel_id=1, source_target_pairs={{0,7},{1,6},{2,5},{3,4},{4,3},{5,2},{6,1},{7,0}} | collective-permute-start | bytes 1843208 | tf_op jit(solution)/shard_map/while/body/ppermute | solution.py:452
  563.0 58.3 %collective-permute-start.3 = (bf16[192,1600]{1,0:T(8,128)(2,1)S(1)}, bf16[192,1600]{1,0:T(8,128)(2,1)}, u32[]{:S(2)}, u32[]{:S(2)}) collective-permute-start(bf16[192,1600]{1,0:T(8,128)(2,1)S(1)} %get-tuple-element.567), channel_id=1, source_target_pairs={{0,4},{1,5},{2,6},{3,7},{4,0},{5,1},{6,2},{7,3}} | collective-permute-start | bytes 1843208 | tf_op jit(solution)/shard_map/while/body/ppermute | solution.py:452
  566.2 58.1 %collective-permute-start.4 = (bf16[192,1600]{1,0:T(8,128)(2,1)S(1)}, bf16[192,1600]{1,0:T(8,128)(2,1)}, u32[]{:S(2)}, u32[]{:S(2)}) collective-permute-start(bf16[192,1600]{1,0:T(8,128)(2,1)S(1)} %get-tuple-element.568), channel_id=1, source_target_pairs={{0,5},{1,4},{2,7},{3,6},{4,1},{5,0},{6,3},{7,2}} | collective-permute-start | bytes 1843208 | tf_op jit(solution)/shard_map/while/body/ppermute | solution.py:452
  567.8 79.6 %collective-permute-start.5 = (bf16[192,1600]{1,0:T(8,128)(2,1)S(1)}, bf16[192,1600]{1,0:T(8,128)(2,1)S(1)}, u32[]{:S(2)}, u32[]{:S(2)}) collective-permute-start(bf16[192,1600]{1,0:T(8,128)(2,1)S(1)} %get-tuple-element.569), channel_id=1, source_target_pairs={{0,6},{1,7},{2,4},{3,5},{4,2},{5,3},{6,0},{7,1}} | collective-permute-start | bytes 1843208 | tf_op jit(solution)/shard_map/while/body/ppermute | solution.py:452
  592.4 68.5 %collective-permute-start.6 = (bf16[192,1600]{1,0:T(8,128)(2,1)S(1)}, bf16[192,1600]{1,0:T(8,128)(2,1)S(1)}, u32[]{:S(2)}, u32[]{:S(2)}) collective-permute-start(bf16[192,1600]{1,0:T(8,128)(2,1)S(1)} %get-tuple-element.570), channel_id=1, source_target_pairs={{0,7},{1,6},{2,5},{3,4},{4,3},{5,2},{6,1},{7,0}} | collective-permute-start | bytes 1843208 | tf_op jit(solution)/shard_map/while/body/ppermute | solution.py:452
  696.5 57.1 %collective-permute-start.3 = (bf16[192,1600]{1,0:T(8,128)(2,1)S(1)}, bf16[192,1600]{1,0:T(8,128)(2,1)}, u32[]{:S(2)}, u32[]{:S(2)}) collective-permute-start(bf16[192,1600]{1,0:T(8,128)(2,1)S(1)} %get-tuple-element.567), channel_id=1, source_target_pairs={{0,4},{1,5},{2,6},{3,7},{4,0},{5,1},{6,2},{7,3}} | collective-permute-start | bytes 1843208 | tf_op jit(solution)/shard_map/while/body/ppermute | solution.py:452
  697.5 58.3 %collective-permute-start.4 = (bf16[192,1600]{1,0:T(8,128)(2,1)S(1)}, bf16[192,1600]{1,0:T(8,128)(2,1)}, u32[]{:S(2)}, u32[]{:S(2)}) collective-permute-start(bf16[192,1600]{1,0:T(8,128)(2,1)S(1)} %get-tuple-element.568), channel_id=1, source_target_pairs={{0,5},{1,4},{2,7},{3,6},{4,1},{5,0},{6,3},{7,2}} | collective-permute-start | bytes 1843208 | tf_op jit(solution)/shard_map/while/body/ppermute | solution.py:452
  699.9 79.0 %collective-permute-start.5 = (bf16[192,1600]{1,0:T(8,128)(2,1)S(1)}, bf16[192,1600]{1,0:T(8,128)(2,1)S(1)}, u32[]{:S(2)}, u32[]{:S(2)}) collective-permute-start(bf16[192,1600]{1,0:T(8,128)(2,1)S(1)} %get-tuple-element.569), channel_id=1, source_target_pairs={{0,6},{1,7},{2,4},{3,5},{4,2},{5,3},{6,0},{7,1}} | collective-permute-start | bytes 1843208 | tf_op jit(solution)/shard_map/while/body/ppermute | solution.py:452
  725.8 65.6 %collective-permute-start.6 = (bf16[192,1600]{1,0:T(8,128)(2,1)S(1)}, bf16[192,1600]{1,0:T(8,128)(2,1)S(1)}, u32[]{:S(2)}, u32[]{:S(2)}) collective-permute-start(bf16[192,1600]{1,0:T(8,128)(2,1)S(1)} %get-tuple-element.570), channel_id=1, source_target_pairs={{0,7},{1,6},{2,5},{3,4},{4,3},{5,2},{6,1},{7,0}} | collective-permute-start | bytes 1843208 | tf_op jit(solution)/shard_map/while/body/ppermute | solution.py:452
  1173.4 100.7 %collective-permute-start.27 = (bf16[1024,1600]{0,1:T(8,128)(2,1)}, bf16[1024,1600]{0,1:T(8,128)(2,1)}, u32[]{:S(2)}, u32[]{:S(2)}) collective-permute-start(bf16[1024,1600]{0,1:T(8,128)(2,1)} %copy.69), channel_id=1, source_target_pairs={{0,1},{1,0},{2,3},{3,2},{4,5},{5,4},{6,7},{7,6}} | collective-permute-start | bytes 9830408 | tf_op jit(solution)/shard_map/ppermute | solution.py:579
  1278.1 165.2 %all-gather.20.cloned.1.call-start = ((), (), s32[]{:S(2)}) async-start(), calls=%async_computation.3 | async-start | bytes 15335424 | tf_op jit(solution)/shard_map/all_gather | solution.py:587
  (61 other events, 1485.9 us)
Sparse Core Ops, SparseCore 0:
  13.5 70.5 all-gather.13
  85.9 74.4 all-gather.25
  162.3 138.8 all-gather.23
  302.9 118.1 all-gather.15
  422.8 225.5 all-gather.27
  650.0 129.1 all-gather.17
  1278.2 70.7 all-gather.21
  1350.8 70.8 all-gather.19
